TPU v7x, 128 devices: a whole 4x4x4 slice. The times are simulated.
128 devices in a mesh: dp: 32 (over z, x, core), tensor: 4 (over y).
Axes of the slice: x: 4, y: 4, z: 4, core: 2. Of those that a mesh axis runs over, the one named last changes fastest.
Arguments:
- activations: bfloat16 [64, 128, 4096], P('dp'), may hold values from -6 to 6
- out_grads: bfloat16 [64, 128, 20480], P('dp', None, 'tensor'), may hold values from -0.625 to 0.625
- act_scale: bfloat16 [64, 32], P('dp'), may hold values from 1 to 16
- grad_scale: bfloat16 [64, 1, 20480], P('dp', None, 'tensor'), may hold values from 1 to 72
- moment: float32 [20480, 4096], P(('tensor', 'dp')), may hold values from -0.6 to 0.6
- second: float32 [20480, 4096], P(('tensor', 'dp')), may hold values from 0.1 to 1
- master: float32 [20480, 4096], P(('tensor', 'dp')), may hold values from -0.0625 to 0.0625
Outputs:
- new_moment: float32 [20480, 4096], P(('tensor', 'dp'))
- new_second: float32 [20480, 4096], P(('tensor', 'dp'))
- new_master: float32 [20480, 4096], P(('tensor', 'dp'))
- weights: bfloat16 [20480, 4096], P(('tensor', 'dp'))
All inputs are finite; a program needn't handle non-finite values.
Results may differ from a plain program's by a relative error of at most 0.015.
Values may be sent and summed in bfloat16 or wider, within the bound.
No kernel may reach another device: no remote copies, remote signals or barrier semaphores. Data moves between devices by JAX's collectives and lax.ppermute only.
A program may use at most 192 MiB of HBM per device.

v0:
```python
import functools

import jax
import jax.numpy as jnp
from jax import lax
from jax.sharding import Mesh
from jax.sharding import PartitionSpec as P

FF = 20480
ROWS = 4096
TILE = 128
DP = ("dp_0", "dp_1", "dp_2")
DP_TENSOR = ("dp_0", "dp_1", "dp_2", "tensor")
TENSOR_DP = ("tensor", "dp_0", "dp_1", "dp_2")


clip_rms = 1.0
beta_first = 0.9
beta_second = 0.95
learn_rate = 0.003
adam_eps = 1e-08


def over_axes(shard, axes):
    return functools.reduce(lax.psum, axes, shard)


def widen(act_scale):
    tiles = act_scale.astype(jnp.float32)
    spread = jnp.broadcast_to(tiles[:, :, None], tiles.shape + (TILE,))
    return spread.reshape(tiles.shape[0], tiles.shape[1] * TILE)


def transposed_product(grads_rows, acts_rows):
    return lax.dot_general(
        grads_rows, acts_rows, (((0,), (0,)), ((), ())), preferred_element_type=jnp.float32
    )


def per_device(activations, out_grads, act_scale, grad_scale, moment, second, master):
    weight_rows = activations.shape[2]
    local_tokens = activations.shape[0] * activations.shape[1]
    acts_deq = (
        (activations.astype(jnp.float32) * widen(act_scale)[:, None, :])
        .astype(jnp.bfloat16)
        .reshape(local_tokens, weight_rows)
    )
    grads_deq = (
        (out_grads.astype(jnp.float32) * grad_scale.astype(jnp.float32))
        .astype(jnp.bfloat16)
        .reshape(local_tokens, out_grads.shape[2])
    )
    grad_owned = lax.psum_scatter(
        transposed_product(grads_deq, acts_deq).astype(jnp.bfloat16),
        DP,
        scatter_dimension=0,
        tiled=True,
    ).astype(jnp.float32)
    squares = over_axes(jnp.sum(grad_owned * grad_owned), DP_TENSOR)
    limit = clip_rms * jnp.sqrt(jnp.float32(FF * ROWS))
    factor = jnp.minimum(1.0, limit / jnp.sqrt(squares))
    clipped = factor * grad_owned
    new_moment = beta_first * moment + (1.0 - beta_first) * clipped
    new_second = beta_second * second + (1.0 - beta_second) * clipped * clipped
    new_master = master - learn_rate * new_moment / (jnp.sqrt(new_second) + adam_eps)
    weights = new_master.astype(jnp.bfloat16)
    return (new_moment, new_second, new_master, weights)


def solution(mesh):
    finer = Mesh(
        mesh.devices.reshape(4, 4, 2, mesh.shape["tensor"]), ("dp_0", "dp_1", "dp_2", "tensor")
    )
    in_specs = (
        P(DP, None, None),
        P(DP, None, "tensor"),
        P(DP, None),
        P(DP, None, "tensor"),
        P(TENSOR_DP, None),
        P(TENSOR_DP, None),
        P(TENSOR_DP, None),
    )
    out_specs = (P(TENSOR_DP, None), P(TENSOR_DP, None), P(TENSOR_DP, None), P(TENSOR_DP, None))
    return jax.shard_map(
        per_device, mesh=finer, in_specs=in_specs, out_specs=out_specs, check_vma=False
    )
```

profile of v0, /device:TPU:0, one launch (start us, length us, event | category | flops | bytes accessed | tf_op | source)
XLA Modules:
  0.0 274.4 jit_solution(12825549376815564013)
XLA Ops:
  7.2 0.0 reduce-scatter.2.cloned.1.call-start
  7.2 0.7 convert_element_type.28
  7.9 0.1 broadcast_bitcast_fusion
  8.0 0.7 bitcast_convert_fusion.1
  8.7 18.6 %bitcast_convert_fusion = bf16[5120,4096]{1,0:T(8,128)(2,1)} fusion(bf16[2,128,5120]{2,1,0:T(8,128)(2,1)} %param.8, f32[2,5120]{1,0:T(2,128)S(1)} %bitcast_convert_fusion.1, bf16[2,128,4096]{2,1,0:T(8,128)(2,1)} %param.7, f32[2,4096]{1,0:T(2,128)S(1)} %bitcast.10), kind=kOutput, calls=%fused_computation | convolution fusion | flops 10765467648 | bytes 46735360 | tf_op jit(solution)/shard_map/dot_general | solution.py:35
  27.4 0.0 copy-start
  27.4 0.0 reduce-scatter.2.cloned.1.call-update
  27.4 194.9 %reduce-scatter.2.cloned.1.call-done = bf16[160,4096]{1,0:T(8,128)(2,1)} async-done(((bf16[5120,4096]{1,0:T(8,128)(2,1)}), bf16[160,4096]{1,0:T(8,128)(2,1)}) %reduce-scatter.2.cloned.1.call-update) | async-done | bytes 1310736 | tf_op jit(solution)/shard_map/reduce_scatter | solution.py:53
  222.3 2.6 fusion.2
  224.9 11.0 %psum.28 = f32[]{:T(128)} all-reduce(f32[]{:T(128)} %fusion.2), channel_id=1, replica_groups=mesh['dp_0'=4,'dp_1'=4,'dp_2'=2,'tensor'=4] {'dp_0'}, use_global_device_ids=true, to_apply=%region_2.0 | all-reduce | flops 1 | bytes 8 | tf_op jit(solution)/shard_map/psum | solution.py:25
  235.9 9.2 %psum.29 = f32[]{:T(128)} all-reduce(f32[]{:T(128)} %psum.28), channel_id=1, replica_groups=mesh['dp_0'=4,'dp_1'=4,'dp_2'=2,'tensor'=4] {'dp_1'}, use_global_device_ids=true, to_apply=%region_3.0 | all-reduce | flops 1 | bytes 8 | tf_op jit(solution)/shard_map/psum | solution.py:25
  245.1 3.1 %psum.30 = f32[]{:T(128)} all-reduce(f32[]{:T(128)} %psum.29), channel_id=1, replica_groups=mesh['dp_0'=4,'dp_1'=4,'dp_2'=2,'tensor'=4] {'dp_2'}, use_global_device_ids=true, to_apply=%region_4.0 | all-reduce | flops 1 | bytes 8 | tf_op jit(solution)/shard_map/psum | solution.py:25
  248.2 11.1 %psum.31 = f32[]{:T(128)} all-reduce(f32[]{:T(128)} %psum.30), channel_id=1, replica_groups=mesh['dp_0'=4,'dp_1'=4,'dp_2'=2,'tensor'=4] {'tensor'}, use_global_device_ids=true, to_apply=%region_5.0 | all-reduce | flops 1 | bytes 8 | tf_op jit(solution)/shard_map/psum | solution.py:25
  260.0 0.0 copy-done
  260.0 7.6 %fusion.6 = (bf16[160,4096]{1,0:T(8,128)(2,1)}, f32[160,4096]{1,0:T(8,128)}, f32[160,4096]{1,0:T(8,128)}, f32[160,4096]{1,0:T(8,128)}) fusion(f32[160,4096]{1,0:T(8,128)S(1)} %copy-done, bf16[160,4096]{1,0:T(8,128)(2,1)} %reduce-scatter.2.cloned.1.call-done, f32[]{:T(128)S(6)} %min.3, f32[160,4096]{1,0:T(8,128)} %param.12, f32[160,4096]{1,0:T(8,128)} %param.11), kind=kLoop, calls=%fused_computation.16 | loop fusion | flops 9175040 | bytes 18350084 | tf_op jit(solution)/shard_map/convert_element_type | solution.py:66
  (1 shorter events, 0.0 us)
Async XLA Ops:
  7.2 215.2 %reduce-scatter.2.cloned.1.call-start = ((), (), s32[]{:S(2)}) async-start(), calls=%async_computation.1 | async-start | bytes 43253760 | tf_op jit(solution)/shard_map/reduce_scatter | solution.py:53
  27.4 232.6 %copy-start = (f32[160,4096]{1,0:T(8,128)S(1)}, f32[160,4096]{1,0:T(8,128)}, u32[]{:S(2)}) copy-start(f32[160,4096]{1,0:T(8,128)} %param.13) | copy-start | bytes 7864324
Sparse Core Ops, SparseCore 0:
  27.5 194.7 reduce-scatter.1
where the time goes:
time: 275 us; the launch traced here: 274 us
  waiting for transfers between devices  195 us (71%)
  blocking collectives  34.4 us (13%)
  matrix products  18.6 us (7%)
  between operations  14.7 us (5%)
  other arithmetic  11.6 us (4%)
    reduce_scatter x1, waiting for transfers between devices, per_device(): lax.psum_scatter(transposed_product(grads_deq, acts_deq).astype(jnp.bfloa...  195 us
    psum x4, blocking collectives, over_axes(): return functools.reduce(lax.psum, axes, shard)  34.4 us
    dot_general x1, matrix products, transposed_product(): lax.dot_general(grads_rows, acts_rows, (((0,), (0,)), ((), ())), preferre...  18.6 us
    convert_element_type x1, other arithmetic, per_device(): weights = new_master.astype(jnp.bfloat16)  7.6 us
  transfers between devices with their start and end apart: 1, of which 1 were waited for; matrix products, arithmetic and copies ran while one was open for 0% of the time, Pallas kernels for 0%

commit v1 on v0

v1 whole, which is shorter than its diff:
```python
import functools

import jax
import jax.numpy as jnp
from jax import lax
from jax.experimental import pallas as pl
from jax.experimental.pallas import tpu as pltpu
from jax.sharding import Mesh
from jax.sharding import PartitionSpec as P


FF = 20480
ROWS = 4096
TILE = 128
DP = ("z", "x", "c")
ALL = ("z", "x", "c", "y")
TENSOR_DP = ("y", "z", "x", "c")


clip_rms = 1.0
beta_first = 0.9
beta_second = 0.95
learn_rate = 0.003
adam_eps = 1e-08

SWAP = [(0, 1), (1, 0)]


def ring(shift):
    return [(i, (i + shift) % 4) for i in range(4)]


def along(axis, a, k):
    return lax.ppermute(a, axis, ring(k))


def swap(a):
    return lax.ppermute(a, "c", SWAP)


def widen(act_scale):
    tiles = act_scale.astype(jnp.float32)
    spread = jnp.broadcast_to(tiles[:, :, None], tiles.shape + (TILE,))
    return spread.reshape(tiles.shape[0], tiles.shape[1] * TILE)


def prep_kernel(place_ref, grads_ref, scale_ref, *refs):
    by_z, by_x, turned = refs[:4], refs[4:8], refs[8]
    tokens = grads_ref.shape[0] * grads_ref.shape[1]
    columns = grads_ref.shape[2]
    deq = (grads_ref[...].astype(jnp.float32) * scale_ref[...].astype(jnp.float32)).reshape(tokens, columns)
    turned[...] = deq.T.astype(jnp.bfloat16)
    own = columns // 8
    j = pl.program_id(0)
    z, x, core = place_ref[0], place_ref[1], place_ref[2]
    for k in range(4):

        @pl.when(lax.rem(z + k, 4) == j)
        def _(k=k):
            for at_x in range(4):
                for side in range(2):
                    who = core if side == 0 else 1 - core
                    at = pl.multiple_of((2 * at_x + who) * own, 32)
                    by_z[k][side, at_x * own : (at_x + 1) * own, :] = turned[pl.ds(at, own), :]

        for side in range(2):
            who = core if side == 0 else 1 - core
            at = pl.multiple_of((2 * lax.rem(x + k, 4) + who) * own, 32)
            by_x[k][side, :, :] = turned[pl.ds(at, own), :]


def prep_grads(place, out_grads, grad_scale):
    blocks, tile, columns = out_grads.shape
    tokens = blocks * tile
    part = columns // 4
    shape = jax.ShapeDtypeStruct((2, part // 2, tokens), jnp.bfloat16)
    return pl.pallas_call(
        prep_kernel,
        grid_spec=pltpu.PrefetchScalarGridSpec(
            num_scalar_prefetch=1,
            grid=(4,),
            in_specs=[
                pl.BlockSpec((blocks, tile, part), lambda j, c: (0, 0, j)),
                pl.BlockSpec((blocks, 1, part), lambda j, c: (0, 0, j)),
            ],
            out_specs=[pl.BlockSpec((2, part // 2, tokens), lambda j, c: (0, 0, 0))] * 4
            + [pl.BlockSpec((2, part // 8, tokens), lambda j, c: (0, j, 0))] * 4,
            scratch_shapes=[pltpu.VMEM((part, tokens), jnp.bfloat16)],
        ),
        out_shape=[shape] * 8,
        compiler_params=pltpu.CompilerParams(vmem_limit_bytes=12 * 2**20),
        cost_estimate=pl.CostEstimate(flops=10**9, bytes_accessed=6 * columns * tokens, transcendentals=0),
        name="prep",
    )(place, out_grads, grad_scale)


WHOLE = pl.BlockSpec(memory_space=pltpu.VMEM)
SCALARS = pl.BlockSpec(memory_space=pltpu.SMEM)


def row_block(place_ref, offset, half):
    return 2 * lax.rem(place_ref[3] + offset, 4) + half


def product_kernel(sides, half, offsets, forms, width, place_ref, *refs):
    lefts, refs = refs[: len(sides)], refs[len(sides) :]
    outs, total = refs[-5:-1], refs[-1]
    me = place_ref[1 - half]
    own = total.shape[0] // 4
    for group, form in enumerate(forms):
        at = pl.multiple_of(row_block(place_ref, offsets[group], half) * width, width)
        value = None
        for left, side, (which, lead) in zip(lefts, sides, form):
            cols = refs[which][:, pl.ds(at, width)] if lead is None else refs[which][lead]
            term = jnp.dot(left[side], cols, preferred_element_type=jnp.float32)
            value = term if value is None else value + term
        total[...] = value
        for k in range(4):
            row = pl.multiple_of(lax.rem(me + k, 4) * own, 32)
            outs[k][:, group * width : (group + 1) * width] = total[pl.ds(row, own), :].astype(jnp.bfloat16)


def product(place, half, offsets, lefts, groups, width):
    arrays, forms = [], []
    for rights in groups:
        form = []
        for array, lead in rights:
            known = [i for i, a in enumerate(arrays) if a is array]
            if not known:
                arrays.append(array)
                known = [len(arrays) - 1]
            form.append((known[0], lead))
        forms.append(form)
    columns, tokens = lefts[0][0].shape[1:]
    own = columns // 4
    return pl.pallas_call(
        functools.partial(product_kernel, [side for _, side in lefts], half, offsets, forms, width),
        in_specs=[SCALARS] + [WHOLE] * (len(lefts) + len(arrays)),
        out_specs=[WHOLE] * 4,
        scratch_shapes=[pltpu.VMEM((columns, width), jnp.float32)],
        out_shape=[jax.ShapeDtypeStruct((own, width * len(groups)), jnp.bfloat16)] * 4,
        compiler_params=pltpu.CompilerParams(vmem_limit_bytes=12 * 2**20),
        cost_estimate=pl.CostEstimate(
            flops=2 * columns * 8 * tokens * width * len(groups),
            bytes_accessed=16 * tokens * (columns + width),
            transcendentals=0,
        ),
        name="product",
    )(place, *[a for a, _ in lefts], *arrays)


def folded(squares):
    high, wide = squares.shape
    value = None
    for r in range(0, high, 8):
        for w in range(0, wide, 128):
            term = squares[r : r + 8, w : w + 128]
            value = term if value is None else value + term
    return value


def sums_kernel(count, last, *refs):
    parts, refs = refs[: 4 * count], refs[4 * count :]
    before, refs = (refs[0], refs[1:]) if last else (None, refs)
    squares = before[...] if last else None
    for n in range(count):
        value = parts[4 * n][...].astype(jnp.float32)
        for k in range(1, 4):
            value = value + parts[4 * n + k][...].astype(jnp.float32)
        refs[n][...] = value
        term = folded(value * value)
        squares = term if squares is None else squares + term
    if last:
        refs[count][...] = jnp.broadcast_to(jnp.sum(squares, keepdims=True)[None], refs[count].shape)
    else:
        refs[count][...] = squares


def sums(pieces, before=None):
    last = before is not None
    flat = [p for piece in pieces for p in piece] + ([before] if last else [])
    shapes = [jax.ShapeDtypeStruct(piece[0].shape, jnp.float32) for piece in pieces]
    shapes.append(jax.ShapeDtypeStruct((128, 1, 128) if last else (8, 128), jnp.float32))
    return pl.pallas_call(
        functools.partial(sums_kernel, len(pieces), last),
        in_specs=[WHOLE] * len(flat),
        out_specs=[WHOLE] * len(shapes),
        out_shape=shapes,
        compiler_params=pltpu.CompilerParams(vmem_limit_bytes=12 * 2**20),
        cost_estimate=pl.CostEstimate(flops=10**8, bytes_accessed=4 * 10**6, transcendentals=0),
        name="sums",
    )(*flat)


def adam_kernel(slots, place_ref, shared, *refs):
    grads, refs = refs[:-8], refs[-8:]
    moment, second, master, out_moment, out_second, out_master, out_weights, grad = refs
    step = pl.program_id(0)
    for n, slot in enumerate(slots):

        @pl.when(step == n)
        def _(which=slot[0]):
            grad[...] = grads[which][...]

    norm = jnp.sqrt(jnp.sum(shared[...], axis=0))
    factor = jnp.minimum(1.0, clip_rms * jnp.sqrt(jnp.float32(FF * ROWS)) / norm)
    clipped = factor[0:1, 0:1] * grad[...]
    new_moment = beta_first * moment[...] + (1.0 - beta_first) * clipped
    new_second = beta_second * second[...] + (1.0 - beta_second) * clipped * clipped
    new_master = master[...] - learn_rate * new_moment / (jnp.sqrt(new_second) + adam_eps)
    out_moment[...] = new_moment
    out_second[...] = new_second
    out_master[...] = new_master
    out_weights[...] = new_master.astype(jnp.bfloat16)


def adam(place, slots, piece, shared, grads, moment, second, master):
    own, rows = moment.shape

    def at(j, place_ref):
        block = row_block(place_ref, *slots[0][2:])
        for n, slot in enumerate(slots[1:], 1):
            block = jnp.where(j == n, row_block(place_ref, *slot[2:]), block)
        return 0, block

    firsts = [min(n for n, slot in enumerate(slots) if slot[0] == i) for i in range(len(grads))]
    block = pl.BlockSpec((own, piece), at)
    wide = jax.ShapeDtypeStruct((own, rows), jnp.float32)
    return pl.pallas_call(
        functools.partial(adam_kernel, slots),
        grid_spec=pltpu.PrefetchScalarGridSpec(
            num_scalar_prefetch=1,
            grid=(len(slots),),
            in_specs=[pl.BlockSpec(shared.shape, lambda j, p: (0, 0, 0))]
            + [
                pl.BlockSpec(
                    (own, piece), lambda j, p, n=n, last=g.shape[1] // piece - 1: (0, jnp.clip(j - n, 0, last))
                )
                for n, g in zip(firsts, grads)
            ]
            + [block] * 3,
            out_specs=[block] * 4,
            scratch_shapes=[pltpu.VMEM((own, piece), jnp.float32)],
        ),
        out_shape=[wide, wide, wide, jax.ShapeDtypeStruct((own, rows), jnp.bfloat16)],
        compiler_params=pltpu.CompilerParams(vmem_limit_bytes=60 * 2**20),
        cost_estimate=pl.CostEstimate(flops=10**7, bytes_accessed=17 * 10**6, transcendentals=10**6),
        name="adam",
    )(place, shared, *grads, moment, second, master)


def step(activations, out_grads, act_scale, grad_scale, moment, second, master):
    z, x, c, y = (lax.axis_index(a).astype(jnp.int32) for a in ("z", "x", "c", "y"))
    place = jnp.stack([z, x, c, y])
    rows = activations.shape[2]
    quarter = rows // 4
    piece = quarter // 2
    tokens = activations.shape[0] * activations.shape[1]

    acts = (
        (activations.astype(jnp.float32) * widen(act_scale)[:, None, :]).astype(jnp.bfloat16).reshape(tokens, rows)
    )
    slabs = [lax.dynamic_slice_in_dim(acts, y * quarter + h * piece, piece, 1) for h in range(2)]
    gather_axis, reduce_axis = ("z", "x"), ("x", "z")

    near = [{k: along(gather_axis[h], slabs[h], k) for k in (1, 2, 3)} for h in range(2)]
    acts_other = swap(acts)

    blocks = prep_grads(place, out_grads, grad_scale)
    sent = [blocks[:4], blocks[4:]]
    arrived = [[sent[h][0]] + [along(gather_axis[h], sent[h][k], k) for k in (1, 2, 3)] for h in range(2)]
    lefts = [[p for a in arrived[h] for p in ((a, 0), (swap(a), 1))] for h in range(2)]

    held = [jnp.stack([near[h][k] for k in (1, 2, 3)]) for h in range(2)]
    up = [along("y", held[h], 1) for h in range(2)]
    down = [along("y", held[h], 3) for h in range(2)]
    across = [along("y", up[0], 1), along("y", down[1], 3)]

    pieces, slots = [], []
    for stage in ([(0, held)], [(3, up), (1, down)], [(2, across)]):
        for h in range(2):
            groups = []
            for n, (offset, source) in enumerate(stage):
                own, other = source[h], swap(source[h])
                rights = [(acts, None), (acts_other, None)]
                for lead in range(3):
                    rights += [(own, lead), (other, lead)]
                groups.append(rights)
                slots.append((len(pieces), n, offset, h))
            parts = product(place, h, [offset for offset, _ in stage], lefts[h], groups, piece)
            pieces.append([parts[0]] + [along(reduce_axis[h], parts[k], k) for k in (1, 2, 3)])

    *first, squares = sums(pieces[:4])
    *second_part, squares = sums(pieces[4:], squares)
    shared = lax.all_to_all(squares, ALL, 0, 0, tiled=True)
    return tuple(adam(place, slots, piece, shared, first + second_part, moment, second, master))


def solution(mesh):
    finer = Mesh(mesh.devices.reshape(4, 4, 2, mesh.shape["tensor"]), ALL)
    in_specs = (
        P(DP, None, None),
        P(DP, None, "y"),
        P(DP, None),
        P(DP, None, "y"),
        P(TENSOR_DP, None),
        P(TENSOR_DP, None),
        P(TENSOR_DP, None),
    )
    out_specs = (P(TENSOR_DP, None),) * 4
    return jax.shard_map(step, mesh=finer, in_specs=in_specs, out_specs=out_specs, check_vma=False)
```

time: 275 us -> 220 us (0.80)
  waiting for transfers between devices: 195 us -> 94 us
  starting transfers between devices: 0.04 us -> 64.6 us
  Pallas kernels: 0 us -> 30.3 us
  matrix products: 18.6 us -> 0 us
  blocking collectives: 34.4 us -> 18 us
  between operations: 14.7 us -> 1.1 us
  other arithmetic: 11.6 us -> 4 us
  local copies, waits for them, and re-layouts: 0.1 us -> 6.55 us
    reduce_scatter x1 -> x0, waiting for transfers between devices: 195 us -> none  [per_device(): lax.psum_scatter(transposed_product(grads_deq, acts_deq).astype(jnp.bfloa...]
    ppermute x0 -> x53, waiting for transfers between devices: none -> 94 us  [the longest x36 91.3 us: along(): return lax.ppermute(a, axis, ring(k))]
    ppermute x0 -> x53, starting transfers between devices: none -> 64.6 us  [the longest x36 61.7 us: along(): return lax.ppermute(a, axis, ring(k))]
    psum x4 -> x0, blocking collectives: 34.4 us -> none  [over_axes(): return functools.reduce(lax.psum, axes, shard)]
    pallas_call x0 -> x10, Pallas kernels: none -> 30.3 us  [the longest x6 16 us: product(): pl.pallas_call(functools.partial(product_kernel, [side for _, side in lef...]
    dot_general x1 -> x0, matrix products: 18.6 us -> none  [transposed_product(): lax.dot_general(grads_rows, acts_rows, (((0,), (0,)), ((), ())), preferre...]
    all_to_all x0 -> x1, blocking collectives: none -> 18 us  [step(): shared = lax.all_to_all(squares, ALL, 0, 0, tiled=True)]
    unnamed x4 -> x21, local copies, waits for them, and re-layouts: 0.1 us -> 6.51 us
  transfers between devices with their start and end apart: 1 -> 53, of which waited for: 1 -> 19; matrix products, arithmetic and copies ran while one was open for 0% -> 1% of each run, Pallas kernels for 0% -> 9%
where the time goes in v1:
time: 220 us; the launch traced here: 219 us
  waiting for transfers between devices  94 us (43%)
  starting transfers between devices  64.6 us (29%)
  Pallas kernels  30.3 us (14%)
  blocking collectives  18 us (8%)
  local copies, waits for them, and re-layouts  6.55 us (3%)
  other arithmetic  4 us (2%)
    ppermute x36, waiting for transfers between devices, along(): return lax.ppermute(a, axis, ring(k))  91.3 us
    ppermute x36, starting transfers between devices, along(): return lax.ppermute(a, axis, ring(k))  61.7 us
    all_to_all x1, blocking collectives, step(): shared = lax.all_to_all(squares, ALL, 0, 0, tiled=True)  18 us
    pallas_call x6, Pallas kernels, product(): pl.pallas_call(functools.partial(product_kernel, [side for _, side in lef...  16 us
    pallas_call x1, Pallas kernels, adam(): pl.pallas_call(functools.partial(adam_kernel, slots), grid_spec=pltpu.Pre...  10.7 us
    unnamed x21, local copies, waits for them, and re-layouts  6.51 us
  transfers between devices with their start and end apart: 53, of which 19 were waited for; matrix products, arithmetic and copies ran while one was open for 1% of the time, Pallas kernels for 9%

profile of v1, /device:TPU:0, one launch (start us, length us, event | category | flops | bytes accessed | tf_op | source)
XLA Modules:
  0.0 218.6 jit_solution(13782169228522356230)
XLA Ops:
  3.5 2.9 %collective-permute-start.26 = (bf16[256,512]{1,0:T(8,128)(2,1)S(1)}, bf16[256,512]{1,0:T(8,128)(2,1)S(1)}, u32[]{:S(2)}, u32[]{:S(2)}) collective-permute-start(bf16[256,512]{1,0:T(8,128)(2,1)S(1)} %get-tuple-element.84), channel_id=1, source_target_pairs={{0,24},{8,0},{16,8},{24,16},{1,25},{9,1},{17,9},{25,17},{2,26},{10... | collective-permute-start | bytes 786440 | tf_op jit(solution)/shard_map/ppermute | solution.py:34
  10.7 3.6 %collective-permute-start.9 = (bf16[256,512]{1,0:T(8,128)(2,1)S(1)}, bf16[256,512]{1,0:T(8,128)(2,1)S(1)}, u32[]{:S(2)}, u32[]{:S(2)}) collective-permute-start(bf16[256,512]{1,0:T(8,128)(2,1)S(1)} %get-tuple-element.85), channel_id=1, source_target_pairs={{0,64},{32,96},{64,0},{96,32},{1,65},{33,97},{65,1},{97,33},{2,66}... | collective-permute-start | bytes 786440 | tf_op jit(solution)/shard_map/ppermute | solution.py:34
  27.0 6.2 %collective-permute-done.10 = bf16[256,512]{1,0:T(8,128)(2,1)S(1)} collective-permute-done((bf16[256,512]{1,0:T(8,128)(2,1)S(1)}, bf16[256,512]{1,0:T(8,128)(2,1)S(1)}, u32[]{:S(2)}, u32[]{:S(2)}) %collective-permute-start.10) | collective-permute-done | bytes 262176 | tf_op jit(solution)/shard_map/ppermute | solution.py:34
  36.0 3.0 %collective-permute-start.27 = (bf16[3,256,512]{2,1,0:T(8,128)(2,1)S(1)}, bf16[3,256,512]{2,1,0:T(8,128)(2,1)S(1)}, u32[]{:S(2)}, u32[]{:S(2)}) collective-permute-start(bf16[3,256,512]{2,1,0:T(8,128)(2,1)S(1)} %pad_maximum_fusion.1.refs_10_), channel_id=1, source_target_pairs={{0,3},{1,0},{2,1},{3,2},{4,7},{5,4},{6,5},{7,6},{8,11},{9,8},{10,9... | collective-permute-start | bytes 2359304 | tf_op jit(solution)/shard_map/ppermute | solution.py:34
  39.0 11.4 %collective-permute-done.20.refs_4_ = bf16[2,640,256]{2,1,0:T(8,128)(2,1)S(1)} collective-permute-done((bf16[2,640,256]{2,1,0:T(8,128)(2,1)S(1)}, bf16[2,640,256]{2,1,0:T(8,128)(2,1)S(1)}, u32[]{:S(2)}, u32[]{:S(2)}) %collective-permute-start.20) | collective-permute-done | bytes 655392 | tf_op jit(solution)/shard_map/ppermute | solution.py:34
  50.4 3.9 %collective-permute-start.3 = (bf16[2,640,256]{2,1,0:T(8,128)(2,1)S(1)}, bf16[2,640,256]{2,1,0:T(8,128)(2,1)S(1)}, u32[]{:S(2)}, u32[]{:S(2)}) collective-permute-start(bf16[2,640,256]{2,1,0:T(8,128)(2,1)S(1)} %get-tuple-element.46), channel_id=1, source_target_pairs={{0,64},{32,96},{64,0},{96,32},{1,65},{33,97},{65,1},{97,33},{2,66}... | collective-permute-start | bytes 1966088 | tf_op jit(solution)/shard_map/ppermute | solution.py:34
  56.8 10.6 %collective-permute-done.3.refs_4_ = bf16[2,640,256]{2,1,0:T(8,128)(2,1)S(1)} collective-permute-done((bf16[2,640,256]{2,1,0:T(8,128)(2,1)S(1)}, bf16[2,640,256]{2,1,0:T(8,128)(2,1)S(1)}, u32[]{:S(2)}, u32[]{:S(2)}) %collective-permute-start.3) | collective-permute-done | bytes 655392 | tf_op jit(solution)/shard_map/ppermute | solution.py:34
  68.9 13.2 %collective-permute-done.5.refs_6_ = bf16[2,640,256]{2,1,0:T(8,128)(2,1)S(1)} collective-permute-done((bf16[2,640,256]{2,1,0:T(8,128)(2,1)S(1)}, bf16[2,640,256]{2,1,0:T(8,128)(2,1)S(1)}, u32[]{:S(2)}, u32[]{:S(2)}) %collective-permute-start.5) | collective-permute-done | bytes 655392 | tf_op jit(solution)/shard_map/ppermute | solution.py:34
  82.2 3.0 %collective-permute-start.42 = (bf16[3,256,512]{2,1,0:T(8,128)(2,1)S(1)}, bf16[3,256,512]{2,1,0:T(8,128)(2,1)S(1)}, u32[]{:S(2)}, u32[]{:S(2)}) collective-permute-start(bf16[3,256,512]{2,1,0:T(8,128)(2,1)S(1)} %pad_maximum_fusion.refs_10_), channel_id=1, source_target_pairs={{0,3},{1,0},{2,1},{3,2},{4,7},{5,4},{6,5},{7,6},{8,11},{9,8},{10,9... | collective-permute-start | bytes 2359304 | tf_op jit(solution)/shard_map/ppermute | solution.py:34
  85.8 7.3 %collective-permute-done.11.refs_10_ = bf16[3,256,512]{2,1,0:T(8,128)(2,1)S(1)} collective-permute-done((bf16[3,256,512]{2,1,0:T(8,128)(2,1)S(1)}, bf16[3,256,512]{2,1,0:T(8,128)(2,1)S(1)}, u32[]{:S(2)}, u32[]{:S(2)}) %collective-permute-start.11) | collective-permute-done | bytes 786464 | tf_op jit(solution)/shard_map/ppermute | solution.py:34
  93.1 7.9 %collective-permute-done.42.refs_12_ = bf16[3,256,512]{2,1,0:T(8,128)(2,1)S(1)} collective-permute-done((bf16[3,256,512]{2,1,0:T(8,128)(2,1)S(1)}, bf16[3,256,512]{2,1,0:T(8,128)(2,1)S(1)}, u32[]{:S(2)}, u32[]{:S(2)}) %collective-permute-start.42) | collective-permute-done | bytes 786464 | tf_op jit(solution)/shard_map/ppermute | solution.py:34
  105.0 3.7 %collective-permute-start.28 = (bf16[3,256,512]{2,1,0:T(8,128)(2,1)S(1)}, bf16[3,256,512]{2,1,0:T(8,128)(2,1)S(1)}, u32[]{:S(2)}, u32[]{:S(2)}) collective-permute-start(bf16[3,256,512]{2,1,0:T(8,128)(2,1)S(1)} %collective-permute-done.27.refs_12_), channel_id=1, source_target_pairs={{0,3},{1,0},{2,1},{3,2},{4,7},{5,4},{6,5},{7,6},{8,11},{9,8},{10,9... | collective-permute-start | bytes 2359304 | tf_op jit(solution)/shard_map/ppermute | solution.py:34
  109.3 16.6 %collective-permute-done.28.refs_10_ = bf16[3,256,512]{2,1,0:T(8,128)(2,1)S(1)} collective-permute-done((bf16[3,256,512]{2,1,0:T(8,128)(2,1)S(1)}, bf16[3,256,512]{2,1,0:T(8,128)(2,1)S(1)}, u32[]{:S(2)}, u32[]{:S(2)}) %collective-permute-start.28) | collective-permute-done | bytes 786464 | tf_op jit(solution)/shard_map/ppermute | solution.py:34
  130.2 3.6 %collective-permute-start.39 = (bf16[160,512]{1,0:T(8,128)(2,1)S(1)}, bf16[160,512]{1,0:T(8,128)(2,1)S(1)}, u32[]{:S(2)}, u32[]{:S(2)}) collective-permute-start(bf16[160,512]{1,0:T(8,128)(2,1)S(1)} %get-tuple-element.66), channel_id=1, source_target_pairs={{0,64},{32,96},{64,0},{96,32},{1,65},{33,97},{65,1},{97,33},{2,66}... | collective-permute-start | bytes 491528 | tf_op jit(solution)/shard_map/ppermute | solution.py:34
  136.7 4.7 %collective-permute-done.39.refs_6_ = bf16[160,512]{1,0:T(8,128)(2,1)S(1)} collective-permute-done((bf16[160,512]{1,0:T(8,128)(2,1)S(1)}, bf16[160,512]{1,0:T(8,128)(2,1)S(1)}, u32[]{:S(2)}, u32[]{:S(2)}) %collective-permute-start.39) | collective-permute-done | bytes 163872 | tf_op jit(solution)/shard_map/ppermute | solution.py:34
  141.6 3.6 %product.11 = (bf16[160,1024]{1,0:T(8,128)(2,1)S(1)}, bf16[160,1024]{1,0:T(8,128)(2,1)S(1)}, bf16[160,1024]{1,0:T(8,128)(2,1)S(1)}, bf16[160,1024]{1,0:T(8,128)(2,1)S(1)}) custom-call(s32[4]{0:T(128)S(1)} %pad_add_fusion.place_ref, bf16[2,640,256]{2,1,0:T(8,128)(2,1)S(1)} %get-tuple-element.52.refs_0_, ...), custom_call_target="tpu_custom_call" | custom-call | flops 2684354560 | bytes 4718592 | tf_op jit(solution)/shard_map/product/pallas_call | solution.py:136
  145.3 3.3 %collective-permute-start.51 = (bf16[160,1024]{1,0:T(8,128)(2,1)S(1)}, bf16[160,1024]{1,0:T(8,128)(2,1)S(1)}, u32[]{:S(2)}, u32[]{:S(2)}) collective-permute-start(bf16[160,1024]{1,0:T(8,128)(2,1)S(1)} %get-tuple-element.74), channel_id=1, source_target_pairs={{0,64},{32,96},{64,0},{96,32},{1,65},{33,97},{65,1},{97,33},{2,66}... | collective-permute-start | bytes 983048 | tf_op jit(solution)/shard_map/ppermute | solution.py:34
  148.7 3.6 %product.10 = (bf16[160,1024]{1,0:T(8,128)(2,1)S(1)}, bf16[160,1024]{1,0:T(8,128)(2,1)S(1)}, bf16[160,1024]{1,0:T(8,128)(2,1)S(1)}, bf16[160,1024]{1,0:T(8,128)(2,1)S(1)}) custom-call(s32[4]{0:T(128)S(1)} %pad_add_fusion.place_ref, bf16[2,640,256]{2,1,0:T(8,128)(2,1)S(1)} %get-tuple-element.44.refs_0_, ...), custom_call_target="tpu_custom_call" | custom-call | flops 2684354560 | bytes 4718592 | tf_op jit(solution)/shard_map/product/pallas_call | solution.py:136
  154.0 3.2 %collective-permute-start.52 = (bf16[160,1024]{1,0:T(8,128)(2,1)S(1)}, bf16[160,1024]{1,0:T(8,128)(2,1)S(1)}, u32[]{:S(2)}, u32[]{:S(2)}) collective-permute-start(bf16[160,1024]{1,0:T(8,128)(2,1)S(1)} %get-tuple-element.75), channel_id=1, source_target_pairs={{0,96},{32,0},{64,32},{96,64},{1,97},{33,1},{65,33},{97,65},{2,98}... | collective-permute-start | bytes 983048 | tf_op jit(solution)/shard_map/ppermute | solution.py:34
  157.2 4.9 %collective-permute-done.50.refs_13_ = bf16[160,1024]{1,0:T(8,128)(2,1)S(1)} collective-permute-done((bf16[160,1024]{1,0:T(8,128)(2,1)S(1)}, bf16[160,1024]{1,0:T(8,128)(2,1)S(1)}, u32[]{:S(2)}, u32[]{:S(2)}) %collective-permute-start.50) | collective-permute-done | bytes 327712 | tf_op jit(solution)/shard_map/ppermute | solution.py:34
  162.1 3.2 %collective-permute-start.45 = (bf16[160,1024]{1,0:T(8,128)(2,1)S(1)}, bf16[160,1024]{1,0:T(8,128)(2,1)S(1)}, u32[]{:S(2)}, u32[]{:S(2)}) collective-permute-start(bf16[160,1024]{1,0:T(8,128)(2,1)S(1)} %get-tuple-element.70), channel_id=1, source_target_pairs={{0,16},{8,24},{16,0},{24,8},{1,17},{9,25},{17,1},{25,9},{2,18},{10... | collective-permute-start | bytes 983048 | tf_op jit(solution)/shard_map/ppermute | solution.py:34
  178.7 3.2 %collective-permute-start.15 = (bf16[160,512]{1,0:T(8,128)(2,1)S(1)}, bf16[160,512]{1,0:T(8,128)(2,1)S(1)}, u32[]{:S(2)}, u32[]{:S(2)}) collective-permute-start(bf16[160,512]{1,0:T(8,128)(2,1)S(1)} %get-tuple-element.50), channel_id=1, source_target_pairs={{0,16},{8,24},{16,0},{24,8},{1,17},{9,25},{17,1},{25,9},{2,18},{10... | collective-permute-start | bytes 491528 | tf_op jit(solution)/shard_map/ppermute | solution.py:34
  189.7 18.0 %all_to_all.5.shared = f32[128,1,128]{2,1,0:T(1,128)} all-to-all(f32[128,1,128]{2,1,0:T(1,128)S(1)} %get-tuple-element.77), channel_id=1, replica_groups=mesh['z'=4,'x'=4,'c'=2,'y'=4] {'z','x','c','y'}, dimensions={0} | all-to-all | bytes 131072 | tf_op jit(solution)/shard_map/all_to_all | solution.py:295
  207.7 10.7 %adam.1 = (f32[160,4096]{1,0:T(8,128)}, f32[160,4096]{1,0:T(8,128)}, f32[160,4096]{1,0:T(8,128)}, bf16[160,4096]{1,0:T(8,128)(2,1)}) custom-call(s32[4]{0:T(128)} %copy-done.6, f32[128,1,128]{2,1,0:T(1,128)} %all_to_all.5.shared, f32[160,512]{1,0:T(8,128)} %copy-done.2, f32[160,512]{1,0:T(8,128)} %copy-done.3, f32[160,1024]{1,0:T(8,128)} %copy-done, ...), custom_call_target="tpu_custom_call" | custom-call | flops 10000000 | bytes 17000000 | tf_op jit(solution)/shard_map/adam/pallas_call | solution.py:229
  (120 shorter events, 62.0 us)
Async XLA Ops:
  6.5 16.3 %collective-permute-start.25 = (bf16[256,512]{1,0:T(8,128)(2,1)S(1)}, bf16[256,512]{1,0:T(8,128)(2,1)}, u32[]{:S(2)}, u32[]{:S(2)}) collective-permute-start(bf16[256,512]{1,0:T(8,128)(2,1)S(1)} %get-tuple-element.84), channel_id=1, source_target_pairs={{0,16},{8,24},{16,0},{24,8},{1,17},{9,25},{17,1},{25,9},{2,18},{10... | collective-permute-start | bytes 786440 | tf_op jit(solution)/shard_map/ppermute | solution.py:34
  18.6 17.4 %collective-permute-start.18 = (bf16[2,640,256]{2,1,0:T(8,128)(2,1)S(1)}, bf16[2,640,256]{2,1,0:T(8,128)(2,1)S(1)}, u32[]{:S(2)}, u32[]{:S(2)}) collective-permute-start(bf16[2,640,256]{2,1,0:T(8,128)(2,1)S(1)} %get-tuple-element.53), channel_id=1, source_target_pairs={{0,8},{8,16},{16,24},{24,0},{1,9},{9,17},{17,25},{25,1},{2,10},{10... | collective-permute-start | bytes 1966088 | tf_op jit(solution)/shard_map/ppermute | solution.py:34
  21.2 29.3 %collective-permute-start.20 = (bf16[2,640,256]{2,1,0:T(8,128)(2,1)S(1)}, bf16[2,640,256]{2,1,0:T(8,128)(2,1)S(1)}, u32[]{:S(2)}, u32[]{:S(2)}) collective-permute-start(bf16[2,640,256]{2,1,0:T(8,128)(2,1)S(1)} %get-tuple-element.54), channel_id=1, source_target_pairs={{0,16},{8,24},{16,0},{24,8},{1,17},{9,25},{17,1},{25,9},{2,18},{10... | collective-permute-start | bytes 1966088 | tf_op jit(solution)/shard_map/ppermute | solution.py:34
  22.8 31.5 %collective-permute-start.22 = (bf16[2,640,256]{2,1,0:T(8,128)(2,1)S(1)}, bf16[2,640,256]{2,1,0:T(8,128)(2,1)S(1)}, u32[]{:S(2)}, u32[]{:S(2)}) collective-permute-start(bf16[2,640,256]{2,1,0:T(8,128)(2,1)S(1)} %get-tuple-element.55), channel_id=1, source_target_pairs={{0,24},{8,0},{16,8},{24,16},{1,25},{9,1},{17,9},{25,17},{2,26},{10... | collective-permute-start | bytes 1966088 | tf_op jit(solution)/shard_map/ppermute | solution.py:34
  23.3 31.8 %collective-permute-start.17 = (bf16[2,640,256]{2,1,0:T(8,128)(2,1)S(1)}, bf16[2,640,256]{2,1,0:T(8,128)(2,1)S(1)}, u32[]{:S(2)}, u32[]{:S(2)}) collective-permute-start(bf16[2,640,256]{2,1,0:T(8,128)(2,1)S(1)} %get-tuple-element.52.refs_0_), channel_id=1, source_target_pairs={{0,4},{4,0},{1,5},{5,1},{2,6},{6,2},{3,7},{7,3},{8,12},{12,8},{9,1... | collective-permute-start | bytes 1966088 | tf_op jit(solution)/shard_map/ppermute | solution.py:38
  33.2 21.9 %collective-permute-start.1 = (bf16[2,640,256]{2,1,0:T(8,128)(2,1)S(1)}, bf16[2,640,256]{2,1,0:T(8,128)(2,1)S(1)}, u32[]{:S(2)}, u32[]{:S(2)}) collective-permute-start(bf16[2,640,256]{2,1,0:T(8,128)(2,1)S(1)} %get-tuple-element.45), channel_id=1, source_target_pairs={{0,32},{32,64},{64,96},{96,0},{1,33},{33,65},{65,97},{97,1},{2,34}... | collective-permute-start | bytes 1966088 | tf_op jit(solution)/shard_map/ppermute | solution.py:34
  36.0 49.2 %collective-permute-start.27 = (bf16[3,256,512]{2,1,0:T(8,128)(2,1)S(1)}, bf16[3,256,512]{2,1,0:T(8,128)(2,1)S(1)}, u32[]{:S(2)}, u32[]{:S(2)}) collective-permute-start(bf16[3,256,512]{2,1,0:T(8,128)(2,1)S(1)} %pad_maximum_fusion.1.refs_10_), channel_id=1, source_target_pairs={{0,3},{1,0},{2,1},{3,2},{4,7},{5,4},{6,5},{7,6},{8,11},{9,8},{10,9... | collective-permute-start | bytes 2359304 | tf_op jit(solution)/shard_map/ppermute | solution.py:34
  50.4 16.9 %collective-permute-start.3 = (bf16[2,640,256]{2,1,0:T(8,128)(2,1)S(1)}, bf16[2,640,256]{2,1,0:T(8,128)(2,1)S(1)}, u32[]{:S(2)}, u32[]{:S(2)}) collective-permute-start(bf16[2,640,256]{2,1,0:T(8,128)(2,1)S(1)} %get-tuple-element.46), channel_id=1, source_target_pairs={{0,64},{32,96},{64,0},{96,32},{1,65},{33,97},{65,1},{97,33},{2,66}... | collective-permute-start | bytes 1966088 | tf_op jit(solution)/shard_map/ppermute | solution.py:34
  54.3 27.8 %collective-permute-start.5 = (bf16[2,640,256]{2,1,0:T(8,128)(2,1)S(1)}, bf16[2,640,256]{2,1,0:T(8,128)(2,1)S(1)}, u32[]{:S(2)}, u32[]{:S(2)}) collective-permute-start(bf16[2,640,256]{2,1,0:T(8,128)(2,1)S(1)} %get-tuple-element.47), channel_id=1, source_target_pairs={{0,96},{32,0},{64,32},{96,64},{1,97},{33,1},{65,33},{97,65},{2,98}... | collective-permute-start | bytes 1966088 | tf_op jit(solution)/shard_map/ppermute | solution.py:34
  55.0 30.1 %collective-permute-start = (bf16[2,640,256]{2,1,0:T(8,128)(2,1)S(1)}, bf16[2,640,256]{2,1,0:T(8,128)(2,1)S(1)}, u32[]{:S(2)}, u32[]{:S(2)}) collective-permute-start(bf16[2,640,256]{2,1,0:T(8,128)(2,1)S(1)} %get-tuple-element.44.refs_0_), channel_id=1, source_target_pairs={{0,4},{4,0},{1,5},{5,1},{2,6},{6,2},{3,7},{7,3},{8,12},{12,8},{9,1... | collective-permute-start | bytes 1966088 | tf_op jit(solution)/shard_map/ppermute | solution.py:38
  55.0 30.6 %collective-permute-start.47 = (bf16[3,256,512]{2,1,0:T(8,128)(2,1)S(1)}, bf16[3,256,512]{2,1,0:T(8,128)(2,1)S(1)}, u32[]{:S(2)}, u32[]{:S(2)}) collective-permute-start(bf16[3,256,512]{2,1,0:T(8,128)(2,1)S(1)} %pad_maximum_fusion.1.refs_10_), channel_id=1, source_target_pairs={{0,1},{1,2},{2,3},{3,0},{4,5},{5,6},{6,7},{7,4},{8,9},{9,10},{10,1... | collective-permute-start | bytes 2359304 | tf_op jit(solution)/shard_map/ppermute | solution.py:34
  67.3 25.8 %collective-permute-start.11 = (bf16[3,256,512]{2,1,0:T(8,128)(2,1)S(1)}, bf16[3,256,512]{2,1,0:T(8,128)(2,1)S(1)}, u32[]{:S(2)}, u32[]{:S(2)}) collective-permute-start(bf16[3,256,512]{2,1,0:T(8,128)(2,1)S(1)} %pad_maximum_fusion.refs_10_), channel_id=1, source_target_pairs={{0,1},{1,2},{2,3},{3,0},{4,5},{5,6},{6,7},{7,4},{8,9},{9,10},{10,1... | collective-permute-start | bytes 2359304 | tf_op jit(solution)/shard_map/ppermute | solution.py:34
  82.2 18.9 %collective-permute-start.42 = (bf16[3,256,512]{2,1,0:T(8,128)(2,1)S(1)}, bf16[3,256,512]{2,1,0:T(8,128)(2,1)S(1)}, u32[]{:S(2)}, u32[]{:S(2)}) collective-permute-start(bf16[3,256,512]{2,1,0:T(8,128)(2,1)S(1)} %pad_maximum_fusion.refs_10_), channel_id=1, source_target_pairs={{0,3},{1,0},{2,1},{3,2},{4,7},{5,4},{6,5},{7,6},{8,11},{9,8},{10,9... | collective-permute-start | bytes 2359304 | tf_op jit(solution)/shard_map/ppermute | solution.py:34
  85.2 16.4 %collective-permute-start.33 = (bf16[3,256,512]{2,1,0:T(8,128)(2,1)S(1)}, bf16[3,256,512]{2,1,0:T(8,128)(2,1)S(1)}, u32[]{:S(2)}, u32[]{:S(2)}) collective-permute-start(bf16[3,256,512]{2,1,0:T(8,128)(2,1)S(1)} %pad_maximum_fusion.refs_10_), channel_id=1, source_target_pairs={{0,4},{4,0},{1,5},{5,1},{2,6},{6,2},{3,7},{7,3},{8,12},{12,8},{9,1... | collective-permute-start | bytes 2359304 | tf_op jit(solution)/shard_map/ppermute | solution.py:38
  85.7 40.1 %collective-permute-start.7 = (bf16[256,4096]{1,0:T(8,128)(2,1)S(1)}, bf16[256,4096]{1,0:T(8,128)(2,1)S(1)}, u32[]{:S(2)}, u32[]{:S(2)}) collective-permute-start(bf16[256,4096]{1,0:T(8,128)(2,1)S(1)} %bitcast.17), channel_id=1, source_target_pairs={{0,4},{4,0},{1,5},{5,1},{2,6},{6,2},{3,7},{7,3},{8,12},{12,8},{9,1... | collective-permute-start | bytes 6291464 | tf_op jit(solution)/shard_map/ppermute | solution.py:38
  105.0 20.8 %collective-permute-start.28 = (bf16[3,256,512]{2,1,0:T(8,128)(2,1)S(1)}, bf16[3,256,512]{2,1,0:T(8,128)(2,1)S(1)}, u32[]{:S(2)}, u32[]{:S(2)}) collective-permute-start(bf16[3,256,512]{2,1,0:T(8,128)(2,1)S(1)} %collective-permute-done.27.refs_12_), channel_id=1, source_target_pairs={{0,3},{1,0},{2,1},{3,2},{4,7},{5,4},{6,5},{7,6},{8,11},{9,8},{10,9... | collective-permute-start | bytes 2359304 | tf_op jit(solution)/shard_map/ppermute | solution.py:34
  108.7 19.8 %collective-permute-start.48 = (bf16[3,256,512]{2,1,0:T(8,128)(2,1)S(1)}, bf16[3,256,512]{2,1,0:T(8,128)(2,1)S(1)}, u32[]{:S(2)}, u32[]{:S(2)}) collective-permute-start(bf16[3,256,512]{2,1,0:T(8,128)(2,1)S(1)} %collective-permute-done.47.refs_10_), channel_id=1, source_target_pairs={{0,4},{4,0},{1,5},{5,1},{2,6},{6,2},{3,7},{7,3},{8,12},{12,8},{9,1... | collective-permute-start | bytes 2359304 | tf_op jit(solution)/shard_map/ppermute | solution.py:38
  108.7 21.5 %collective-permute-start.41 = (bf16[3,256,512]{2,1,0:T(8,128)(2,1)S(1)}, bf16[3,256,512]{2,1,0:T(8,128)(2,1)S(1)}, u32[]{:S(2)}, u32[]{:S(2)}) collective-permute-start(bf16[3,256,512]{2,1,0:T(8,128)(2,1)S(1)} %collective-permute-done.11.refs_10_), channel_id=1, source_target_pairs={{0,4},{4,0},{1,5},{5,1},{2,6},{6,2},{3,7},{7,3},{8,12},{12,8},{9,1... | collective-permute-start | bytes 2359304 | tf_op jit(solution)/shard_map/ppermute | solution.py:38
  109.3 24.5 %collective-permute-start.12 = (bf16[3,256,512]{2,1,0:T(8,128)(2,1)S(1)}, bf16[3,256,512]{2,1,0:T(8,128)(2,1)S(1)}, u32[]{:S(2)}, u32[]{:S(2)}) collective-permute-start(bf16[3,256,512]{2,1,0:T(8,128)(2,1)S(1)} %collective-permute-done.11.refs_10_), channel_id=1, source_target_pairs={{0,1},{1,2},{2,3},{3,0},{4,5},{5,6},{6,7},{7,4},{8,9},{9,10},{10,1... | collective-permute-start | bytes 2359304 | tf_op jit(solution)/shard_map/ppermute | solution.py:34
  125.8 39.5 %collective-permute-start.29 = (bf16[3,256,512]{2,1,0:T(8,128)(2,1)S(1)}, bf16[3,256,512]{2,1,0:T(8,128)(2,1)S(1)}, u32[]{:S(2)}, u32[]{:S(2)}) collective-permute-start(bf16[3,256,512]{2,1,0:T(8,128)(2,1)S(1)} %collective-permute-done.28.refs_10_), channel_id=1, source_target_pairs={{0,4},{4,0},{1,5},{5,1},{2,6},{6,2},{3,7},{7,3},{8,12},{12,8},{9,1... | collective-permute-start | bytes 2359304 | tf_op jit(solution)/shard_map/ppermute | solution.py:38
  133.8 36.4 %collective-permute-start.13 = (bf16[3,256,512]{2,1,0:T(8,128)(2,1)S(1)}, bf16[3,256,512]{2,1,0:T(8,128)(2,1)S(1)}, u32[]{:S(2)}, u32[]{:S(2)}) collective-permute-start(bf16[3,256,512]{2,1,0:T(8,128)(2,1)S(1)} %collective-permute-done.12.refs_10_), channel_id=1, source_target_pairs={{0,4},{4,0},{1,5},{5,1},{2,6},{6,2},{3,7},{7,3},{8,12},{12,8},{9,1... | collective-permute-start | bytes 2359304 | tf_op jit(solution)/shard_map/ppermute | solution.py:38
  145.2 16.9 %collective-permute-start.50 = (bf16[160,1024]{1,0:T(8,128)(2,1)S(1)}, bf16[160,1024]{1,0:T(8,128)(2,1)S(1)}, u32[]{:S(2)}, u32[]{:S(2)}) collective-permute-start(bf16[160,1024]{1,0:T(8,128)(2,1)S(1)} %get-tuple-element.73), channel_id=1, source_target_pairs={{0,32},{32,64},{64,96},{96,0},{1,33},{33,65},{65,97},{97,1},{2,34}... | collective-permute-start | bytes 983048 | tf_op jit(solution)/shard_map/ppermute | solution.py:34
  145.3 16.8 %collective-permute-start.51 = (bf16[160,1024]{1,0:T(8,128)(2,1)S(1)}, bf16[160,1024]{1,0:T(8,128)(2,1)S(1)}, u32[]{:S(2)}, u32[]{:S(2)}) collective-permute-start(bf16[160,1024]{1,0:T(8,128)(2,1)S(1)} %get-tuple-element.74), channel_id=1, source_target_pairs={{0,64},{32,96},{64,0},{96,32},{1,65},{33,97},{65,1},{97,33},{2,66}... | collective-permute-start | bytes 983048 | tf_op jit(solution)/shard_map/ppermute | solution.py:34
  154.0 18.5 %collective-permute-start.52 = (bf16[160,1024]{1,0:T(8,128)(2,1)S(1)}, bf16[160,1024]{1,0:T(8,128)(2,1)S(1)}, u32[]{:S(2)}, u32[]{:S(2)}) collective-permute-start(bf16[160,1024]{1,0:T(8,128)(2,1)S(1)} %get-tuple-element.75), channel_id=1, source_target_pairs={{0,96},{32,0},{64,32},{96,64},{1,97},{33,1},{65,33},{97,65},{2,98}... | collective-permute-start | bytes 983048 | tf_op jit(solution)/shard_map/ppermute | solution.py:34
  (38 other events, 456.9 us)

commit v2 on v1

v2 whole, which is shorter than its diff:
```python
import functools

import jax
import jax.numpy as jnp
from jax import lax
from jax.experimental import pallas as pl
from jax.experimental.pallas import tpu as pltpu
from jax.sharding import Mesh
from jax.sharding import PartitionSpec as P


FF = 20480
ROWS = 4096
TILE = 128
DP = ("z", "x", "c")
ALL = ("z", "x", "c", "y")
TENSOR_DP = ("y", "z", "x", "c")


clip_rms = 1.0
beta_first = 0.9
beta_second = 0.95
learn_rate = 0.003
adam_eps = 1e-08

SWAP = [(0, 1), (1, 0)]
WHOLE = pl.BlockSpec(memory_space=pltpu.VMEM)
SCALARS = pl.BlockSpec(memory_space=pltpu.SMEM)


def ring(shift):
    return [(i, (i + shift) % 4) for i in range(4)]


def crossed(shift, first_over_z):
    pairs = []
    for z in range(4):
        for x in range(4):
            for c in range(2):
                over_z = (c == 0) == first_over_z
                to = ((z + shift) % 4, x) if over_z else (z, (x + shift) % 4)
                pairs.append(((z * 4 + x) * 2 + c, (to[0] * 4 + to[1]) * 2 + c))
    return pairs


def gathered(a, k):
    return lax.ppermute(a, DP, crossed(k, True))


def scattered(a, k):
    return lax.ppermute(a, DP, crossed(k, False))


def along_y(a, k):
    return lax.ppermute(a, "y", ring(k))


def swapped(a):
    return lax.ppermute(a, "c", SWAP)


def gather_at(place_ref):
    return jnp.where(place_ref[2] == 0, place_ref[0], place_ref[1])


def reduce_at(place_ref):
    return jnp.where(place_ref[2] == 0, place_ref[1], place_ref[0])


def dequantized(acts_ref, scale_ref, at):
    blocks, tile, width = acts_ref.shape
    scales = scale_ref[...].astype(jnp.float32)
    lane = lax.broadcasted_iota(jnp.int32, scales.shape, 1)
    strips = []
    for t in range(width // TILE):
        chosen = jnp.sum(jnp.where(lane == at * (width // TILE) + t, scales, 0.0), axis=1, keepdims=True)
        strip = acts_ref[:, :, t * TILE : (t + 1) * TILE].astype(jnp.float32) * chosen[:, :, None]
        strips.append(strip.astype(jnp.bfloat16).reshape(blocks * tile, TILE))
    return strips


def slab_kernel(place_ref, mine_ref, theirs_ref, scale_ref, *outs):
    core, y = place_ref[2], place_ref[3]
    for source, at, out in ((mine_ref, 2 * y + core, outs[0]), (theirs_ref, 2 * y + 1 - core, outs[1])):
        for t, strip in enumerate(dequantized(source, scale_ref, at)):
            out[:, t * TILE : (t + 1) * TILE] = strip


def slab(place, activations, act_scale):
    blocks, tile, rows = activations.shape
    piece = rows // 8
    shape = jax.ShapeDtypeStruct((blocks * tile, piece), jnp.bfloat16)
    acts = pltpu.with_memory_space_constraint(activations, pltpu.HBM)
    return pl.pallas_call(
        slab_kernel,
        grid_spec=pltpu.PrefetchScalarGridSpec(
            num_scalar_prefetch=1,
            grid=(1,),
            in_specs=[
                pl.BlockSpec((blocks, tile, piece), lambda j, p: (0, 0, 2 * p[3] + p[2])),
                pl.BlockSpec((blocks, tile, piece), lambda j, p: (0, 0, 2 * p[3] + 1 - p[2])),
                pl.BlockSpec(act_scale.shape, lambda j, p: (0, 0)),
            ],
            out_specs=[pl.BlockSpec(shape.shape, lambda j, p: (0, 0))] * 2,
        ),
        out_shape=[shape, shape],
        compiler_params=pltpu.CompilerParams(vmem_limit_bytes=8 * 2**20),
        cost_estimate=pl.CostEstimate(flops=10**6, bytes_accessed=10**6, transcendentals=0),
        name="slab",
    )(place, acts, acts, act_scale)


def acts_kernel(place_ref, own_ref, other_ref, own_scale_ref, other_scale_ref, whole_ref, opposite_ref):
    j = pl.program_id(0)
    tokens = whole_ref.shape[0] // 2
    at = 2 * j + place_ref[2]
    for n, (source, scale) in enumerate(((own_ref, own_scale_ref), (other_ref, other_scale_ref))):
        for t, strip in enumerate(dequantized(source, scale, at)):
            whole_ref[n * tokens : (n + 1) * tokens, t * TILE : (t + 1) * TILE] = strip

    @pl.when(lax.rem(place_ref[3] + 2, 4) == j)
    def _():
        opposite_ref[...] = whole_ref[...]


def all_acts(place, own, other, own_scale, other_scale):
    blocks, tile, rows = own.shape
    tokens, piece = 2 * blocks * tile, rows // 8
    block = pl.BlockSpec((blocks, tile, piece), lambda j, p: (0, 0, 2 * j + p[2]))
    scale = pl.BlockSpec(own_scale.shape, lambda j, p: (0, 0))
    return pl.pallas_call(
        acts_kernel,
        grid_spec=pltpu.PrefetchScalarGridSpec(
            num_scalar_prefetch=1,
            grid=(4,),
            in_specs=[block, block, scale, scale],
            out_specs=[
                pl.BlockSpec((tokens, piece), lambda j, p: (0, j)),
                pl.BlockSpec((tokens, piece), lambda j, p: (0, 0)),
            ],
        ),
        out_shape=[
            jax.ShapeDtypeStruct((tokens, 4 * piece), jnp.bfloat16),
            jax.ShapeDtypeStruct((tokens, piece), jnp.bfloat16),
        ],
        compiler_params=pltpu.CompilerParams(vmem_limit_bytes=8 * 2**20),
        cost_estimate=pl.CostEstimate(flops=10**6, bytes_accessed=4 * 10**6, transcendentals=0),
        name="acts",
    )(place, pltpu.with_memory_space_constraint(own, pltpu.HBM), other, own_scale, other_scale)


def prep_kernel(place_ref, own_ref, other_ref, own_scale_ref, other_scale_ref, *refs):
    outs, turned = refs[:4], refs[4]
    tokens = own_ref.shape[0] * own_ref.shape[1]
    columns = own_ref.shape[2]
    for n, (source, scale) in enumerate(((own_ref, own_scale_ref), (other_ref, other_scale_ref))):
        deq = (source[...].astype(jnp.float32) * scale[...].astype(jnp.float32)).reshape(tokens, columns)
        turned[:, n * tokens : (n + 1) * tokens] = deq.T.astype(jnp.bfloat16)
    both = columns // 4
    j = pl.program_id(0)
    me = gather_at(place_ref)
    for k in range(4):
        to = lax.rem(me + k, 4)

        @pl.when(jnp.logical_and(place_ref[2] == 0, to == j))
        def _(k=k):
            outs[k][...] = turned[...]

        @pl.when(place_ref[2] == 1)
        def _(k=k, to=to):
            at = pl.multiple_of(to * both, 32)
            outs[k][pl.ds(pl.multiple_of(j * both, 32), both), :] = turned[pl.ds(at, both), :]


def prep_grads(place, own, other, own_scale, other_scale):
    blocks, tile, columns = own.shape
    tokens = blocks * tile
    part = columns // 4
    shape = jax.ShapeDtypeStruct((part, 2 * tokens), jnp.bfloat16)
    block = pl.BlockSpec((blocks, tile, part), lambda j, p: (0, 0, j))
    scale = pl.BlockSpec((blocks, 1, part), lambda j, p: (0, 0, j))
    return pl.pallas_call(
        prep_kernel,
        grid_spec=pltpu.PrefetchScalarGridSpec(
            num_scalar_prefetch=1,
            grid=(4,),
            in_specs=[block, block, scale, scale],
            out_specs=[pl.BlockSpec(shape.shape, lambda j, p: (0, 0))] * 4,
            scratch_shapes=[pltpu.VMEM(shape.shape, jnp.bfloat16)],
        ),
        out_shape=[shape] * 4,
        compiler_params=pltpu.CompilerParams(vmem_limit_bytes=20 * 2**20),
        cost_estimate=pl.CostEstimate(flops=10**9, bytes_accessed=8 * columns * tokens, transcendentals=0),
        name="prep",
    )(place, pltpu.with_memory_space_constraint(own, pltpu.HBM), other, own_scale, other_scale)


def product_kernel(offsets, forms, width, place_ref, *refs):
    lefts, refs = refs[:4], refs[4:]
    outs, total = refs[-5:-1], refs[-1]
    me = reduce_at(place_ref)
    columns = total.shape[0]
    both = columns // 4
    for group, form in enumerate(forms):
        at = pl.multiple_of(lax.rem(place_ref[3] + offsets[group], 4) * width, width)
        for start in range(0, columns, columns // 2):
            value = None
            for left, (which, lead) in zip(lefts, form):
                if which == 0:
                    cols = refs[0][:, pl.ds(at, width)]
                else:
                    cols = refs[which][...] if lead is None else refs[which][lead]
                term = jnp.dot(left[start : start + columns // 2, :], cols, preferred_element_type=jnp.float32)
                value = term if value is None else value + term
            total[start : start + columns // 2, :] = value
        for k in range(4):
            row = pl.multiple_of(lax.rem(me + k, 4) * both, 32)
            outs[k][:, group * width : (group + 1) * width] = total[pl.ds(row, both), :].astype(jnp.bfloat16)


def product(place, offsets, lefts, acts, groups, width):
    arrays, forms = [acts], []
    for rights in groups:
        form = [(0, None)]
        for array, lead in rights:
            known = [i for i, a in enumerate(arrays) if a is array]
            if not known:
                arrays.append(array)
                known = [len(arrays) - 1]
            form.append((known[0], lead))
        forms.append(form)
    columns, tokens = lefts[0].shape
    both = columns // 4
    return pl.pallas_call(
        functools.partial(product_kernel, offsets, forms, width),
        in_specs=[SCALARS] + [WHOLE] * (4 + len(arrays)),
        out_specs=[WHOLE] * 4,
        scratch_shapes=[pltpu.VMEM((columns, width), jnp.float32)],
        out_shape=[jax.ShapeDtypeStruct((both, width * len(groups)), jnp.bfloat16)] * 4,
        compiler_params=pltpu.CompilerParams(vmem_limit_bytes=12 * 2**20),
        cost_estimate=pl.CostEstimate(
            flops=8 * columns * tokens * width * len(groups),
            bytes_accessed=8 * tokens * (columns + width),
            transcendentals=0,
        ),
        name="product",
    )(place, *lefts, *arrays)


def folded(squares):
    high, wide = squares.shape
    value = None
    for r in range(0, high, 8):
        for w in range(0, wide, 128):
            term = squares[r : r + 8, w : w + 128]
            value = term if value is None else value + term
    return value


def sums_kernel(count, last, place_ref, *refs):
    parts, refs = refs[: 4 * count], refs[4 * count :]
    before, refs = (refs[0], refs[1:]) if last else (None, refs)
    squares = before[...] if last else None
    own = refs[0].shape[0]
    core = place_ref[2]
    for n in range(count):
        for side in range(2):
            who = core if side == 0 else 1 - core
            at = pl.ds(pl.multiple_of(who * own, 32), own)
            value = parts[4 * n][at, :].astype(jnp.float32)
            for k in range(1, 4):
                value = value + parts[4 * n + k][at, :].astype(jnp.float32)
            refs[2 * n + side][...] = value
            term = folded(value * value)
            squares = term if squares is None else squares + term
    if last:
        refs[-1][...] = jnp.broadcast_to(jnp.sum(squares, keepdims=True)[None], refs[-1].shape)
    else:
        refs[-1][...] = squares


def sums(place, pieces, before=None):
    last = before is not None
    flat = [p for piece in pieces for p in piece] + ([before] if last else [])
    shapes = []
    for piece in pieces:
        both, width = piece[0].shape
        shapes += [pltpu.HBM((both // 2, width), jnp.float32)] * 2
    shapes.append(jax.ShapeDtypeStruct((128, 1, 128) if last else (8, 128), jnp.float32))
    *values, squares = pl.pallas_call(
        functools.partial(sums_kernel, len(pieces), last),
        in_specs=[SCALARS] + [WHOLE] * len(flat),
        out_specs=[WHOLE] * len(shapes),
        out_shape=shapes,
        compiler_params=pltpu.CompilerParams(vmem_limit_bytes=8 * 2**20),
        cost_estimate=pl.CostEstimate(flops=10**8, bytes_accessed=4 * 10**6, transcendentals=0),
        name="sums",
    )(place, *flat)
    return values[::2], values[1::2], squares


def adam_kernel(slots, place_ref, shared, *refs):
    grads, refs = refs[:-8], refs[-8:]
    moment, second, master, out_moment, out_second, out_master, out_weights, grad = refs
    step = pl.program_id(0)
    wide = grad.shape[1] // 2
    core = place_ref[2]
    for n, (_, which, _) in enumerate(slots):

        @pl.when(step == n)
        def _(which=which):
            grad[:, pl.ds(pl.multiple_of(core * wide, wide), wide)] = grads[2 * which][...]
            grad[:, pl.ds(pl.multiple_of((1 - core) * wide, wide), wide)] = grads[2 * which + 1][...]

    norm = jnp.sqrt(jnp.sum(shared[...], axis=0))
    factor = jnp.minimum(1.0, clip_rms * jnp.sqrt(jnp.float32(FF * ROWS)) / norm)
    clipped = factor[0:1, 0:1] * grad[...]
    new_moment = beta_first * moment[...] + (1.0 - beta_first) * clipped
    new_second = beta_second * second[...] + (1.0 - beta_second) * clipped * clipped
    new_master = master[...] - learn_rate * new_moment / (jnp.sqrt(new_second) + adam_eps)
    out_moment[...] = new_moment
    out_second[...] = new_second
    out_master[...] = new_master
    out_weights[...] = new_master.astype(jnp.bfloat16)


def chosen(j, values):
    found = values[0]
    for n, value in enumerate(values[1:], 1):
        found = jnp.where(j == n, value, found)
    return found


def adam(place, slots, shared, pairs, moment, second, master):
    own, rows = moment.shape
    quarter = rows // 4
    block = pl.BlockSpec((own, quarter), lambda j, p: (0, lax.rem(p[3] + chosen(j, [s[0] for s in slots]), 4)))

    def source(i):
        at, blocks = 0, []
        for _, which, lead in slots:
            at = lead if which == i else at
            blocks.append(at)
        return [pl.BlockSpec((own, quarter // 2), lambda j, p: (0, chosen(j, blocks)))] * 2

    wide = jax.ShapeDtypeStruct((own, rows), jnp.float32)
    return pl.pallas_call(
        functools.partial(adam_kernel, slots),
        grid_spec=pltpu.PrefetchScalarGridSpec(
            num_scalar_prefetch=1,
            grid=(len(slots),),
            in_specs=[pl.BlockSpec(shared.shape, lambda j, p: (0, 0, 0))]
            + [spec for i in range(len(pairs)) for spec in source(i)]
            + [block] * 3,
            out_specs=[block] * 4,
            scratch_shapes=[pltpu.VMEM((own, quarter), jnp.float32)],
        ),
        out_shape=[wide, wide, wide, jax.ShapeDtypeStruct((own, rows), jnp.bfloat16)],
        compiler_params=pltpu.CompilerParams(vmem_limit_bytes=60 * 2**20),
        cost_estimate=pl.CostEstimate(flops=10**7, bytes_accessed=17 * 10**6, transcendentals=10**6),
        name="adam",
    )(place, shared, *[a for pair in pairs for a in pair], moment, second, master)


PRODUCTS = ((0,), (3, 1), (2,))
EARLY = 2


def step(activations, out_grads, act_scale, grad_scale, moment, second, master):
    place = jnp.stack([lax.axis_index(a).astype(jnp.int32) for a in ("z", "x", "c", "y")])
    piece = activations.shape[2] // 8

    mine, theirs = slab(place, activations, act_scale)
    held_own = jnp.concatenate([mine, swapped(theirs)], 0)
    near = [gathered(held_own, k) for k in (1, 2, 3)]

    lefts = prep_grads(place, out_grads, swapped(out_grads), grad_scale, swapped(grad_scale))
    lefts = [lefts[0]] + [gathered(lefts[k], k) for k in (1, 2, 3)]

    acts, opposite = all_acts(place, activations, swapped(activations), act_scale, swapped(act_scale))

    held = jnp.stack(near)
    across = [gathered(opposite, k) for k in (1, 2, 3)]
    sources = {0: held, 3: along_y(held, 1), 1: along_y(held, 3)}
    rights = {offset: [(array, lead) for lead in range(3)] for offset, array in sources.items()}
    rights[2] = [(array, None) for array in across]

    pieces, slots = [], []
    for number, offsets in enumerate(PRODUCTS):
        slots += [(offset, number, n) for n, offset in enumerate(offsets)]
        parts = product(place, offsets, lefts, acts, [rights[offset] for offset in offsets], piece)
        pieces.append([parts[0]] + [scattered(parts[k], k) for k in (1, 2, 3)])

    kept, given, squares = sums(place, pieces[:EARLY])
    more_kept, more_given, squares = sums(place, pieces[EARLY:], squares)
    kept, given = kept + more_kept, given + more_given
    pairs = [(own, pltpu.with_memory_space_constraint(swapped(other), pltpu.HBM)) for own, other in zip(kept, given)]
    shared = lax.all_to_all(squares, ALL, 0, 0, tiled=True)
    return tuple(adam(place, slots, shared, pairs, moment, second, master))


def solution(mesh):
    finer = Mesh(mesh.devices.reshape(4, 4, 2, mesh.shape["tensor"]), ALL)
    in_specs = (
        P(DP, None, None),
        P(DP, None, "y"),
        P(DP, None),
        P(DP, None, "y"),
        P(TENSOR_DP, None),
        P(TENSOR_DP, None),
        P(TENSOR_DP, None),
    )
    out_specs = (P(TENSOR_DP, None),) * 4
    return jax.shard_map(step, mesh=finer, in_specs=in_specs, out_specs=out_specs, check_vma=False)
```

time: 220 us -> 154 us (0.70)
  waiting for transfers between devices: 94 us -> 58 us
  starting transfers between devices: 64.6 us -> 40.4 us
  Pallas kernels: 30.3 us -> 37 us
  local copies, waits for them, and re-layouts: 6.55 us -> 1.84 us
  other arithmetic: 4 us -> 0.25 us
  blocking collectives: 18 us -> 14.7 us
    ppermute x53 -> x28, waiting for transfers between devices: 94 us -> 58 us  [the longest x9 37.7 us: gathered(): return lax.ppermute(a, DP, crossed(k, True))]
    ppermute x53 -> x28, starting transfers between devices: 64.6 us -> 40.4 us  [the longest x9 20.4 us: scattered(): return lax.ppermute(a, DP, crossed(k, False))]
    unnamed x21 -> x16, local copies, waits for them, and re-layouts: 6.51 us -> 1.82 us
    all_to_all x1, blocking collectives: 18 us -> 14.7 us  [step(): shared = lax.all_to_all(squares, ALL, 0, 0, tiled=True)]
    pallas_call x6 -> x5, Pallas kernels: 16 us -> 19 us  [the longest x3 13.7 us: product(): pl.pallas_call(functools.partial(product_kernel, offsets, forms, width),...]
    convert_element_type x2 -> x0, other arithmetic: 2.71 us -> none  [the longest x1 2.06 us: step(): (activations.astype(jnp.float32) * widen(act_scale)[:, None, :]).astype(j...]
    pallas_call x2, Pallas kernels: 1.08 us -> 3.73 us  [sums(): pl.pallas_call(functools.partial(sums_kernel, len(pieces), last), in_spec...]
  transfers between devices with their start and end apart: 53 -> 28, of which waited for: 19 -> 9; matrix products, arithmetic and copies ran while one was open for 1% -> 0% of each run, Pallas kernels for 9% -> 18%
where the time goes in v2:
time: 154 us; the launch traced here: 153 us
  waiting for transfers between devices  58 us (38%)
  starting transfers between devices  40.4 us (26%)
  Pallas kernels  37 us (24%)
  blocking collectives  14.7 us (10%)
  local copies, waits for them, and re-layouts  1.84 us (1%)
    ppermute x9, waiting for transfers between devices, gathered(): return lax.ppermute(a, DP, crossed(k, True))  37.7 us
    ppermute x9, starting transfers between devices, scattered(): return lax.ppermute(a, DP, crossed(k, False))  20.4 us
    ppermute x9, waiting for transfers between devices, scattered(): return lax.ppermute(a, DP, crossed(k, False))  15 us
    all_to_all x1, blocking collectives, step(): shared = lax.all_to_all(squares, ALL, 0, 0, tiled=True)  14.7 us
    ppermute x9, starting transfers between devices, gathered(): return lax.ppermute(a, DP, crossed(k, True))  14.7 us
    pallas_call x3, Pallas kernels, product(): pl.pallas_call(functools.partial(product_kernel, offsets, forms, width),...  13.7 us
    pallas_call x1, Pallas kernels, adam(): pl.pallas_call(functools.partial(adam_kernel, slots), grid_spec=pltpu.Pre...  9.62 us
    ppermute x8, waiting for transfers between devices, swapped(): return lax.ppermute(a, 'c', SWAP)  5.26 us
  transfers between devices with their start and end apart: 28, of which 9 were waited for; matrix products, arithmetic and copies ran while one was open for 0% of the time, Pallas kernels for 18%

profile of v2, /device:TPU:0, one launch (start us, length us, event | category | flops | bytes accessed | tf_op | source)
XLA Modules:
  0.0 153.0 jit_solution(13486465977011021425)
XLA Ops:
  4.0 5.2 %collective-permute-done.13 = bf16[256,512]{1,0:T(8,128)(2,1)S(1)} collective-permute-done((bf16[256,512]{1,0:T(8,128)(2,1)S(1)}, bf16[256,512]{1,0:T(8,128)(2,1)S(1)}, u32[]{:S(2)}, u32[]{:S(2)}) %collective-permute-start.13) | collective-permute-done | bytes 262176 | tf_op jit(solution)/shard_map/ppermute | solution.py:59
  9.2 2.1 %collective-permute-start.14 = (bf16[512,512]{1,0:T(8,128)(2,1)S(1)}, bf16[512,512]{1,0:T(8,128)(2,1)S(1)}, u32[]{:S(2)}, u32[]{:S(2)}) collective-permute-start(bf16[512,512]{1,0:T(8,128)(2,1)S(1)} %constant_dynamic-update-slice_fusion), channel_id=1, source_target_pairs={{0,32},{4,12},{8,40},{12,20},{16,48},{20,28},{24,56},{28,4},{32,64... | collective-permute-start | bytes 1572872 | tf_op jit(solution)/shard_map/ppermute | solution.py:47
  11.3 3.6 %collective-permute-start.15 = (bf16[512,512]{1,0:T(8,128)(2,1)S(1)}, bf16[512,512]{1,0:T(8,128)(2,1)S(1)}, u32[]{:S(2)}, u32[]{:S(2)}) collective-permute-start(bf16[512,512]{1,0:T(8,128)(2,1)S(1)} %constant_dynamic-update-slice_fusion), channel_id=1, source_target_pairs={{0,64},{4,20},{8,72},{12,28},{16,80},{20,4},{24,88},{28,12},{32,96... | collective-permute-start | bytes 1572872 | tf_op jit(solution)/shard_map/ppermute | solution.py:47
  16.0 4.6 %collective-permute-done.14 = bf16[512,512]{1,0:T(8,128)(2,1)S(1)} collective-permute-done((bf16[512,512]{1,0:T(8,128)(2,1)S(1)}, bf16[512,512]{1,0:T(8,128)(2,1)S(1)}, u32[]{:S(2)}, u32[]{:S(2)}) %collective-permute-start.14) | collective-permute-done | bytes 524320 | tf_op jit(solution)/shard_map/ppermute | solution.py:47
  20.6 7.1 %collective-permute-done.15 = bf16[512,512]{1,0:T(8,128)(2,1)S(1)} collective-permute-done((bf16[512,512]{1,0:T(8,128)(2,1)S(1)}, bf16[512,512]{1,0:T(8,128)(2,1)S(1)}, u32[]{:S(2)}, u32[]{:S(2)}) %collective-permute-start.15) | collective-permute-done | bytes 524320 | tf_op jit(solution)/shard_map/ppermute | solution.py:47
  29.5 2.4 %collective-permute-start.21 = (bf16[3,512,512]{2,1,0:T(8,128)(2,1)S(1)}, bf16[3,512,512]{2,1,0:T(8,128)(2,1)S(1)}, u32[]{:S(2)}, u32[]{:S(2)}) collective-permute-start(bf16[3,512,512]{2,1,0:T(8,128)(2,1)S(1)} %pad_maximum_fusion.refs_5_), channel_id=1, source_target_pairs={{0,3},{1,0},{2,1},{3,2},{4,7},{5,4},{6,5},{7,6},{8,11},{9,8},{10,9... | collective-permute-start | bytes 4718600 | tf_op jit(solution)/shard_map/ppermute | solution.py:55
  31.9 4.6 %prep.1 = (bf16[1280,512]{1,0:T(8,128)(2,1)S(1)}, bf16[1280,512]{1,0:T(8,128)(2,1)S(1)}, bf16[1280,512]{1,0:T(8,128)(2,1)S(1)}, bf16[1280,512]{1,0:T(8,128)(2,1)S(1)}) custom-call(s32[4]{0:T(128)S(1)} %pad_add_fusion.place_ref, bf16[2,128,5120]{2,1,0:T(8,128)(2,1)} %own_ref.2, bf16[2,128,5120]{2,1,0:T(8,128)(2,1)S(1)} %collective-permute-done.other_ref, ...), custom_call_target="tpu_custom_call" | custom-call | flops 1000000000 | bytes 10485760 | tf_op jit(solution)/shard_map/prep/pallas_call | solution.py:182
  37.4 2.1 %collective-permute-start.3 = (bf16[1280,512]{1,0:T(8,128)(2,1)S(1)}, bf16[1280,512]{1,0:T(8,128)(2,1)S(1)}, u32[]{:S(2)}, u32[]{:S(2)}) collective-permute-start(bf16[1280,512]{1,0:T(8,128)(2,1)S(1)} %get-tuple-element.34), channel_id=1, source_target_pairs={{0,64},{4,20},{8,72},{12,28},{16,80},{20,4},{24,88},{28,12},{32,96... | collective-permute-start | bytes 3932168 | tf_op jit(solution)/shard_map/ppermute | solution.py:47
  41.0 3.5 %acts.1 = (bf16[512,2048]{1,0:T(8,128)(2,1)S(1)}, bf16[512,512]{1,0:T(8,128)(2,1)S(1)}) custom-call(s32[4]{0:T(128)S(1)} %pad_add_fusion.place_ref, bf16[2,128,4096]{2,1,0:T(8,128)(2,1)} %theirs_ref.1, bf16[2,128,4096]{2,1,0:T(8,128)(2,1)} %collective-permute-done.5.other_ref, bf16[2,32]{1,0:T(2,128)(2,1)S(1)} %copy-done.2, ...), custom_call_target="tpu_custom_call" | custom-call | flops 1000000 | bytes 4000000 | tf_op jit(solution)/shard_map/acts/pallas_call | solution.py:131
  44.6 24.9 %collective-permute-done.2.refs_1_ = bf16[1280,512]{1,0:T(8,128)(2,1)S(1)} collective-permute-done((bf16[1280,512]{1,0:T(8,128)(2,1)S(1)}, bf16[1280,512]{1,0:T(8,128)(2,1)S(1)}, u32[]{:S(2)}, u32[]{:S(2)}) %collective-permute-start.2) | collective-permute-done | bytes 1310752 | tf_op jit(solution)/shard_map/ppermute | solution.py:47
  70.6 2.4 %collective-permute-start.9 = (bf16[512,512]{1,0:T(8,128)(2,1)S(1)}, bf16[512,512]{1,0:T(8,128)(2,1)S(1)}, u32[]{:S(2)}, u32[]{:S(2)}) collective-permute-start(bf16[512,512]{1,0:T(8,128)(2,1)S(1)} %get-tuple-element.37), channel_id=1, source_target_pairs={{0,96},{4,28},{8,104},{12,4},{16,112},{20,12},{24,120},{28,20},{32... | collective-permute-start | bytes 1572872 | tf_op jit(solution)/shard_map/ppermute | solution.py:47
  73.0 3.6 %product.4 = (bf16[320,512]{1,0:T(8,128)(2,1)S(1)}, bf16[320,512]{1,0:T(8,128)(2,1)S(1)}, bf16[320,512]{1,0:T(8,128)(2,1)S(1)}, bf16[320,512]{1,0:T(8,128)(2,1)S(1)}) custom-call(s32[4]{0:T(128)S(1)} %pad_add_fusion.place_ref, bf16[1280,512]{1,0:T(8,128)(2,1)S(1)} %get-tuple-element.32.refs_0_, bf16[1280,512]{1,0:T(8,128)(2,1)S(1)} %collective-permute-done.2.refs_1_, ...), custom_call_target="tpu_custom_call" | custom-call | flops 2684354560 | bytes 7340032 | tf_op jit(solution)/shard_map/product/pallas_call | solution.py:234
  78.4 6.5 %product.5 = (bf16[320,1024]{1,0:T(8,128)(2,1)S(1)}, bf16[320,1024]{1,0:T(8,128)(2,1)S(1)}, bf16[320,1024]{1,0:T(8,128)(2,1)S(1)}, bf16[320,1024]{1,0:T(8,128)(2,1)S(1)}) custom-call(s32[4]{0:T(128)S(1)} %pad_add_fusion.place_ref, bf16[1280,512]{1,0:T(8,128)(2,1)S(1)} %get-tuple-element.32.refs_0_, bf16[1280,512]{1,0:T(8,128)(2,1)S(1)} %collective-permute-done.2.refs_1_, ...), custom_call_target="tpu_custom_call" | custom-call | flops 5368709120 | bytes 7340032 | tf_op jit(solution)/shard_map/product/pallas_call | solution.py:234
  87.5 3.0 %collective-permute-start.23 = (bf16[320,1024]{1,0:T(8,128)(2,1)S(1)}, bf16[320,1024]{1,0:T(8,128)(2,1)S(1)}, u32[]{:S(2)}, u32[]{:S(2)}) collective-permute-start(bf16[320,1024]{1,0:T(8,128)(2,1)S(1)} %get-tuple-element.50), channel_id=1, source_target_pairs={{0,16},{4,68},{8,24},{12,76},{16,0},{20,84},{24,8},{28,92},{32,48}... | collective-permute-start | bytes 1966088 | tf_op jit(solution)/shard_map/ppermute | solution.py:51
  92.0 4.4 %collective-permute-start.18 = (bf16[320,512]{1,0:T(8,128)(2,1)S(1)}, bf16[320,512]{1,0:T(8,128)(2,1)S(1)}, u32[]{:S(2)}, u32[]{:S(2)}) collective-permute-start(bf16[320,512]{1,0:T(8,128)(2,1)S(1)} %get-tuple-element.46), channel_id=1, source_target_pairs={{0,16},{4,68},{8,24},{12,76},{16,0},{20,84},{24,8},{28,92},{32,48}... | collective-permute-start | bytes 983048 | tf_op jit(solution)/shard_map/ppermute | solution.py:51
  97.1 3.6 %product.3 = (bf16[320,512]{1,0:T(8,128)(2,1)S(1)}, bf16[320,512]{1,0:T(8,128)(2,1)S(1)}, bf16[320,512]{1,0:T(8,128)(2,1)S(1)}, bf16[320,512]{1,0:T(8,128)(2,1)S(1)}) custom-call(s32[4]{0:T(128)S(1)} %pad_add_fusion.place_ref, bf16[1280,512]{1,0:T(8,128)(2,1)S(1)} %get-tuple-element.32.refs_0_, bf16[1280,512]{1,0:T(8,128)(2,1)S(1)} %collective-permute-done.2.refs_1_, ...), custom_call_target="tpu_custom_call" | custom-call | flops 2684354560 | bytes 7340032 | tf_op jit(solution)/shard_map/product/pallas_call | solution.py:234
  100.7 6.6 %collective-permute-done.18.refs_2_ = bf16[320,512]{1,0:T(8,128)(2,1)S(1)} collective-permute-done((bf16[320,512]{1,0:T(8,128)(2,1)S(1)}, bf16[320,512]{1,0:T(8,128)(2,1)S(1)}, u32[]{:S(2)}, u32[]{:S(2)}) %collective-permute-start.18) | collective-permute-done | bytes 327712 | tf_op jit(solution)/shard_map/ppermute | solution.py:51
  107.3 3.8 %collective-permute-start.10 = (bf16[320,512]{1,0:T(8,128)(2,1)S(1)}, bf16[320,512]{1,0:T(8,128)(2,1)S(1)}, u32[]{:S(2)}, u32[]{:S(2)}) collective-permute-start(bf16[320,512]{1,0:T(8,128)(2,1)S(1)} %get-tuple-element.39), channel_id=1, source_target_pairs={{0,8},{4,36},{8,16},{12,44},{16,24},{20,52},{24,0},{28,60},{32,40}... | collective-permute-start | bytes 983048 | tf_op jit(solution)/shard_map/ppermute | solution.py:51
  111.1 2.3 %collective-permute-done.19.refs_3_ = bf16[320,512]{1,0:T(8,128)(2,1)S(1)} collective-permute-done((bf16[320,512]{1,0:T(8,128)(2,1)S(1)}, bf16[320,512]{1,0:T(8,128)(2,1)S(1)}, u32[]{:S(2)}, u32[]{:S(2)}) %collective-permute-start.19) | collective-permute-done | bytes 327712 | tf_op jit(solution)/shard_map/ppermute | solution.py:51
  117.1 2.2 %sums.2 = (f32[160,512]{1,0:T(8,128)}, f32[160,512]{1,0:T(8,128)}, f32[160,1024]{1,0:T(8,128)}, f32[160,1024]{1,0:T(8,128)}, f32[8,128]{1,0:T(8,128)S(1)}) custom-call(s32[4]{0:T(128)S(1)} %pad_add_fusion.place_ref, bf16[320,512]{1,0:T(8,128)(2,1)S(1)} %get-tuple-element.44.refs_0_, bf16[320,512]{1,0:T(8,128)(2,1)S(1)} %collective-permute-done.17.refs_1_, ...), custom_call_target="tpu_custom_call" | custom-call | flops 100000000 | bytes 4000000 | tf_op jit(solution)/shard_map/sums/pallas_call | solution.py:290
  119.3 3.3 %collective-permute-done.11.refs_2_ = bf16[320,512]{1,0:T(8,128)(2,1)S(1)} collective-permute-done((bf16[320,512]{1,0:T(8,128)(2,1)S(1)}, bf16[320,512]{1,0:T(8,128)(2,1)S(1)}, u32[]{:S(2)}, u32[]{:S(2)}) %collective-permute-start.11) | collective-permute-done | bytes 327712 | tf_op jit(solution)/shard_map/ppermute | solution.py:51
  122.6 2.8 %collective-permute-done.12.refs_3_ = bf16[320,512]{1,0:T(8,128)(2,1)S(1)} collective-permute-done((bf16[320,512]{1,0:T(8,128)(2,1)S(1)}, bf16[320,512]{1,0:T(8,128)(2,1)S(1)}, u32[]{:S(2)}, u32[]{:S(2)}) %collective-permute-start.12) | collective-permute-done | bytes 327712 | tf_op jit(solution)/shard_map/ppermute | solution.py:51
  127.4 14.7 %all_to_all.5.shared = f32[128,1,128]{2,1,0:T(1,128)} all-to-all(f32[128,1,128]{2,1,0:T(1,128)S(1)} %get-tuple-element.53), channel_id=1, replica_groups=mesh['z'=4,'x'=4,'c'=2,'y'=4] {'z','x','c','y'}, dimensions={0} | all-to-all | bytes 131072 | tf_op jit(solution)/shard_map/all_to_all | solution.py:398
  143.3 9.6 %adam.1 = (f32[160,4096]{1,0:T(8,128)}, f32[160,4096]{1,0:T(8,128)}, f32[160,4096]{1,0:T(8,128)}, bf16[160,4096]{1,0:T(8,128)(2,1)}) custom-call(s32[4]{0:T(128)} %copy-done, f32[128,1,128]{2,1,0:T(1,128)} %all_to_all.5.shared, f32[160,512]{1,0:T(8,128)} %get-tuple-element.54.refs_0_, f32[160,512]{1,0:T(8,128)} %copy-done.5, ...), custom_call_target="tpu_custom_call" | custom-call | flops 10000000 | bytes 17000000 | tf_op jit(solution)/shard_map/adam/pallas_call | solution.py:347
  (61 shorter events, 23.2 us)
Async XLA Ops:
  0.6 31.3 %collective-permute-start = (bf16[2,128,5120]{2,1,0:T(8,128)(2,1)}, bf16[2,128,5120]{2,1,0:T(8,128)(2,1)S(1)}, u32[]{:S(2)}, u32[]{:S(2)}) collective-permute-start(bf16[2,128,5120]{2,1,0:T(8,128)(2,1)} %own_ref.2), channel_id=1, source_target_pairs={{0,4},{4,0},{1,5},{5,1},{2,6},{6,2},{3,7},{7,3},{8,12},{12,8},{9,1... | collective-permute-start | bytes 7864328 | tf_op jit(solution)/shard_map/ppermute | solution.py:59
  0.7 38.8 %collective-permute-start.5 = (bf16[2,128,4096]{2,1,0:T(8,128)(2,1)}, bf16[2,128,4096]{2,1,0:T(8,128)(2,1)}, u32[]{:S(2)}, u32[]{:S(2)}) collective-permute-start(bf16[2,128,4096]{2,1,0:T(8,128)(2,1)} %theirs_ref.1), channel_id=1, source_target_pairs={{0,4},{4,0},{1,5},{5,1},{2,6},{6,2},{3,7},{7,3},{8,12},{12,8},{9,1... | collective-permute-start | bytes 6291464 | tf_op jit(solution)/shard_map/ppermute | solution.py:59
  9.2 11.4 %collective-permute-start.14 = (bf16[512,512]{1,0:T(8,128)(2,1)S(1)}, bf16[512,512]{1,0:T(8,128)(2,1)S(1)}, u32[]{:S(2)}, u32[]{:S(2)}) collective-permute-start(bf16[512,512]{1,0:T(8,128)(2,1)S(1)} %constant_dynamic-update-slice_fusion), channel_id=1, source_target_pairs={{0,32},{4,12},{8,40},{12,20},{16,48},{20,28},{24,56},{28,4},{32,64... | collective-permute-start | bytes 1572872 | tf_op jit(solution)/shard_map/ppermute | solution.py:47
  11.3 16.4 %collective-permute-start.15 = (bf16[512,512]{1,0:T(8,128)(2,1)S(1)}, bf16[512,512]{1,0:T(8,128)(2,1)S(1)}, u32[]{:S(2)}, u32[]{:S(2)}) collective-permute-start(bf16[512,512]{1,0:T(8,128)(2,1)S(1)} %constant_dynamic-update-slice_fusion), channel_id=1, source_target_pairs={{0,64},{4,20},{8,72},{12,28},{16,80},{20,4},{24,88},{28,12},{32,96... | collective-permute-start | bytes 1572872 | tf_op jit(solution)/shard_map/ppermute | solution.py:47
  14.9 12.8 %collective-permute-start.16 = (bf16[512,512]{1,0:T(8,128)(2,1)S(1)}, bf16[512,512]{1,0:T(8,128)(2,1)S(1)}, u32[]{:S(2)}, u32[]{:S(2)}) collective-permute-start(bf16[512,512]{1,0:T(8,128)(2,1)S(1)} %constant_dynamic-update-slice_fusion), channel_id=1, source_target_pairs={{0,96},{4,28},{8,104},{12,4},{16,112},{20,12},{24,120},{28,20},{32... | collective-permute-start | bytes 1572872 | tf_op jit(solution)/shard_map/ppermute | solution.py:47
  20.6 16.8 %collective-permute-start.6 = (bf16[2,32]{1,0:T(2,128)(2,1)S(1)}, bf16[2,32]{1,0:T(2,128)(2,1)S(1)}, u32[]{:S(2)}, u32[]{:S(2)}) collective-permute-start(bf16[2,32]{1,0:T(2,128)(2,1)S(1)} %copy-done.2), channel_id=1, source_target_pairs={{0,4},{4,0},{1,5},{5,1},{2,6},{6,2},{3,7},{7,3},{8,12},{12,8},{9,1... | collective-permute-start | bytes 392 | tf_op jit(solution)/shard_map/ppermute | solution.py:59
  27.9 48.8 %collective-permute-start.20 = (bf16[3,512,512]{2,1,0:T(8,128)(2,1)S(1)}, bf16[3,512,512]{2,1,0:T(8,128)(2,1)S(1)}, u32[]{:S(2)}, u32[]{:S(2)}) collective-permute-start(bf16[3,512,512]{2,1,0:T(8,128)(2,1)S(1)} %pad_maximum_fusion.refs_5_), channel_id=1, source_target_pairs={{0,1},{1,2},{2,3},{3,0},{4,5},{5,6},{6,7},{7,4},{8,9},{9,10},{10,1... | collective-permute-start | bytes 4718600 | tf_op jit(solution)/shard_map/ppermute | solution.py:55
  29.5 48.9 %collective-permute-start.21 = (bf16[3,512,512]{2,1,0:T(8,128)(2,1)S(1)}, bf16[3,512,512]{2,1,0:T(8,128)(2,1)S(1)}, u32[]{:S(2)}, u32[]{:S(2)}) collective-permute-start(bf16[3,512,512]{2,1,0:T(8,128)(2,1)S(1)} %pad_maximum_fusion.refs_5_), channel_id=1, source_target_pairs={{0,3},{1,0},{2,1},{3,2},{4,7},{5,4},{6,5},{7,6},{8,11},{9,8},{10,9... | collective-permute-start | bytes 4718600 | tf_op jit(solution)/shard_map/ppermute | solution.py:55
  36.5 32.9 %collective-permute-start.2 = (bf16[1280,512]{1,0:T(8,128)(2,1)S(1)}, bf16[1280,512]{1,0:T(8,128)(2,1)S(1)}, u32[]{:S(2)}, u32[]{:S(2)}) collective-permute-start(bf16[1280,512]{1,0:T(8,128)(2,1)S(1)} %get-tuple-element.33), channel_id=1, source_target_pairs={{0,32},{4,12},{8,40},{12,20},{16,48},{20,28},{24,56},{28,4},{32,64... | collective-permute-start | bytes 3932168 | tf_op jit(solution)/shard_map/ppermute | solution.py:47
  37.4 32.1 %collective-permute-start.3 = (bf16[1280,512]{1,0:T(8,128)(2,1)S(1)}, bf16[1280,512]{1,0:T(8,128)(2,1)S(1)}, u32[]{:S(2)}, u32[]{:S(2)}) collective-permute-start(bf16[1280,512]{1,0:T(8,128)(2,1)S(1)} %get-tuple-element.34), channel_id=1, source_target_pairs={{0,64},{4,20},{8,72},{12,28},{16,80},{20,4},{24,88},{28,12},{32,96... | collective-permute-start | bytes 3932168 | tf_op jit(solution)/shard_map/ppermute | solution.py:47
  39.5 31.1 %collective-permute-start.4 = (bf16[1280,512]{1,0:T(8,128)(2,1)S(1)}, bf16[1280,512]{1,0:T(8,128)(2,1)S(1)}, u32[]{:S(2)}, u32[]{:S(2)}) collective-permute-start(bf16[1280,512]{1,0:T(8,128)(2,1)S(1)} %get-tuple-element.35), channel_id=1, source_target_pairs={{0,96},{4,28},{8,104},{12,4},{16,112},{20,12},{24,120},{28,20},{32... | collective-permute-start | bytes 3932168 | tf_op jit(solution)/shard_map/ppermute | solution.py:47
  69.5 18.1 %collective-permute-start.7 = (bf16[512,512]{1,0:T(8,128)(2,1)S(1)}, bf16[512,512]{1,0:T(8,128)(2,1)S(1)}, u32[]{:S(2)}, u32[]{:S(2)}) collective-permute-start(bf16[512,512]{1,0:T(8,128)(2,1)S(1)} %get-tuple-element.37), channel_id=1, source_target_pairs={{0,32},{4,12},{8,40},{12,20},{16,48},{20,28},{24,56},{28,4},{32,64... | collective-permute-start | bytes 1572872 | tf_op jit(solution)/shard_map/ppermute | solution.py:47
  69.5 21.1 %collective-permute-start.8 = (bf16[512,512]{1,0:T(8,128)(2,1)S(1)}, bf16[512,512]{1,0:T(8,128)(2,1)S(1)}, u32[]{:S(2)}, u32[]{:S(2)}) collective-permute-start(bf16[512,512]{1,0:T(8,128)(2,1)S(1)} %get-tuple-element.37), channel_id=1, source_target_pairs={{0,64},{4,20},{8,72},{12,28},{16,80},{20,4},{24,88},{28,12},{32,96... | collective-permute-start | bytes 1572872 | tf_op jit(solution)/shard_map/ppermute | solution.py:47
  70.6 21.4 %collective-permute-start.9 = (bf16[512,512]{1,0:T(8,128)(2,1)S(1)}, bf16[512,512]{1,0:T(8,128)(2,1)S(1)}, u32[]{:S(2)}, u32[]{:S(2)}) collective-permute-start(bf16[512,512]{1,0:T(8,128)(2,1)S(1)} %get-tuple-element.37), channel_id=1, source_target_pairs={{0,96},{4,28},{8,104},{12,4},{16,112},{20,12},{24,120},{28,20},{32... | collective-permute-start | bytes 1572872 | tf_op jit(solution)/shard_map/ppermute | solution.py:47
  76.6 19.8 %collective-permute-start.17 = (bf16[320,512]{1,0:T(8,128)(2,1)S(1)}, bf16[320,512]{1,0:T(8,128)(2,1)S(1)}, u32[]{:S(2)}, u32[]{:S(2)}) collective-permute-start(bf16[320,512]{1,0:T(8,128)(2,1)S(1)} %get-tuple-element.45), channel_id=1, source_target_pairs={{0,8},{4,36},{8,16},{12,44},{16,24},{20,52},{24,0},{28,60},{32,40}... | collective-permute-start | bytes 983048 | tf_op jit(solution)/shard_map/ppermute | solution.py:51
  84.9 30.2 %collective-permute-start.22 = (bf16[320,1024]{1,0:T(8,128)(2,1)S(1)}, bf16[320,1024]{1,0:T(8,128)(2,1)S(1)}, u32[]{:S(2)}, u32[]{:S(2)}) collective-permute-start(bf16[320,1024]{1,0:T(8,128)(2,1)S(1)} %get-tuple-element.49), channel_id=1, source_target_pairs={{0,8},{4,36},{8,16},{12,44},{16,24},{20,52},{24,0},{28,60},{32,40}... | collective-permute-start | bytes 1966088 | tf_op jit(solution)/shard_map/ppermute | solution.py:51
  87.5 29.6 %collective-permute-start.23 = (bf16[320,1024]{1,0:T(8,128)(2,1)S(1)}, bf16[320,1024]{1,0:T(8,128)(2,1)S(1)}, u32[]{:S(2)}, u32[]{:S(2)}) collective-permute-start(bf16[320,1024]{1,0:T(8,128)(2,1)S(1)} %get-tuple-element.50), channel_id=1, source_target_pairs={{0,16},{4,68},{8,24},{12,76},{16,0},{20,84},{24,8},{28,92},{32,48}... | collective-permute-start | bytes 1966088 | tf_op jit(solution)/shard_map/ppermute | solution.py:51
  90.5 26.6 %collective-permute-start.24 = (bf16[320,1024]{1,0:T(8,128)(2,1)S(1)}, bf16[320,1024]{1,0:T(8,128)(2,1)S(1)}, u32[]{:S(2)}, u32[]{:S(2)}) collective-permute-start(bf16[320,1024]{1,0:T(8,128)(2,1)S(1)} %get-tuple-element.51), channel_id=1, source_target_pairs={{0,24},{4,100},{8,0},{12,108},{16,8},{20,116},{24,16},{28,124},{32... | collective-permute-start | bytes 1966088 | tf_op jit(solution)/shard_map/ppermute | solution.py:51
  92.0 15.3 %collective-permute-start.18 = (bf16[320,512]{1,0:T(8,128)(2,1)S(1)}, bf16[320,512]{1,0:T(8,128)(2,1)S(1)}, u32[]{:S(2)}, u32[]{:S(2)}) collective-permute-start(bf16[320,512]{1,0:T(8,128)(2,1)S(1)} %get-tuple-element.46), channel_id=1, source_target_pairs={{0,16},{4,68},{8,24},{12,76},{16,0},{20,84},{24,8},{28,92},{32,48}... | collective-permute-start | bytes 983048 | tf_op jit(solution)/shard_map/ppermute | solution.py:51
  96.4 16.9 %collective-permute-start.19 = (bf16[320,512]{1,0:T(8,128)(2,1)S(1)}, bf16[320,512]{1,0:T(8,128)(2,1)S(1)}, u32[]{:S(2)}, u32[]{:S(2)}) collective-permute-start(bf16[320,512]{1,0:T(8,128)(2,1)S(1)} %get-tuple-element.47), channel_id=1, source_target_pairs={{0,24},{4,100},{8,0},{12,108},{16,8},{20,116},{24,16},{28,124},{32... | collective-permute-start | bytes 983048 | tf_op jit(solution)/shard_map/ppermute | solution.py:51
  107.3 12.0 %collective-permute-start.10 = (bf16[320,512]{1,0:T(8,128)(2,1)S(1)}, bf16[320,512]{1,0:T(8,128)(2,1)S(1)}, u32[]{:S(2)}, u32[]{:S(2)}) collective-permute-start(bf16[320,512]{1,0:T(8,128)(2,1)S(1)} %get-tuple-element.39), channel_id=1, source_target_pairs={{0,8},{4,36},{8,16},{12,44},{16,24},{20,52},{24,0},{28,60},{32,40}... | collective-permute-start | bytes 983048 | tf_op jit(solution)/shard_map/ppermute | solution.py:51
  119.3 22.9 %collective-permute-start.26 = (f32[160,1024]{1,0:T(8,128)}, f32[160,1024]{1,0:T(8,128)S(1)}, u32[]{:S(2)}, u32[]{:S(2)}) collective-permute-start(f32[160,1024]{1,0:T(8,128)} %get-tuple-element.57), channel_id=1, source_target_pairs={{0,4},{4,0},{1,5},{5,1},{2,6},{6,2},{3,7},{7,3},{8,12},{12,8},{9,1... | collective-permute-start | bytes 1966088 | tf_op jit(solution)/shard_map/ppermute | solution.py:59
  126.9 15.2 %collective-permute-start.27 = (f32[160,512]{1,0:T(8,128)}, f32[160,512]{1,0:T(8,128)S(1)}, u32[]{:S(2)}, u32[]{:S(2)}) collective-permute-start(f32[160,512]{1,0:T(8,128)} %get-tuple-element.59), channel_id=1, source_target_pairs={{0,4},{4,0},{1,5},{5,1},{2,6},{6,2},{3,7},{7,3},{8,12},{12,8},{9,1... | collective-permute-start | bytes 983048 | tf_op jit(solution)/shard_map/ppermute | solution.py:59
  126.9 15.2 %collective-permute-start.25 = (f32[160,512]{1,0:T(8,128)}, f32[160,512]{1,0:T(8,128)S(1)}, u32[]{:S(2)}, u32[]{:S(2)}) collective-permute-start(f32[160,512]{1,0:T(8,128)} %get-tuple-element.55), channel_id=1, source_target_pairs={{0,4},{4,0},{1,5},{5,1},{2,6},{6,2},{3,7},{7,3},{8,12},{12,8},{9,1... | collective-permute-start | bytes 983048 | tf_op jit(solution)/shard_map/ppermute | solution.py:59
  (11 other events, 186.1 us)

commit v3 on v2

--- a/solution.py
+++ b/solution.py
@@ -107,7 +107,7 @@
         compiler_params=pltpu.CompilerParams(vmem_limit_bytes=8 * 2**20),
         cost_estimate=pl.CostEstimate(flops=10**6, bytes_accessed=10**6, transcendentals=0),
         name="slab",
-    )(place, acts, acts, act_scale)
+    )(place, acts, acts, pltpu.with_memory_space_constraint(act_scale, pltpu.HBM))
 
 
 def acts_kernel(place_ref, own_ref, other_ref, own_scale_ref, other_scale_ref, whole_ref, opposite_ref):
@@ -270,7 +270,7 @@
             value = parts[4 * n][at, :].astype(jnp.float32)
             for k in range(1, 4):
                 value = value + parts[4 * n + k][at, :].astype(jnp.float32)
-            refs[2 * n + side][...] = value
+            refs[2 * n + side][...] = value.astype(jnp.bfloat16)
             term = folded(value * value)
             squares = term if squares is None else squares + term
     if last:
@@ -285,7 +285,7 @@
     shapes = []
     for piece in pieces:
         both, width = piece[0].shape
-        shapes += [pltpu.HBM((both // 2, width), jnp.float32)] * 2
+        shapes += [pltpu.HBM((both // 2, width), jnp.bfloat16)] * 2
     shapes.append(jax.ShapeDtypeStruct((128, 1, 128) if last else (8, 128), jnp.float32))
     *values, squares = pl.pallas_call(
         functools.partial(sums_kernel, len(pieces), last),
@@ -300,66 +300,73 @@
 
 
 def adam_kernel(slots, place_ref, shared, *refs):
-    grads, refs = refs[:-8], refs[-8:]
-    moment, second, master, out_moment, out_second, out_master, out_weights, grad = refs
-    step = pl.program_id(0)
-    wide = grad.shape[1] // 2
-    core = place_ref[2]
-    for n, (_, which, _) in enumerate(slots):
-
-        @pl.when(step == n)
-        def _(which=which):
-            grad[:, pl.ds(pl.multiple_of(core * wide, wide), wide)] = grads[2 * which][...]
-            grad[:, pl.ds(pl.multiple_of((1 - core) * wide, wide), wide)] = grads[2 * which + 1][...]
+    count = 2 * len({which for _, which, _ in slots})
+    grads, refs = refs[:count], refs[count:]
+    sources, targets = refs[:3], refs[3:7]
+    grad_in, read, written, weights_out, in_sems, out_sems = refs[7:]
+    piece = grad_in.shape[2]
+    core, y = place_ref[2], place_ref[3]
+    blocks = [(offset, which, lead, side) for offset, which, lead in slots for side in range(2)]
+    ats, fetches = [], []
+    for n, (offset, which, lead, side) in enumerate(blocks):
+        half = core if side == 0 else 1 - core
+        at = pl.ds(pl.multiple_of((2 * lax.rem(y + offset, 4) + half) * piece, piece), piece)
+        ats.append(at)
+        from_grad = grads[2 * which + side].at[:, lead * piece : (lead + 1) * piece]
+        copies = [pltpu.make_async_copy(from_grad, grad_in.at[n], in_sems.at[n, 3])]
+        for i, source in enumerate(sources):
+            copies.append(pltpu.make_async_copy(source.at[:, at], read.at[n, i], in_sems.at[n, i]))
+        for copy in copies:
+            copy.start()
+        fetches.append(copies)
 
     norm = jnp.sqrt(jnp.sum(shared[...], axis=0))
     factor = jnp.minimum(1.0, clip_rms * jnp.sqrt(jnp.float32(FF * ROWS)) / norm)
-    clipped = factor[0:1, 0:1] * grad[...]
-    new_moment = beta_first * moment[...] + (1.0 - beta_first) * clipped
-    new_second = beta_second * second[...] + (1.0 - beta_second) * clipped * clipped
-    new_master = master[...] - learn_rate * new_moment / (jnp.sqrt(new_second) + adam_eps)
-    out_moment[...] = new_moment
-    out_second[...] = new_second
-    out_master[...] = new_master
-    out_weights[...] = new_master.astype(jnp.bfloat16)
-
-
-def chosen(j, values):
-    found = values[0]
-    for n, value in enumerate(values[1:], 1):
-        found = jnp.where(j == n, value, found)
-    return found
+    stores = []
+    for n, at in enumerate(ats):
+        for copy in fetches[n]:
+            copy.wait()
+        clipped = factor[0:1, 0:1] * grad_in[n].astype(jnp.float32)
+        new_moment = beta_first * read[n, 0] + (1.0 - beta_first) * clipped
+        new_second = beta_second * read[n, 1] + (1.0 - beta_second) * clipped * clipped
+        new_master = read[n, 2] - learn_rate * new_moment / (jnp.sqrt(new_second) + adam_eps)
+        written[n, 0] = new_moment
+        written[n, 1] = new_second
+        written[n, 2] = new_master
+        weights_out[n] = new_master.astype(jnp.bfloat16)
+        for i, target in enumerate(targets):
+            result = weights_out.at[n] if i == 3 else written.at[n, i]
+            copy = pltpu.make_async_copy(result, target.at[:, at], out_sems.at[n, i])
+            copy.start()
+            stores.append(copy)
+    for copy in stores:
+        copy.wait()
 
 
 def adam(place, slots, shared, pairs, moment, second, master):
     own, rows = moment.shape
-    quarter = rows // 4
-    block = pl.BlockSpec((own, quarter), lambda j, p: (0, lax.rem(p[3] + chosen(j, [s[0] for s in slots]), 4)))
-
-    def source(i):
-        at, blocks = 0, []
-        for _, which, lead in slots:
-            at = lead if which == i else at
-            blocks.append(at)
-        return [pl.BlockSpec((own, quarter // 2), lambda j, p: (0, chosen(j, blocks)))] * 2
-
+    piece = rows // 8
+    hbm = pl.BlockSpec(memory_space=pltpu.HBM)
     wide = jax.ShapeDtypeStruct((own, rows), jnp.float32)
+    flat = [a for pair in pairs for a in pair] + [moment, second, master]
+    flat = [pltpu.with_memory_space_constraint(a, pltpu.HBM) for a in flat]
     return pl.pallas_call(
         functools.partial(adam_kernel, slots),
-        grid_spec=pltpu.PrefetchScalarGridSpec(
-            num_scalar_prefetch=1,
-            grid=(len(slots),),
-            in_specs=[pl.BlockSpec(shared.shape, lambda j, p: (0, 0, 0))]
-            + [spec for i in range(len(pairs)) for spec in source(i)]
-            + [block] * 3,
-            out_specs=[block] * 4,
-            scratch_shapes=[pltpu.VMEM((own, quarter), jnp.float32)],
-        ),
+        in_specs=[SCALARS, WHOLE] + [hbm] * len(flat),
+        out_specs=[hbm] * 4,
+        scratch_shapes=[
+            pltpu.VMEM((8, own, piece), jnp.bfloat16),
+            pltpu.VMEM((8, 3, own, piece), jnp.float32),
+            pltpu.VMEM((8, 3, own, piece), jnp.float32),
+            pltpu.VMEM((8, own, piece), jnp.bfloat16),
+            pltpu.SemaphoreType.DMA((8, 4)),
+            pltpu.SemaphoreType.DMA((8, 4)),
+        ],
         out_shape=[wide, wide, wide, jax.ShapeDtypeStruct((own, rows), jnp.bfloat16)],
         compiler_params=pltpu.CompilerParams(vmem_limit_bytes=60 * 2**20),
         cost_estimate=pl.CostEstimate(flops=10**7, bytes_accessed=17 * 10**6, transcendentals=10**6),
         name="adam",
-    )(place, shared, *[a for pair in pairs for a in pair], moment, second, master)
+    )(place, shared, *flat)
 
 
 PRODUCTS = ((0,), (3, 1), (2,))
@@ -394,7 +401,7 @@
     kept, given, squares = sums(place, pieces[:EARLY])
     more_kept, more_given, squares = sums(place, pieces[EARLY:], squares)
     kept, given = kept + more_kept, given + more_given
-    pairs = [(own, pltpu.with_memory_space_constraint(swapped(other), pltpu.HBM)) for own, other in zip(kept, given)]
+    pairs = [(own, swapped(other)) for own, other in zip(kept, given)]
     shared = lax.all_to_all(squares, ALL, 0, 0, tiled=True)
     return tuple(adam(place, slots, shared, pairs, moment, second, master))
 

time: 154 us -> 153 us (level)
  no operation moved by 1% of the time
where the time goes in v3:
time: 153 us; the launch traced here: 152 us
  waiting for transfers between devices  58.9 us (38%)
  starting transfers between devices  40.4 us (26%)
  Pallas kernels  35.7 us (23%)
  blocking collectives  14.7 us (10%)
    ppermute x9, waiting for transfers between devices, gathered(): return lax.ppermute(a, DP, crossed(k, True))  37.7 us
    ppermute x9, starting transfers between devices, scattered(): return lax.ppermute(a, DP, crossed(k, False))  20.4 us
    ppermute x9, waiting for transfers between devices, scattered(): return lax.ppermute(a, DP, crossed(k, False))  15.3 us
    all_to_all x1, blocking collectives, step(): shared = lax.all_to_all(squares, ALL, 0, 0, tiled=True)  14.7 us
    ppermute x9, starting transfers between devices, gathered(): return lax.ppermute(a, DP, crossed(k, True))  14.7 us
    pallas_call x3, Pallas kernels, product(): pl.pallas_call(functools.partial(product_kernel, offsets, forms, width),...  13.7 us
    pallas_call x1, Pallas kernels, adam(): pl.pallas_call(functools.partial(adam_kernel, slots), in_specs=[SCALARS,...  8.71 us
    ppermute x8, waiting for transfers between devices, swapped(): return lax.ppermute(a, 'c', SWAP)  5.91 us
  transfers between devices with their start and end apart: 28, of which 9 were waited for; matrix products, arithmetic and copies ran while one was open for 0% of the time, Pallas kernels for 18%

profile of v3, /device:TPU:0, one launch (start us, length us, event | category | flops | bytes accessed | tf_op | source)
XLA Modules:
  0.0 151.8 jit_solution(779088175373766982)
XLA Ops:
  3.3 5.9 %collective-permute-done.13 = bf16[256,512]{1,0:T(8,128)(2,1)S(1)} collective-permute-done((bf16[256,512]{1,0:T(8,128)(2,1)S(1)}, bf16[256,512]{1,0:T(8,128)(2,1)S(1)}, u32[]{:S(2)}, u32[]{:S(2)}) %collective-permute-start.13) | collective-permute-done | bytes 262176 | tf_op jit(solution)/shard_map/ppermute | solution.py:59
  9.2 2.1 %collective-permute-start.14 = (bf16[512,512]{1,0:T(8,128)(2,1)S(1)}, bf16[512,512]{1,0:T(8,128)(2,1)S(1)}, u32[]{:S(2)}, u32[]{:S(2)}) collective-permute-start(bf16[512,512]{1,0:T(8,128)(2,1)S(1)} %constant_dynamic-update-slice_fusion), channel_id=1, source_target_pairs={{0,32},{4,12},{8,40},{12,20},{16,48},{20,28},{24,56},{28,4},{32,64... | collective-permute-start | bytes 1572872 | tf_op jit(solution)/shard_map/ppermute | solution.py:47
  11.3 3.6 %collective-permute-start.15 = (bf16[512,512]{1,0:T(8,128)(2,1)S(1)}, bf16[512,512]{1,0:T(8,128)(2,1)S(1)}, u32[]{:S(2)}, u32[]{:S(2)}) collective-permute-start(bf16[512,512]{1,0:T(8,128)(2,1)S(1)} %constant_dynamic-update-slice_fusion), channel_id=1, source_target_pairs={{0,64},{4,20},{8,72},{12,28},{16,80},{20,4},{24,88},{28,12},{32,96... | collective-permute-start | bytes 1572872 | tf_op jit(solution)/shard_map/ppermute | solution.py:47
  16.0 4.6 %collective-permute-done.14 = bf16[512,512]{1,0:T(8,128)(2,1)S(1)} collective-permute-done((bf16[512,512]{1,0:T(8,128)(2,1)S(1)}, bf16[512,512]{1,0:T(8,128)(2,1)S(1)}, u32[]{:S(2)}, u32[]{:S(2)}) %collective-permute-start.14) | collective-permute-done | bytes 524320 | tf_op jit(solution)/shard_map/ppermute | solution.py:47
  20.6 7.1 %collective-permute-done.15 = bf16[512,512]{1,0:T(8,128)(2,1)S(1)} collective-permute-done((bf16[512,512]{1,0:T(8,128)(2,1)S(1)}, bf16[512,512]{1,0:T(8,128)(2,1)S(1)}, u32[]{:S(2)}, u32[]{:S(2)}) %collective-permute-start.15) | collective-permute-done | bytes 524320 | tf_op jit(solution)/shard_map/ppermute | solution.py:47
  29.5 2.4 %collective-permute-start.21 = (bf16[3,512,512]{2,1,0:T(8,128)(2,1)S(1)}, bf16[3,512,512]{2,1,0:T(8,128)(2,1)S(1)}, u32[]{:S(2)}, u32[]{:S(2)}) collective-permute-start(bf16[3,512,512]{2,1,0:T(8,128)(2,1)S(1)} %pad_maximum_fusion.refs_5_), channel_id=1, source_target_pairs={{0,3},{1,0},{2,1},{3,2},{4,7},{5,4},{6,5},{7,6},{8,11},{9,8},{10,9... | collective-permute-start | bytes 4718600 | tf_op jit(solution)/shard_map/ppermute | solution.py:55
  31.9 4.6 %prep.1 = (bf16[1280,512]{1,0:T(8,128)(2,1)S(1)}, bf16[1280,512]{1,0:T(8,128)(2,1)S(1)}, bf16[1280,512]{1,0:T(8,128)(2,1)S(1)}, bf16[1280,512]{1,0:T(8,128)(2,1)S(1)}) custom-call(s32[4]{0:T(128)S(1)} %pad_add_fusion.place_ref, bf16[2,128,5120]{2,1,0:T(8,128)(2,1)} %own_ref.2, bf16[2,128,5120]{2,1,0:T(8,128)(2,1)S(1)} %collective-permute-done.other_ref, ...), custom_call_target="tpu_custom_call" | custom-call | flops 1000000000 | bytes 10485760 | tf_op jit(solution)/shard_map/prep/pallas_call | solution.py:182
  37.4 2.1 %collective-permute-start.3 = (bf16[1280,512]{1,0:T(8,128)(2,1)S(1)}, bf16[1280,512]{1,0:T(8,128)(2,1)S(1)}, u32[]{:S(2)}, u32[]{:S(2)}) collective-permute-start(bf16[1280,512]{1,0:T(8,128)(2,1)S(1)} %get-tuple-element.34), channel_id=1, source_target_pairs={{0,64},{4,20},{8,72},{12,28},{16,80},{20,4},{24,88},{28,12},{32,96... | collective-permute-start | bytes 3932168 | tf_op jit(solution)/shard_map/ppermute | solution.py:47
  41.0 3.5 %acts.1 = (bf16[512,2048]{1,0:T(8,128)(2,1)S(1)}, bf16[512,512]{1,0:T(8,128)(2,1)S(1)}) custom-call(s32[4]{0:T(128)S(1)} %pad_add_fusion.place_ref, bf16[2,128,4096]{2,1,0:T(8,128)(2,1)} %theirs_ref.1, bf16[2,128,4096]{2,1,0:T(8,128)(2,1)} %collective-permute-done.5.other_ref, bf16[2,32]{1,0:T(2,128)(2,1)S(1)} %copy-done.1, ...), custom_call_target="tpu_custom_call" | custom-call | flops 1000000 | bytes 4000000 | tf_op jit(solution)/shard_map/acts/pallas_call | solution.py:131
  44.6 24.9 %collective-permute-done.2.refs_1_ = bf16[1280,512]{1,0:T(8,128)(2,1)S(1)} collective-permute-done((bf16[1280,512]{1,0:T(8,128)(2,1)S(1)}, bf16[1280,512]{1,0:T(8,128)(2,1)S(1)}, u32[]{:S(2)}, u32[]{:S(2)}) %collective-permute-start.2) | collective-permute-done | bytes 1310752 | tf_op jit(solution)/shard_map/ppermute | solution.py:47
  70.6 2.4 %collective-permute-start.9 = (bf16[512,512]{1,0:T(8,128)(2,1)S(1)}, bf16[512,512]{1,0:T(8,128)(2,1)S(1)}, u32[]{:S(2)}, u32[]{:S(2)}) collective-permute-start(bf16[512,512]{1,0:T(8,128)(2,1)S(1)} %get-tuple-element.37), channel_id=1, source_target_pairs={{0,96},{4,28},{8,104},{12,4},{16,112},{20,12},{24,120},{28,20},{32... | collective-permute-start | bytes 1572872 | tf_op jit(solution)/shard_map/ppermute | solution.py:47
  73.0 3.6 %product.4 = (bf16[320,512]{1,0:T(8,128)(2,1)S(1)}, bf16[320,512]{1,0:T(8,128)(2,1)S(1)}, bf16[320,512]{1,0:T(8,128)(2,1)S(1)}, bf16[320,512]{1,0:T(8,128)(2,1)S(1)}) custom-call(s32[4]{0:T(128)S(1)} %pad_add_fusion.place_ref, bf16[1280,512]{1,0:T(8,128)(2,1)S(1)} %get-tuple-element.32.refs_0_, bf16[1280,512]{1,0:T(8,128)(2,1)S(1)} %collective-permute-done.2.refs_1_, ...), custom_call_target="tpu_custom_call" | custom-call | flops 2684354560 | bytes 7340032 | tf_op jit(solution)/shard_map/product/pallas_call | solution.py:234
  78.4 6.5 %product.5 = (bf16[320,1024]{1,0:T(8,128)(2,1)S(1)}, bf16[320,1024]{1,0:T(8,128)(2,1)S(1)}, bf16[320,1024]{1,0:T(8,128)(2,1)S(1)}, bf16[320,1024]{1,0:T(8,128)(2,1)S(1)}) custom-call(s32[4]{0:T(128)S(1)} %pad_add_fusion.place_ref, bf16[1280,512]{1,0:T(8,128)(2,1)S(1)} %get-tuple-element.32.refs_0_, bf16[1280,512]{1,0:T(8,128)(2,1)S(1)} %collective-permute-done.2.refs_1_, ...), custom_call_target="tpu_custom_call" | custom-call | flops 5368709120 | bytes 7340032 | tf_op jit(solution)/shard_map/product/pallas_call | solution.py:234
  87.5 3.0 %collective-permute-start.23 = (bf16[320,1024]{1,0:T(8,128)(2,1)S(1)}, bf16[320,1024]{1,0:T(8,128)(2,1)S(1)}, u32[]{:S(2)}, u32[]{:S(2)}) collective-permute-start(bf16[320,1024]{1,0:T(8,128)(2,1)S(1)} %get-tuple-element.50), channel_id=1, source_target_pairs={{0,16},{4,68},{8,24},{12,76},{16,0},{20,84},{24,8},{28,92},{32,48}... | collective-permute-start | bytes 1966088 | tf_op jit(solution)/shard_map/ppermute | solution.py:51
  92.0 4.4 %collective-permute-start.18 = (bf16[320,512]{1,0:T(8,128)(2,1)S(1)}, bf16[320,512]{1,0:T(8,128)(2,1)S(1)}, u32[]{:S(2)}, u32[]{:S(2)}) collective-permute-start(bf16[320,512]{1,0:T(8,128)(2,1)S(1)} %get-tuple-element.46), channel_id=1, source_target_pairs={{0,16},{4,68},{8,24},{12,76},{16,0},{20,84},{24,8},{28,92},{32,48}... | collective-permute-start | bytes 983048 | tf_op jit(solution)/shard_map/ppermute | solution.py:51
  97.1 3.6 %product.3 = (bf16[320,512]{1,0:T(8,128)(2,1)S(1)}, bf16[320,512]{1,0:T(8,128)(2,1)S(1)}, bf16[320,512]{1,0:T(8,128)(2,1)S(1)}, bf16[320,512]{1,0:T(8,128)(2,1)S(1)}) custom-call(s32[4]{0:T(128)S(1)} %pad_add_fusion.place_ref, bf16[1280,512]{1,0:T(8,128)(2,1)S(1)} %get-tuple-element.32.refs_0_, bf16[1280,512]{1,0:T(8,128)(2,1)S(1)} %collective-permute-done.2.refs_1_, ...), custom_call_target="tpu_custom_call" | custom-call | flops 2684354560 | bytes 7340032 | tf_op jit(solution)/shard_map/product/pallas_call | solution.py:234
  100.7 6.6 %collective-permute-done.18.refs_2_ = bf16[320,512]{1,0:T(8,128)(2,1)S(1)} collective-permute-done((bf16[320,512]{1,0:T(8,128)(2,1)S(1)}, bf16[320,512]{1,0:T(8,128)(2,1)S(1)}, u32[]{:S(2)}, u32[]{:S(2)}) %collective-permute-start.18) | collective-permute-done | bytes 327712 | tf_op jit(solution)/shard_map/ppermute | solution.py:51
  107.3 3.8 %collective-permute-start.10 = (bf16[320,512]{1,0:T(8,128)(2,1)S(1)}, bf16[320,512]{1,0:T(8,128)(2,1)S(1)}, u32[]{:S(2)}, u32[]{:S(2)}) collective-permute-start(bf16[320,512]{1,0:T(8,128)(2,1)S(1)} %get-tuple-element.39), channel_id=1, source_target_pairs={{0,8},{4,36},{8,16},{12,44},{16,24},{20,52},{24,0},{28,60},{32,40}... | collective-permute-start | bytes 983048 | tf_op jit(solution)/shard_map/ppermute | solution.py:51
  111.1 2.3 %collective-permute-done.19.refs_3_ = bf16[320,512]{1,0:T(8,128)(2,1)S(1)} collective-permute-done((bf16[320,512]{1,0:T(8,128)(2,1)S(1)}, bf16[320,512]{1,0:T(8,128)(2,1)S(1)}, u32[]{:S(2)}, u32[]{:S(2)}) %collective-permute-start.19) | collective-permute-done | bytes 327712 | tf_op jit(solution)/shard_map/ppermute | solution.py:51
  115.1 2.0 %collective-permute-start.12 = (bf16[320,512]{1,0:T(8,128)(2,1)S(1)}, bf16[320,512]{1,0:T(8,128)(2,1)S(1)}, u32[]{:S(2)}, u32[]{:S(2)}) collective-permute-start(bf16[320,512]{1,0:T(8,128)(2,1)S(1)} %get-tuple-element.41), channel_id=1, source_target_pairs={{0,24},{4,100},{8,0},{12,108},{16,8},{20,116},{24,16},{28,124},{32... | collective-permute-start | bytes 983048 | tf_op jit(solution)/shard_map/ppermute | solution.py:51
  119.0 3.6 %collective-permute-done.11.refs_2_ = bf16[320,512]{1,0:T(8,128)(2,1)S(1)} collective-permute-done((bf16[320,512]{1,0:T(8,128)(2,1)S(1)}, bf16[320,512]{1,0:T(8,128)(2,1)S(1)}, u32[]{:S(2)}, u32[]{:S(2)}) %collective-permute-start.11) | collective-permute-done | bytes 327712 | tf_op jit(solution)/shard_map/ppermute | solution.py:51
  122.6 2.8 %collective-permute-done.12.refs_3_ = bf16[320,512]{1,0:T(8,128)(2,1)S(1)} collective-permute-done((bf16[320,512]{1,0:T(8,128)(2,1)S(1)}, bf16[320,512]{1,0:T(8,128)(2,1)S(1)}, u32[]{:S(2)}, u32[]{:S(2)}) %collective-permute-start.12) | collective-permute-done | bytes 327712 | tf_op jit(solution)/shard_map/ppermute | solution.py:51
  127.4 14.7 %all_to_all.5.shared = f32[128,1,128]{2,1,0:T(1,128)} all-to-all(f32[128,1,128]{2,1,0:T(1,128)S(1)} %get-tuple-element.53), channel_id=1, replica_groups=mesh['z'=4,'x'=4,'c'=2,'y'=4] {'z','x','c','y'}, dimensions={0} | all-to-all | bytes 131072 | tf_op jit(solution)/shard_map/all_to_all | solution.py:405
  143.0 8.7 %adam.1 = (f32[160,4096]{1,0:T(8,128)}, f32[160,4096]{1,0:T(8,128)}, f32[160,4096]{1,0:T(8,128)}, bf16[160,4096]{1,0:T(8,128)(2,1)}) custom-call(s32[4]{0:T(128)} %copy-done, f32[128,1,128]{2,1,0:T(1,128)} %all_to_all.5.shared, bf16[160,512]{1,0:T(8,128)(2,1)} %get-tuple-element.54.refs_0_, bf16[160,512]{1,0:T(8,128)(2,1)} %copy-done.4, ...), custom_call_target="tpu_custom_call" | custom-call | flops 10000000 | bytes 17000000 | tf_op jit(solution)/shard_map/adam/pallas_call | solution.py:353
  (59 shorter events, 22.1 us)
Async XLA Ops:
  0.6 31.3 %collective-permute-start = (bf16[2,128,5120]{2,1,0:T(8,128)(2,1)}, bf16[2,128,5120]{2,1,0:T(8,128)(2,1)S(1)}, u32[]{:S(2)}, u32[]{:S(2)}) collective-permute-start(bf16[2,128,5120]{2,1,0:T(8,128)(2,1)} %own_ref.2), channel_id=1, source_target_pairs={{0,4},{4,0},{1,5},{5,1},{2,6},{6,2},{3,7},{7,3},{8,12},{12,8},{9,1... | collective-permute-start | bytes 7864328 | tf_op jit(solution)/shard_map/ppermute | solution.py:59
  0.7 38.8 %collective-permute-start.5 = (bf16[2,128,4096]{2,1,0:T(8,128)(2,1)}, bf16[2,128,4096]{2,1,0:T(8,128)(2,1)}, u32[]{:S(2)}, u32[]{:S(2)}) collective-permute-start(bf16[2,128,4096]{2,1,0:T(8,128)(2,1)} %theirs_ref.1), channel_id=1, source_target_pairs={{0,4},{4,0},{1,5},{5,1},{2,6},{6,2},{3,7},{7,3},{8,12},{12,8},{9,1... | collective-permute-start | bytes 6291464 | tf_op jit(solution)/shard_map/ppermute | solution.py:59
  9.2 11.4 %collective-permute-start.14 = (bf16[512,512]{1,0:T(8,128)(2,1)S(1)}, bf16[512,512]{1,0:T(8,128)(2,1)S(1)}, u32[]{:S(2)}, u32[]{:S(2)}) collective-permute-start(bf16[512,512]{1,0:T(8,128)(2,1)S(1)} %constant_dynamic-update-slice_fusion), channel_id=1, source_target_pairs={{0,32},{4,12},{8,40},{12,20},{16,48},{20,28},{24,56},{28,4},{32,64... | collective-permute-start | bytes 1572872 | tf_op jit(solution)/shard_map/ppermute | solution.py:47
  11.3 16.4 %collective-permute-start.15 = (bf16[512,512]{1,0:T(8,128)(2,1)S(1)}, bf16[512,512]{1,0:T(8,128)(2,1)S(1)}, u32[]{:S(2)}, u32[]{:S(2)}) collective-permute-start(bf16[512,512]{1,0:T(8,128)(2,1)S(1)} %constant_dynamic-update-slice_fusion), channel_id=1, source_target_pairs={{0,64},{4,20},{8,72},{12,28},{16,80},{20,4},{24,88},{28,12},{32,96... | collective-permute-start | bytes 1572872 | tf_op jit(solution)/shard_map/ppermute | solution.py:47
  14.9 12.8 %collective-permute-start.16 = (bf16[512,512]{1,0:T(8,128)(2,1)S(1)}, bf16[512,512]{1,0:T(8,128)(2,1)S(1)}, u32[]{:S(2)}, u32[]{:S(2)}) collective-permute-start(bf16[512,512]{1,0:T(8,128)(2,1)S(1)} %constant_dynamic-update-slice_fusion), channel_id=1, source_target_pairs={{0,96},{4,28},{8,104},{12,4},{16,112},{20,12},{24,120},{28,20},{32... | collective-permute-start | bytes 1572872 | tf_op jit(solution)/shard_map/ppermute | solution.py:47
  20.6 16.8 %collective-permute-start.6 = (bf16[2,32]{1,0:T(2,128)(2,1)S(1)}, bf16[2,32]{1,0:T(2,128)(2,1)S(1)}, u32[]{:S(2)}, u32[]{:S(2)}) collective-permute-start(bf16[2,32]{1,0:T(2,128)(2,1)S(1)} %copy-done.1), channel_id=1, source_target_pairs={{0,4},{4,0},{1,5},{5,1},{2,6},{6,2},{3,7},{7,3},{8,12},{12,8},{9,1... | collective-permute-start | bytes 392 | tf_op jit(solution)/shard_map/ppermute | solution.py:59
  27.9 48.8 %collective-permute-start.20 = (bf16[3,512,512]{2,1,0:T(8,128)(2,1)S(1)}, bf16[3,512,512]{2,1,0:T(8,128)(2,1)S(1)}, u32[]{:S(2)}, u32[]{:S(2)}) collective-permute-start(bf16[3,512,512]{2,1,0:T(8,128)(2,1)S(1)} %pad_maximum_fusion.refs_5_), channel_id=1, source_target_pairs={{0,1},{1,2},{2,3},{3,0},{4,5},{5,6},{6,7},{7,4},{8,9},{9,10},{10,1... | collective-permute-start | bytes 4718600 | tf_op jit(solution)/shard_map/ppermute | solution.py:55
  29.5 48.9 %collective-permute-start.21 = (bf16[3,512,512]{2,1,0:T(8,128)(2,1)S(1)}, bf16[3,512,512]{2,1,0:T(8,128)(2,1)S(1)}, u32[]{:S(2)}, u32[]{:S(2)}) collective-permute-start(bf16[3,512,512]{2,1,0:T(8,128)(2,1)S(1)} %pad_maximum_fusion.refs_5_), channel_id=1, source_target_pairs={{0,3},{1,0},{2,1},{3,2},{4,7},{5,4},{6,5},{7,6},{8,11},{9,8},{10,9... | collective-permute-start | bytes 4718600 | tf_op jit(solution)/shard_map/ppermute | solution.py:55
  36.5 32.9 %collective-permute-start.2 = (bf16[1280,512]{1,0:T(8,128)(2,1)S(1)}, bf16[1280,512]{1,0:T(8,128)(2,1)S(1)}, u32[]{:S(2)}, u32[]{:S(2)}) collective-permute-start(bf16[1280,512]{1,0:T(8,128)(2,1)S(1)} %get-tuple-element.33), channel_id=1, source_target_pairs={{0,32},{4,12},{8,40},{12,20},{16,48},{20,28},{24,56},{28,4},{32,64... | collective-permute-start | bytes 3932168 | tf_op jit(solution)/shard_map/ppermute | solution.py:47
  37.4 32.1 %collective-permute-start.3 = (bf16[1280,512]{1,0:T(8,128)(2,1)S(1)}, bf16[1280,512]{1,0:T(8,128)(2,1)S(1)}, u32[]{:S(2)}, u32[]{:S(2)}) collective-permute-start(bf16[1280,512]{1,0:T(8,128)(2,1)S(1)} %get-tuple-element.34), channel_id=1, source_target_pairs={{0,64},{4,20},{8,72},{12,28},{16,80},{20,4},{24,88},{28,12},{32,96... | collective-permute-start | bytes 3932168 | tf_op jit(solution)/shard_map/ppermute | solution.py:47
  39.5 31.1 %collective-permute-start.4 = (bf16[1280,512]{1,0:T(8,128)(2,1)S(1)}, bf16[1280,512]{1,0:T(8,128)(2,1)S(1)}, u32[]{:S(2)}, u32[]{:S(2)}) collective-permute-start(bf16[1280,512]{1,0:T(8,128)(2,1)S(1)} %get-tuple-element.35), channel_id=1, source_target_pairs={{0,96},{4,28},{8,104},{12,4},{16,112},{20,12},{24,120},{28,20},{32... | collective-permute-start | bytes 3932168 | tf_op jit(solution)/shard_map/ppermute | solution.py:47
  69.5 18.1 %collective-permute-start.7 = (bf16[512,512]{1,0:T(8,128)(2,1)S(1)}, bf16[512,512]{1,0:T(8,128)(2,1)S(1)}, u32[]{:S(2)}, u32[]{:S(2)}) collective-permute-start(bf16[512,512]{1,0:T(8,128)(2,1)S(1)} %get-tuple-element.37), channel_id=1, source_target_pairs={{0,32},{4,12},{8,40},{12,20},{16,48},{20,28},{24,56},{28,4},{32,64... | collective-permute-start | bytes 1572872 | tf_op jit(solution)/shard_map/ppermute | solution.py:47
  69.5 21.1 %collective-permute-start.8 = (bf16[512,512]{1,0:T(8,128)(2,1)S(1)}, bf16[512,512]{1,0:T(8,128)(2,1)S(1)}, u32[]{:S(2)}, u32[]{:S(2)}) collective-permute-start(bf16[512,512]{1,0:T(8,128)(2,1)S(1)} %get-tuple-element.37), channel_id=1, source_target_pairs={{0,64},{4,20},{8,72},{12,28},{16,80},{20,4},{24,88},{28,12},{32,96... | collective-permute-start | bytes 1572872 | tf_op jit(solution)/shard_map/ppermute | solution.py:47
  70.6 21.4 %collective-permute-start.9 = (bf16[512,512]{1,0:T(8,128)(2,1)S(1)}, bf16[512,512]{1,0:T(8,128)(2,1)S(1)}, u32[]{:S(2)}, u32[]{:S(2)}) collective-permute-start(bf16[512,512]{1,0:T(8,128)(2,1)S(1)} %get-tuple-element.37), channel_id=1, source_target_pairs={{0,96},{4,28},{8,104},{12,4},{16,112},{20,12},{24,120},{28,20},{32... | collective-permute-start | bytes 1572872 | tf_op jit(solution)/shard_map/ppermute | solution.py:47
  76.6 19.8 %collective-permute-start.17 = (bf16[320,512]{1,0:T(8,128)(2,1)S(1)}, bf16[320,512]{1,0:T(8,128)(2,1)S(1)}, u32[]{:S(2)}, u32[]{:S(2)}) collective-permute-start(bf16[320,512]{1,0:T(8,128)(2,1)S(1)} %get-tuple-element.45), channel_id=1, source_target_pairs={{0,8},{4,36},{8,16},{12,44},{16,24},{20,52},{24,0},{28,60},{32,40}... | collective-permute-start | bytes 983048 | tf_op jit(solution)/shard_map/ppermute | solution.py:51
  84.9 30.2 %collective-permute-start.22 = (bf16[320,1024]{1,0:T(8,128)(2,1)S(1)}, bf16[320,1024]{1,0:T(8,128)(2,1)S(1)}, u32[]{:S(2)}, u32[]{:S(2)}) collective-permute-start(bf16[320,1024]{1,0:T(8,128)(2,1)S(1)} %get-tuple-element.49), channel_id=1, source_target_pairs={{0,8},{4,36},{8,16},{12,44},{16,24},{20,52},{24,0},{28,60},{32,40}... | collective-permute-start | bytes 1966088 | tf_op jit(solution)/shard_map/ppermute | solution.py:51
  87.5 29.6 %collective-permute-start.23 = (bf16[320,1024]{1,0:T(8,128)(2,1)S(1)}, bf16[320,1024]{1,0:T(8,128)(2,1)S(1)}, u32[]{:S(2)}, u32[]{:S(2)}) collective-permute-start(bf16[320,1024]{1,0:T(8,128)(2,1)S(1)} %get-tuple-element.50), channel_id=1, source_target_pairs={{0,16},{4,68},{8,24},{12,76},{16,0},{20,84},{24,8},{28,92},{32,48}... | collective-permute-start | bytes 1966088 | tf_op jit(solution)/shard_map/ppermute | solution.py:51
  90.5 26.6 %collective-permute-start.24 = (bf16[320,1024]{1,0:T(8,128)(2,1)S(1)}, bf16[320,1024]{1,0:T(8,128)(2,1)S(1)}, u32[]{:S(2)}, u32[]{:S(2)}) collective-permute-start(bf16[320,1024]{1,0:T(8,128)(2,1)S(1)} %get-tuple-element.51), channel_id=1, source_target_pairs={{0,24},{4,100},{8,0},{12,108},{16,8},{20,116},{24,16},{28,124},{32... | collective-permute-start | bytes 1966088 | tf_op jit(solution)/shard_map/ppermute | solution.py:51
  92.0 15.3 %collective-permute-start.18 = (bf16[320,512]{1,0:T(8,128)(2,1)S(1)}, bf16[320,512]{1,0:T(8,128)(2,1)S(1)}, u32[]{:S(2)}, u32[]{:S(2)}) collective-permute-start(bf16[320,512]{1,0:T(8,128)(2,1)S(1)} %get-tuple-element.46), channel_id=1, source_target_pairs={{0,16},{4,68},{8,24},{12,76},{16,0},{20,84},{24,8},{28,92},{32,48}... | collective-permute-start | bytes 983048 | tf_op jit(solution)/shard_map/ppermute | solution.py:51
  96.4 16.9 %collective-permute-start.19 = (bf16[320,512]{1,0:T(8,128)(2,1)S(1)}, bf16[320,512]{1,0:T(8,128)(2,1)S(1)}, u32[]{:S(2)}, u32[]{:S(2)}) collective-permute-start(bf16[320,512]{1,0:T(8,128)(2,1)S(1)} %get-tuple-element.47), channel_id=1, source_target_pairs={{0,24},{4,100},{8,0},{12,108},{16,8},{20,116},{24,16},{28,124},{32... | collective-permute-start | bytes 983048 | tf_op jit(solution)/shard_map/ppermute | solution.py:51
  107.3 11.7 %collective-permute-start.10 = (bf16[320,512]{1,0:T(8,128)(2,1)S(1)}, bf16[320,512]{1,0:T(8,128)(2,1)S(1)}, u32[]{:S(2)}, u32[]{:S(2)}) collective-permute-start(bf16[320,512]{1,0:T(8,128)(2,1)S(1)} %get-tuple-element.39), channel_id=1, source_target_pairs={{0,8},{4,36},{8,16},{12,44},{16,24},{20,52},{24,0},{28,60},{32,40}... | collective-permute-start | bytes 983048 | tf_op jit(solution)/shard_map/ppermute | solution.py:51
  119.0 23.1 %collective-permute-start.26 = (bf16[160,1024]{1,0:T(8,128)(2,1)}, bf16[160,1024]{1,0:T(8,128)(2,1)S(1)}, u32[]{:S(2)}, u32[]{:S(2)}) collective-permute-start(bf16[160,1024]{1,0:T(8,128)(2,1)} %get-tuple-element.57), channel_id=1, source_target_pairs={{0,4},{4,0},{1,5},{5,1},{2,6},{6,2},{3,7},{7,3},{8,12},{12,8},{9,1... | collective-permute-start | bytes 983048 | tf_op jit(solution)/shard_map/ppermute | solution.py:59
  126.9 15.2 %collective-permute-start.27 = (bf16[160,512]{1,0:T(8,128)(2,1)}, bf16[160,512]{1,0:T(8,128)(2,1)S(1)}, u32[]{:S(2)}, u32[]{:S(2)}) collective-permute-start(bf16[160,512]{1,0:T(8,128)(2,1)} %get-tuple-element.59), channel_id=1, source_target_pairs={{0,4},{4,0},{1,5},{5,1},{2,6},{6,2},{3,7},{7,3},{8,12},{12,8},{9,1... | collective-permute-start | bytes 491528 | tf_op jit(solution)/shard_map/ppermute | solution.py:59
  126.9 15.2 %collective-permute-start.25 = (bf16[160,512]{1,0:T(8,128)(2,1)}, bf16[160,512]{1,0:T(8,128)(2,1)S(1)}, u32[]{:S(2)}, u32[]{:S(2)}) collective-permute-start(bf16[160,512]{1,0:T(8,128)(2,1)} %get-tuple-element.55), channel_id=1, source_target_pairs={{0,4},{4,0},{1,5},{5,1},{2,6},{6,2},{3,7},{7,3},{8,12},{12,8},{9,1... | collective-permute-start | bytes 491528 | tf_op jit(solution)/shard_map/ppermute | solution.py:59
  (10 other events, 187.6 us)

commit v4 on v3

--- a/solution.py
+++ b/solution.py
@@ -302,7 +302,7 @@
 def adam_kernel(slots, place_ref, shared, *refs):
     count = 2 * len({which for _, which, _ in slots})
     grads, refs = refs[:count], refs[count:]
-    sources, targets = refs[:3], refs[3:7]
+    sources, held, targets = refs[:2], refs[2], refs[3:7]
     grad_in, read, written, weights_out, in_sems, out_sems = refs[7:]
     piece = grad_in.shape[2]
     core, y = place_ref[2], place_ref[3]
@@ -327,9 +327,9 @@
         for copy in fetches[n]:
             copy.wait()
         clipped = factor[0:1, 0:1] * grad_in[n].astype(jnp.float32)
-        new_moment = beta_first * read[n, 0] + (1.0 - beta_first) * clipped
-        new_second = beta_second * read[n, 1] + (1.0 - beta_second) * clipped * clipped
-        new_master = read[n, 2] - learn_rate * new_moment / (jnp.sqrt(new_second) + adam_eps)
+        new_moment = beta_first * held[:, at] + (1.0 - beta_first) * clipped
+        new_second = beta_second * read[n, 0] + (1.0 - beta_second) * clipped * clipped
+        new_master = read[n, 1] - learn_rate * new_moment / (jnp.sqrt(new_second) + adam_eps)
         written[n, 0] = new_moment
         written[n, 1] = new_second
         written[n, 2] = new_master
@@ -348,25 +348,26 @@
     piece = rows // 8
     hbm = pl.BlockSpec(memory_space=pltpu.HBM)
     wide = jax.ShapeDtypeStruct((own, rows), jnp.float32)
-    flat = [a for pair in pairs for a in pair] + [moment, second, master]
+    flat = [a for pair in pairs for a in pair] + [second, master]
     flat = [pltpu.with_memory_space_constraint(a, pltpu.HBM) for a in flat]
+    moment = pltpu.with_memory_space_constraint(moment, pltpu.VMEM)
     return pl.pallas_call(
         functools.partial(adam_kernel, slots),
-        in_specs=[SCALARS, WHOLE] + [hbm] * len(flat),
+        in_specs=[SCALARS, WHOLE] + [hbm] * len(flat) + [WHOLE],
         out_specs=[hbm] * 4,
         scratch_shapes=[
             pltpu.VMEM((8, own, piece), jnp.bfloat16),
-            pltpu.VMEM((8, 3, own, piece), jnp.float32),
+            pltpu.VMEM((8, 2, own, piece), jnp.float32),
             pltpu.VMEM((8, 3, own, piece), jnp.float32),
             pltpu.VMEM((8, own, piece), jnp.bfloat16),
             pltpu.SemaphoreType.DMA((8, 4)),
             pltpu.SemaphoreType.DMA((8, 4)),
         ],
         out_shape=[wide, wide, wide, jax.ShapeDtypeStruct((own, rows), jnp.bfloat16)],
-        compiler_params=pltpu.CompilerParams(vmem_limit_bytes=60 * 2**20),
+        compiler_params=pltpu.CompilerParams(vmem_limit_bytes=24 * 2**20),
         cost_estimate=pl.CostEstimate(flops=10**7, bytes_accessed=17 * 10**6, transcendentals=10**6),
         name="adam",
-    )(place, shared, *flat)
+    )(place, shared, *flat, moment)
 
 
 PRODUCTS = ((0,), (3, 1), (2,))

time: 153 us -> 150 us (0.980)
  Pallas kernels: 35.7 us -> 33.5 us
    pallas_call x1, Pallas kernels: 8.71 us -> 6.4 us  [adam(): pl.pallas_call(functools.partial(adam_kernel, slots), in_specs=[SCALARS,...]
where the time goes in v4:
time: 150 us; the launch traced here: 149 us
  waiting for transfers between devices  59 us (39%)
  starting transfers between devices  40.3 us (27%)
  Pallas kernels  33.5 us (22%)
  blocking collectives  14.3 us (10%)
    ppermute x9, waiting for transfers between devices, gathered(): return lax.ppermute(a, DP, crossed(k, True))  37.7 us
    ppermute x9, starting transfers between devices, scattered(): return lax.ppermute(a, DP, crossed(k, False))  20.3 us
    ppermute x9, waiting for transfers between devices, scattered(): return lax.ppermute(a, DP, crossed(k, False))  15.3 us
    ppermute x9, starting transfers between devices, gathered(): return lax.ppermute(a, DP, crossed(k, True))  14.7 us
    all_to_all x1, blocking collectives, step(): shared = lax.all_to_all(squares, ALL, 0, 0, tiled=True)  14.3 us
    pallas_call x3, Pallas kernels, product(): pl.pallas_call(functools.partial(product_kernel, offsets, forms, width),...  13.7 us
    pallas_call x1, Pallas kernels, adam(): pl.pallas_call(functools.partial(adam_kernel, slots), in_specs=[SCALARS,...  6.4 us
    ppermute x8, waiting for transfers between devices, swapped(): return lax.ppermute(a, 'c', SWAP)  5.92 us
  transfers between devices with their start and end apart: 28, of which 9 were waited for; matrix products, arithmetic and copies ran while one was open for 0% of the time, Pallas kernels for 18%

profile of v4, /device:TPU:0, one launch (start us, length us, event | category | flops | bytes accessed | tf_op | source)
XLA Modules:
  0.0 149.2 jit_solution(12453579627004698055)
XLA Ops:
  3.3 5.9 %collective-permute-done.13 = bf16[256,512]{1,0:T(8,128)(2,1)S(1)} collective-permute-done((bf16[256,512]{1,0:T(8,128)(2,1)S(1)}, bf16[256,512]{1,0:T(8,128)(2,1)S(1)}, u32[]{:S(2)}, u32[]{:S(2)}) %collective-permute-start.13) | collective-permute-done | bytes 262176 | tf_op jit(solution)/shard_map/ppermute | solution.py:59
  9.2 2.1 %collective-permute-start.14 = (bf16[512,512]{1,0:T(8,128)(2,1)S(1)}, bf16[512,512]{1,0:T(8,128)(2,1)S(1)}, u32[]{:S(2)}, u32[]{:S(2)}) collective-permute-start(bf16[512,512]{1,0:T(8,128)(2,1)S(1)} %constant_dynamic-update-slice_fusion), channel_id=1, source_target_pairs={{0,32},{4,12},{8,40},{12,20},{16,48},{20,28},{24,56},{28,4},{32,64... | collective-permute-start | bytes 1572872 | tf_op jit(solution)/shard_map/ppermute | solution.py:47
  11.3 3.6 %collective-permute-start.15 = (bf16[512,512]{1,0:T(8,128)(2,1)S(1)}, bf16[512,512]{1,0:T(8,128)(2,1)S(1)}, u32[]{:S(2)}, u32[]{:S(2)}) collective-permute-start(bf16[512,512]{1,0:T(8,128)(2,1)S(1)} %constant_dynamic-update-slice_fusion), channel_id=1, source_target_pairs={{0,64},{4,20},{8,72},{12,28},{16,80},{20,4},{24,88},{28,12},{32,96... | collective-permute-start | bytes 1572872 | tf_op jit(solution)/shard_map/ppermute | solution.py:47
  16.0 4.6 %collective-permute-done.14 = bf16[512,512]{1,0:T(8,128)(2,1)S(1)} collective-permute-done((bf16[512,512]{1,0:T(8,128)(2,1)S(1)}, bf16[512,512]{1,0:T(8,128)(2,1)S(1)}, u32[]{:S(2)}, u32[]{:S(2)}) %collective-permute-start.14) | collective-permute-done | bytes 524320 | tf_op jit(solution)/shard_map/ppermute | solution.py:47
  20.6 7.1 %collective-permute-done.15 = bf16[512,512]{1,0:T(8,128)(2,1)S(1)} collective-permute-done((bf16[512,512]{1,0:T(8,128)(2,1)S(1)}, bf16[512,512]{1,0:T(8,128)(2,1)S(1)}, u32[]{:S(2)}, u32[]{:S(2)}) %collective-permute-start.15) | collective-permute-done | bytes 524320 | tf_op jit(solution)/shard_map/ppermute | solution.py:47
  29.5 2.4 %collective-permute-start.21 = (bf16[3,512,512]{2,1,0:T(8,128)(2,1)S(1)}, bf16[3,512,512]{2,1,0:T(8,128)(2,1)S(1)}, u32[]{:S(2)}, u32[]{:S(2)}) collective-permute-start(bf16[3,512,512]{2,1,0:T(8,128)(2,1)S(1)} %pad_maximum_fusion.refs_5_), channel_id=1, source_target_pairs={{0,3},{1,0},{2,1},{3,2},{4,7},{5,4},{6,5},{7,6},{8,11},{9,8},{10,9... | collective-permute-start | bytes 4718600 | tf_op jit(solution)/shard_map/ppermute | solution.py:55
  31.9 4.6 %prep.1 = (bf16[1280,512]{1,0:T(8,128)(2,1)S(1)}, bf16[1280,512]{1,0:T(8,128)(2,1)S(1)}, bf16[1280,512]{1,0:T(8,128)(2,1)S(1)}, bf16[1280,512]{1,0:T(8,128)(2,1)S(1)}) custom-call(s32[4]{0:T(128)S(1)} %pad_add_fusion.place_ref, bf16[2,128,5120]{2,1,0:T(8,128)(2,1)} %own_ref.2, bf16[2,128,5120]{2,1,0:T(8,128)(2,1)S(1)} %collective-permute-done.other_ref, ...), custom_call_target="tpu_custom_call" | custom-call | flops 1000000000 | bytes 10485760 | tf_op jit(solution)/shard_map/prep/pallas_call | solution.py:182
  37.4 2.1 %collective-permute-start.3 = (bf16[1280,512]{1,0:T(8,128)(2,1)S(1)}, bf16[1280,512]{1,0:T(8,128)(2,1)S(1)}, u32[]{:S(2)}, u32[]{:S(2)}) collective-permute-start(bf16[1280,512]{1,0:T(8,128)(2,1)S(1)} %get-tuple-element.34), channel_id=1, source_target_pairs={{0,64},{4,20},{8,72},{12,28},{16,80},{20,4},{24,88},{28,12},{32,96... | collective-permute-start | bytes 3932168 | tf_op jit(solution)/shard_map/ppermute | solution.py:47
  41.0 3.5 %acts.1 = (bf16[512,2048]{1,0:T(8,128)(2,1)S(1)}, bf16[512,512]{1,0:T(8,128)(2,1)S(1)}) custom-call(s32[4]{0:T(128)S(1)} %pad_add_fusion.place_ref, bf16[2,128,4096]{2,1,0:T(8,128)(2,1)} %theirs_ref.1, bf16[2,128,4096]{2,1,0:T(8,128)(2,1)} %collective-permute-done.5.other_ref, bf16[2,32]{1,0:T(2,128)(2,1)S(1)} %copy-done.1, ...), custom_call_target="tpu_custom_call" | custom-call | flops 1000000 | bytes 4000000 | tf_op jit(solution)/shard_map/acts/pallas_call | solution.py:131
  44.6 24.9 %collective-permute-done.2.refs_1_ = bf16[1280,512]{1,0:T(8,128)(2,1)S(1)} collective-permute-done((bf16[1280,512]{1,0:T(8,128)(2,1)S(1)}, bf16[1280,512]{1,0:T(8,128)(2,1)S(1)}, u32[]{:S(2)}, u32[]{:S(2)}) %collective-permute-start.2) | collective-permute-done | bytes 1310752 | tf_op jit(solution)/shard_map/ppermute | solution.py:47
  70.6 2.4 %collective-permute-start.9 = (bf16[512,512]{1,0:T(8,128)(2,1)S(1)}, bf16[512,512]{1,0:T(8,128)(2,1)S(1)}, u32[]{:S(2)}, u32[]{:S(2)}) collective-permute-start(bf16[512,512]{1,0:T(8,128)(2,1)S(1)} %get-tuple-element.37), channel_id=1, source_target_pairs={{0,96},{4,28},{8,104},{12,4},{16,112},{20,12},{24,120},{28,20},{32... | collective-permute-start | bytes 1572872 | tf_op jit(solution)/shard_map/ppermute | solution.py:47
  73.0 3.6 %product.4 = (bf16[320,512]{1,0:T(8,128)(2,1)S(1)}, bf16[320,512]{1,0:T(8,128)(2,1)S(1)}, bf16[320,512]{1,0:T(8,128)(2,1)S(1)}, bf16[320,512]{1,0:T(8,128)(2,1)S(1)}) custom-call(s32[4]{0:T(128)S(1)} %pad_add_fusion.place_ref, bf16[1280,512]{1,0:T(8,128)(2,1)S(1)} %get-tuple-element.32.refs_0_, bf16[1280,512]{1,0:T(8,128)(2,1)S(1)} %collective-permute-done.2.refs_1_, ...), custom_call_target="tpu_custom_call" | custom-call | flops 2684354560 | bytes 7340032 | tf_op jit(solution)/shard_map/product/pallas_call | solution.py:234
  78.4 6.5 %product.5 = (bf16[320,1024]{1,0:T(8,128)(2,1)S(1)}, bf16[320,1024]{1,0:T(8,128)(2,1)S(1)}, bf16[320,1024]{1,0:T(8,128)(2,1)S(1)}, bf16[320,1024]{1,0:T(8,128)(2,1)S(1)}) custom-call(s32[4]{0:T(128)S(1)} %pad_add_fusion.place_ref, bf16[1280,512]{1,0:T(8,128)(2,1)S(1)} %get-tuple-element.32.refs_0_, bf16[1280,512]{1,0:T(8,128)(2,1)S(1)} %collective-permute-done.2.refs_1_, ...), custom_call_target="tpu_custom_call" | custom-call | flops 5368709120 | bytes 7340032 | tf_op jit(solution)/shard_map/product/pallas_call | solution.py:234
  87.5 3.0 %collective-permute-start.23 = (bf16[320,1024]{1,0:T(8,128)(2,1)S(1)}, bf16[320,1024]{1,0:T(8,128)(2,1)S(1)}, u32[]{:S(2)}, u32[]{:S(2)}) collective-permute-start(bf16[320,1024]{1,0:T(8,128)(2,1)S(1)} %get-tuple-element.50), channel_id=1, source_target_pairs={{0,16},{4,68},{8,24},{12,76},{16,0},{20,84},{24,8},{28,92},{32,48}... | collective-permute-start | bytes 1966088 | tf_op jit(solution)/shard_map/ppermute | solution.py:51
  92.0 4.4 %collective-permute-start.18 = (bf16[320,512]{1,0:T(8,128)(2,1)S(1)}, bf16[320,512]{1,0:T(8,128)(2,1)S(1)}, u32[]{:S(2)}, u32[]{:S(2)}) collective-permute-start(bf16[320,512]{1,0:T(8,128)(2,1)S(1)} %get-tuple-element.46), channel_id=1, source_target_pairs={{0,16},{4,68},{8,24},{12,76},{16,0},{20,84},{24,8},{28,92},{32,48}... | collective-permute-start | bytes 983048 | tf_op jit(solution)/shard_map/ppermute | solution.py:51
  97.0 3.6 %product.3 = (bf16[320,512]{1,0:T(8,128)(2,1)S(1)}, bf16[320,512]{1,0:T(8,128)(2,1)S(1)}, bf16[320,512]{1,0:T(8,128)(2,1)S(1)}, bf16[320,512]{1,0:T(8,128)(2,1)S(1)}) custom-call(s32[4]{0:T(128)S(1)} %pad_add_fusion.place_ref, bf16[1280,512]{1,0:T(8,128)(2,1)S(1)} %get-tuple-element.32.refs_0_, bf16[1280,512]{1,0:T(8,128)(2,1)S(1)} %collective-permute-done.2.refs_1_, ...), custom_call_target="tpu_custom_call" | custom-call | flops 2684354560 | bytes 7340032 | tf_op jit(solution)/shard_map/product/pallas_call | solution.py:234
  100.6 6.7 %collective-permute-done.18.refs_2_ = bf16[320,512]{1,0:T(8,128)(2,1)S(1)} collective-permute-done((bf16[320,512]{1,0:T(8,128)(2,1)S(1)}, bf16[320,512]{1,0:T(8,128)(2,1)S(1)}, u32[]{:S(2)}, u32[]{:S(2)}) %collective-permute-start.18) | collective-permute-done | bytes 327712 | tf_op jit(solution)/shard_map/ppermute | solution.py:51
  107.3 3.8 %collective-permute-start.10 = (bf16[320,512]{1,0:T(8,128)(2,1)S(1)}, bf16[320,512]{1,0:T(8,128)(2,1)S(1)}, u32[]{:S(2)}, u32[]{:S(2)}) collective-permute-start(bf16[320,512]{1,0:T(8,128)(2,1)S(1)} %get-tuple-element.39), channel_id=1, source_target_pairs={{0,8},{4,36},{8,16},{12,44},{16,24},{20,52},{24,0},{28,60},{32,40}... | collective-permute-start | bytes 983048 | tf_op jit(solution)/shard_map/ppermute | solution.py:51
  111.1 2.3 %collective-permute-done.19.refs_3_ = bf16[320,512]{1,0:T(8,128)(2,1)S(1)} collective-permute-done((bf16[320,512]{1,0:T(8,128)(2,1)S(1)}, bf16[320,512]{1,0:T(8,128)(2,1)S(1)}, u32[]{:S(2)}, u32[]{:S(2)}) %collective-permute-start.19) | collective-permute-done | bytes 327712 | tf_op jit(solution)/shard_map/ppermute | solution.py:51
  115.1 2.0 %collective-permute-start.12 = (bf16[320,512]{1,0:T(8,128)(2,1)S(1)}, bf16[320,512]{1,0:T(8,128)(2,1)S(1)}, u32[]{:S(2)}, u32[]{:S(2)}) collective-permute-start(bf16[320,512]{1,0:T(8,128)(2,1)S(1)} %get-tuple-element.41), channel_id=1, source_target_pairs={{0,24},{4,100},{8,0},{12,108},{16,8},{20,116},{24,16},{28,124},{32... | collective-permute-start | bytes 983048 | tf_op jit(solution)/shard_map/ppermute | solution.py:51
  119.0 3.6 %collective-permute-done.11.refs_2_ = bf16[320,512]{1,0:T(8,128)(2,1)S(1)} collective-permute-done((bf16[320,512]{1,0:T(8,128)(2,1)S(1)}, bf16[320,512]{1,0:T(8,128)(2,1)S(1)}, u32[]{:S(2)}, u32[]{:S(2)}) %collective-permute-start.11) | collective-permute-done | bytes 327712 | tf_op jit(solution)/shard_map/ppermute | solution.py:51
  122.6 2.8 %collective-permute-done.12.refs_3_ = bf16[320,512]{1,0:T(8,128)(2,1)S(1)} collective-permute-done((bf16[320,512]{1,0:T(8,128)(2,1)S(1)}, bf16[320,512]{1,0:T(8,128)(2,1)S(1)}, u32[]{:S(2)}, u32[]{:S(2)}) %collective-permute-start.12) | collective-permute-done | bytes 327712 | tf_op jit(solution)/shard_map/ppermute | solution.py:51
  127.4 14.3 %all_to_all.5.shared = f32[128,1,128]{2,1,0:T(1,128)S(1)} all-to-all(f32[128,1,128]{2,1,0:T(1,128)S(1)} %get-tuple-element.53), channel_id=1, replica_groups=mesh['z'=4,'x'=4,'c'=2,'y'=4] {'z','x','c','y'}, dimensions={0} | all-to-all | bytes 131072 | tf_op jit(solution)/shard_map/all_to_all | solution.py:406
  142.6 6.4 %adam.1 = (f32[160,4096]{1,0:T(8,128)}, f32[160,4096]{1,0:T(8,128)}, f32[160,4096]{1,0:T(8,128)}, bf16[160,4096]{1,0:T(8,128)(2,1)}) custom-call(s32[4]{0:T(128)S(1)} %pad_add_fusion.place_ref, f32[128,1,128]{2,1,0:T(1,128)S(1)} %all_to_all.5.shared, bf16[160,512]{1,0:T(8,128)(2,1)} %get-tuple-element.54.refs_0_, bf16[160,512]{1,0:T(8,128)(2,1)} %copy-done.4, ...), custom_call_target="tpu_custom_call" | custom-call | flops 10000000 | bytes 17000000 | tf_op jit(solution)/shard_map/adam/pallas_call | solution.py:354
  (59 shorter events, 22.1 us)
Async XLA Ops:
  0.6 31.3 %collective-permute-start = (bf16[2,128,5120]{2,1,0:T(8,128)(2,1)}, bf16[2,128,5120]{2,1,0:T(8,128)(2,1)S(1)}, u32[]{:S(2)}, u32[]{:S(2)}) collective-permute-start(bf16[2,128,5120]{2,1,0:T(8,128)(2,1)} %own_ref.2), channel_id=1, source_target_pairs={{0,4},{4,0},{1,5},{5,1},{2,6},{6,2},{3,7},{7,3},{8,12},{12,8},{9,1... | collective-permute-start | bytes 7864328 | tf_op jit(solution)/shard_map/ppermute | solution.py:59
  0.7 38.8 %collective-permute-start.5 = (bf16[2,128,4096]{2,1,0:T(8,128)(2,1)}, bf16[2,128,4096]{2,1,0:T(8,128)(2,1)}, u32[]{:S(2)}, u32[]{:S(2)}) collective-permute-start(bf16[2,128,4096]{2,1,0:T(8,128)(2,1)} %theirs_ref.1), channel_id=1, source_target_pairs={{0,4},{4,0},{1,5},{5,1},{2,6},{6,2},{3,7},{7,3},{8,12},{12,8},{9,1... | collective-permute-start | bytes 6291464 | tf_op jit(solution)/shard_map/ppermute | solution.py:59
  9.2 11.4 %collective-permute-start.14 = (bf16[512,512]{1,0:T(8,128)(2,1)S(1)}, bf16[512,512]{1,0:T(8,128)(2,1)S(1)}, u32[]{:S(2)}, u32[]{:S(2)}) collective-permute-start(bf16[512,512]{1,0:T(8,128)(2,1)S(1)} %constant_dynamic-update-slice_fusion), channel_id=1, source_target_pairs={{0,32},{4,12},{8,40},{12,20},{16,48},{20,28},{24,56},{28,4},{32,64... | collective-permute-start | bytes 1572872 | tf_op jit(solution)/shard_map/ppermute | solution.py:47
  11.3 16.4 %collective-permute-start.15 = (bf16[512,512]{1,0:T(8,128)(2,1)S(1)}, bf16[512,512]{1,0:T(8,128)(2,1)S(1)}, u32[]{:S(2)}, u32[]{:S(2)}) collective-permute-start(bf16[512,512]{1,0:T(8,128)(2,1)S(1)} %constant_dynamic-update-slice_fusion), channel_id=1, source_target_pairs={{0,64},{4,20},{8,72},{12,28},{16,80},{20,4},{24,88},{28,12},{32,96... | collective-permute-start | bytes 1572872 | tf_op jit(solution)/shard_map/ppermute | solution.py:47
  14.9 12.8 %collective-permute-start.16 = (bf16[512,512]{1,0:T(8,128)(2,1)S(1)}, bf16[512,512]{1,0:T(8,128)(2,1)S(1)}, u32[]{:S(2)}, u32[]{:S(2)}) collective-permute-start(bf16[512,512]{1,0:T(8,128)(2,1)S(1)} %constant_dynamic-update-slice_fusion), channel_id=1, source_target_pairs={{0,96},{4,28},{8,104},{12,4},{16,112},{20,12},{24,120},{28,20},{32... | collective-permute-start | bytes 1572872 | tf_op jit(solution)/shard_map/ppermute | solution.py:47
  20.6 16.8 %collective-permute-start.6 = (bf16[2,32]{1,0:T(2,128)(2,1)S(1)}, bf16[2,32]{1,0:T(2,128)(2,1)S(1)}, u32[]{:S(2)}, u32[]{:S(2)}) collective-permute-start(bf16[2,32]{1,0:T(2,128)(2,1)S(1)} %copy-done.1), channel_id=1, source_target_pairs={{0,4},{4,0},{1,5},{5,1},{2,6},{6,2},{3,7},{7,3},{8,12},{12,8},{9,1... | collective-permute-start | bytes 392 | tf_op jit(solution)/shard_map/ppermute | solution.py:59
  27.9 48.8 %collective-permute-start.20 = (bf16[3,512,512]{2,1,0:T(8,128)(2,1)S(1)}, bf16[3,512,512]{2,1,0:T(8,128)(2,1)S(1)}, u32[]{:S(2)}, u32[]{:S(2)}) collective-permute-start(bf16[3,512,512]{2,1,0:T(8,128)(2,1)S(1)} %pad_maximum_fusion.refs_5_), channel_id=1, source_target_pairs={{0,1},{1,2},{2,3},{3,0},{4,5},{5,6},{6,7},{7,4},{8,9},{9,10},{10,1... | collective-permute-start | bytes 4718600 | tf_op jit(solution)/shard_map/ppermute | solution.py:55
  29.5 48.9 %collective-permute-start.21 = (bf16[3,512,512]{2,1,0:T(8,128)(2,1)S(1)}, bf16[3,512,512]{2,1,0:T(8,128)(2,1)S(1)}, u32[]{:S(2)}, u32[]{:S(2)}) collective-permute-start(bf16[3,512,512]{2,1,0:T(8,128)(2,1)S(1)} %pad_maximum_fusion.refs_5_), channel_id=1, source_target_pairs={{0,3},{1,0},{2,1},{3,2},{4,7},{5,4},{6,5},{7,6},{8,11},{9,8},{10,9... | collective-permute-start | bytes 4718600 | tf_op jit(solution)/shard_map/ppermute | solution.py:55
  36.5 32.9 %collective-permute-start.2 = (bf16[1280,512]{1,0:T(8,128)(2,1)S(1)}, bf16[1280,512]{1,0:T(8,128)(2,1)S(1)}, u32[]{:S(2)}, u32[]{:S(2)}) collective-permute-start(bf16[1280,512]{1,0:T(8,128)(2,1)S(1)} %get-tuple-element.33), channel_id=1, source_target_pairs={{0,32},{4,12},{8,40},{12,20},{16,48},{20,28},{24,56},{28,4},{32,64... | collective-permute-start | bytes 3932168 | tf_op jit(solution)/shard_map/ppermute | solution.py:47
  37.4 32.1 %collective-permute-start.3 = (bf16[1280,512]{1,0:T(8,128)(2,1)S(1)}, bf16[1280,512]{1,0:T(8,128)(2,1)S(1)}, u32[]{:S(2)}, u32[]{:S(2)}) collective-permute-start(bf16[1280,512]{1,0:T(8,128)(2,1)S(1)} %get-tuple-element.34), channel_id=1, source_target_pairs={{0,64},{4,20},{8,72},{12,28},{16,80},{20,4},{24,88},{28,12},{32,96... | collective-permute-start | bytes 3932168 | tf_op jit(solution)/shard_map/ppermute | solution.py:47
  39.5 31.1 %collective-permute-start.4 = (bf16[1280,512]{1,0:T(8,128)(2,1)S(1)}, bf16[1280,512]{1,0:T(8,128)(2,1)S(1)}, u32[]{:S(2)}, u32[]{:S(2)}) collective-permute-start(bf16[1280,512]{1,0:T(8,128)(2,1)S(1)} %get-tuple-element.35), channel_id=1, source_target_pairs={{0,96},{4,28},{8,104},{12,4},{16,112},{20,12},{24,120},{28,20},{32... | collective-permute-start | bytes 3932168 | tf_op jit(solution)/shard_map/ppermute | solution.py:47
  69.5 18.1 %collective-permute-start.7 = (bf16[512,512]{1,0:T(8,128)(2,1)S(1)}, bf16[512,512]{1,0:T(8,128)(2,1)S(1)}, u32[]{:S(2)}, u32[]{:S(2)}) collective-permute-start(bf16[512,512]{1,0:T(8,128)(2,1)S(1)} %get-tuple-element.37), channel_id=1, source_target_pairs={{0,32},{4,12},{8,40},{12,20},{16,48},{20,28},{24,56},{28,4},{32,64... | collective-permute-start | bytes 1572872 | tf_op jit(solution)/shard_map/ppermute | solution.py:47
  69.5 21.1 %collective-permute-start.8 = (bf16[512,512]{1,0:T(8,128)(2,1)S(1)}, bf16[512,512]{1,0:T(8,128)(2,1)S(1)}, u32[]{:S(2)}, u32[]{:S(2)}) collective-permute-start(bf16[512,512]{1,0:T(8,128)(2,1)S(1)} %get-tuple-element.37), channel_id=1, source_target_pairs={{0,64},{4,20},{8,72},{12,28},{16,80},{20,4},{24,88},{28,12},{32,96... | collective-permute-start | bytes 1572872 | tf_op jit(solution)/shard_map/ppermute | solution.py:47
  70.6 21.4 %collective-permute-start.9 = (bf16[512,512]{1,0:T(8,128)(2,1)S(1)}, bf16[512,512]{1,0:T(8,128)(2,1)S(1)}, u32[]{:S(2)}, u32[]{:S(2)}) collective-permute-start(bf16[512,512]{1,0:T(8,128)(2,1)S(1)} %get-tuple-element.37), channel_id=1, source_target_pairs={{0,96},{4,28},{8,104},{12,4},{16,112},{20,12},{24,120},{28,20},{32... | collective-permute-start | bytes 1572872 | tf_op jit(solution)/shard_map/ppermute | solution.py:47
  76.6 19.8 %collective-permute-start.17 = (bf16[320,512]{1,0:T(8,128)(2,1)S(1)}, bf16[320,512]{1,0:T(8,128)(2,1)S(1)}, u32[]{:S(2)}, u32[]{:S(2)}) collective-permute-start(bf16[320,512]{1,0:T(8,128)(2,1)S(1)} %get-tuple-element.45), channel_id=1, source_target_pairs={{0,8},{4,36},{8,16},{12,44},{16,24},{20,52},{24,0},{28,60},{32,40}... | collective-permute-start | bytes 983048 | tf_op jit(solution)/shard_map/ppermute | solution.py:51
  84.9 30.2 %collective-permute-start.22 = (bf16[320,1024]{1,0:T(8,128)(2,1)S(1)}, bf16[320,1024]{1,0:T(8,128)(2,1)S(1)}, u32[]{:S(2)}, u32[]{:S(2)}) collective-permute-start(bf16[320,1024]{1,0:T(8,128)(2,1)S(1)} %get-tuple-element.49), channel_id=1, source_target_pairs={{0,8},{4,36},{8,16},{12,44},{16,24},{20,52},{24,0},{28,60},{32,40}... | collective-permute-start | bytes 1966088 | tf_op jit(solution)/shard_map/ppermute | solution.py:51
  87.5 29.6 %collective-permute-start.23 = (bf16[320,1024]{1,0:T(8,128)(2,1)S(1)}, bf16[320,1024]{1,0:T(8,128)(2,1)S(1)}, u32[]{:S(2)}, u32[]{:S(2)}) collective-permute-start(bf16[320,1024]{1,0:T(8,128)(2,1)S(1)} %get-tuple-element.50), channel_id=1, source_target_pairs={{0,16},{4,68},{8,24},{12,76},{16,0},{20,84},{24,8},{28,92},{32,48}... | collective-permute-start | bytes 1966088 | tf_op jit(solution)/shard_map/ppermute | solution.py:51
  90.5 26.6 %collective-permute-start.24 = (bf16[320,1024]{1,0:T(8,128)(2,1)S(1)}, bf16[320,1024]{1,0:T(8,128)(2,1)S(1)}, u32[]{:S(2)}, u32[]{:S(2)}) collective-permute-start(bf16[320,1024]{1,0:T(8,128)(2,1)S(1)} %get-tuple-element.51), channel_id=1, source_target_pairs={{0,24},{4,100},{8,0},{12,108},{16,8},{20,116},{24,16},{28,124},{32... | collective-permute-start | bytes 1966088 | tf_op jit(solution)/shard_map/ppermute | solution.py:51
  92.0 15.3 %collective-permute-start.18 = (bf16[320,512]{1,0:T(8,128)(2,1)S(1)}, bf16[320,512]{1,0:T(8,128)(2,1)S(1)}, u32[]{:S(2)}, u32[]{:S(2)}) collective-permute-start(bf16[320,512]{1,0:T(8,128)(2,1)S(1)} %get-tuple-element.46), channel_id=1, source_target_pairs={{0,16},{4,68},{8,24},{12,76},{16,0},{20,84},{24,8},{28,92},{32,48}... | collective-permute-start | bytes 983048 | tf_op jit(solution)/shard_map/ppermute | solution.py:51
  96.4 17.0 %collective-permute-start.19 = (bf16[320,512]{1,0:T(8,128)(2,1)S(1)}, bf16[320,512]{1,0:T(8,128)(2,1)S(1)}, u32[]{:S(2)}, u32[]{:S(2)}) collective-permute-start(bf16[320,512]{1,0:T(8,128)(2,1)S(1)} %get-tuple-element.47), channel_id=1, source_target_pairs={{0,24},{4,100},{8,0},{12,108},{16,8},{20,116},{24,16},{28,124},{32... | collective-permute-start | bytes 983048 | tf_op jit(solution)/shard_map/ppermute | solution.py:51
  107.3 11.7 %collective-permute-start.10 = (bf16[320,512]{1,0:T(8,128)(2,1)S(1)}, bf16[320,512]{1,0:T(8,128)(2,1)S(1)}, u32[]{:S(2)}, u32[]{:S(2)}) collective-permute-start(bf16[320,512]{1,0:T(8,128)(2,1)S(1)} %get-tuple-element.39), channel_id=1, source_target_pairs={{0,8},{4,36},{8,16},{12,44},{16,24},{20,52},{24,0},{28,60},{32,40}... | collective-permute-start | bytes 983048 | tf_op jit(solution)/shard_map/ppermute | solution.py:51
  119.0 22.7 %collective-permute-start.26 = (bf16[160,1024]{1,0:T(8,128)(2,1)}, bf16[160,1024]{1,0:T(8,128)(2,1)S(1)}, u32[]{:S(2)}, u32[]{:S(2)}) collective-permute-start(bf16[160,1024]{1,0:T(8,128)(2,1)} %get-tuple-element.57), channel_id=1, source_target_pairs={{0,4},{4,0},{1,5},{5,1},{2,6},{6,2},{3,7},{7,3},{8,12},{12,8},{9,1... | collective-permute-start | bytes 983048 | tf_op jit(solution)/shard_map/ppermute | solution.py:59
  126.9 14.8 %collective-permute-start.27 = (bf16[160,512]{1,0:T(8,128)(2,1)}, bf16[160,512]{1,0:T(8,128)(2,1)S(1)}, u32[]{:S(2)}, u32[]{:S(2)}) collective-permute-start(bf16[160,512]{1,0:T(8,128)(2,1)} %get-tuple-element.59), channel_id=1, source_target_pairs={{0,4},{4,0},{1,5},{5,1},{2,6},{6,2},{3,7},{7,3},{8,12},{12,8},{9,1... | collective-permute-start | bytes 491528 | tf_op jit(solution)/shard_map/ppermute | solution.py:59
  126.9 14.8 %collective-permute-start.25 = (bf16[160,512]{1,0:T(8,128)(2,1)}, bf16[160,512]{1,0:T(8,128)(2,1)S(1)}, u32[]{:S(2)}, u32[]{:S(2)}) collective-permute-start(bf16[160,512]{1,0:T(8,128)(2,1)} %get-tuple-element.55), channel_id=1, source_target_pairs={{0,4},{4,0},{1,5},{5,1},{2,6},{6,2},{3,7},{7,3},{8,12},{12,8},{9,1... | collective-permute-start | bytes 491528 | tf_op jit(solution)/shard_map/ppermute | solution.py:59
  (10 other events, 89.0 us)

commit v5 on v4

--- a/solution.py
+++ b/solution.py
@@ -312,8 +312,10 @@
         half = core if side == 0 else 1 - core
         at = pl.ds(pl.multiple_of((2 * lax.rem(y + offset, 4) + half) * piece, piece), piece)
         ats.append(at)
-        from_grad = grads[2 * which + side].at[:, lead * piece : (lead + 1) * piece]
-        copies = [pltpu.make_async_copy(from_grad, grad_in.at[n], in_sems.at[n, 3])]
+        copies = []
+        if side == 0:
+            from_grad = grads[2 * which].at[:, lead * piece : (lead + 1) * piece]
+            copies.append(pltpu.make_async_copy(from_grad, grad_in.at[n // 2], in_sems.at[n, 3]))
         for i, source in enumerate(sources):
             copies.append(pltpu.make_async_copy(source.at[:, at], read.at[n, i], in_sems.at[n, i]))
         for copy in copies:
@@ -326,7 +328,9 @@
     for n, at in enumerate(ats):
         for copy in fetches[n]:
             copy.wait()
-        clipped = factor[0:1, 0:1] * grad_in[n].astype(jnp.float32)
+        _, which, lead, side = blocks[n]
+        grad = grad_in[n // 2] if side == 0 else grads[2 * which + 1][:, lead * piece : (lead + 1) * piece]
+        clipped = factor[0:1, 0:1] * grad.astype(jnp.float32)
         new_moment = beta_first * held[:, at] + (1.0 - beta_first) * clipped
         new_second = beta_second * read[n, 0] + (1.0 - beta_second) * clipped * clipped
         new_master = read[n, 1] - learn_rate * new_moment / (jnp.sqrt(new_second) + adam_eps)
@@ -348,15 +352,15 @@
     piece = rows // 8
     hbm = pl.BlockSpec(memory_space=pltpu.HBM)
     wide = jax.ShapeDtypeStruct((own, rows), jnp.float32)
-    flat = [a for pair in pairs for a in pair] + [second, master]
-    flat = [pltpu.with_memory_space_constraint(a, pltpu.HBM) for a in flat]
-    moment = pltpu.with_memory_space_constraint(moment, pltpu.VMEM)
+    flat = [a for pair in pairs for a in pair] + [second, master, moment]
+    spaces = [pltpu.HBM, pltpu.VMEM] * len(pairs) + [pltpu.HBM, pltpu.HBM, pltpu.VMEM]
+    flat = [pltpu.with_memory_space_constraint(a, space) for a, space in zip(flat, spaces)]
     return pl.pallas_call(
         functools.partial(adam_kernel, slots),
-        in_specs=[SCALARS, WHOLE] + [hbm] * len(flat) + [WHOLE],
+        in_specs=[SCALARS, WHOLE] + [pl.BlockSpec(memory_space=space) for space in spaces],
         out_specs=[hbm] * 4,
         scratch_shapes=[
-            pltpu.VMEM((8, own, piece), jnp.bfloat16),
+            pltpu.VMEM((4, own, piece), jnp.bfloat16),
             pltpu.VMEM((8, 2, own, piece), jnp.float32),
             pltpu.VMEM((8, 3, own, piece), jnp.float32),
             pltpu.VMEM((8, own, piece), jnp.bfloat16),
@@ -367,7 +371,7 @@
         compiler_params=pltpu.CompilerParams(vmem_limit_bytes=24 * 2**20),
         cost_estimate=pl.CostEstimate(flops=10**7, bytes_accessed=17 * 10**6, transcendentals=10**6),
         name="adam",
-    )(place, shared, *flat, moment)
+    )(place, shared, *flat)
 
 
 PRODUCTS = ((0,), (3, 1), (2,))

time: 150 us -> 149 us (level)
  no operation moved by 1% of the time
where the time goes in v5:
time: 149 us; the launch traced here: 148 us
  waiting for transfers between devices  59 us (40%)
  starting transfers between devices  40.3 us (27%)
  Pallas kernels  33.2 us (22%)
  blocking collectives  14.3 us (10%)
    ppermute x9, waiting for transfers between devices, gathered(): return lax.ppermute(a, DP, crossed(k, True))  37.7 us
    ppermute x9, starting transfers between devices, scattered(): return lax.ppermute(a, DP, crossed(k, False))  20.3 us
    ppermute x9, waiting for transfers between devices, scattered(): return lax.ppermute(a, DP, crossed(k, False))  15.3 us
    ppermute x9, starting transfers between devices, gathered(): return lax.ppermute(a, DP, crossed(k, True))  14.7 us
    all_to_all x1, blocking collectives, step(): shared = lax.all_to_all(squares, ALL, 0, 0, tiled=True)  14.3 us
    pallas_call x3, Pallas kernels, product(): pl.pallas_call(functools.partial(product_kernel, offsets, forms, width),...  13.7 us
    pallas_call x1, Pallas kernels, adam(): pl.pallas_call(functools.partial(adam_kernel, slots), in_specs=[SCALARS,...  6.12 us
    ppermute x8, waiting for transfers between devices, swapped(): return lax.ppermute(a, 'c', SWAP)  5.92 us
  transfers between devices with their start and end apart: 28, of which 9 were waited for; matrix products, arithmetic and copies ran while one was open for 0% of the time, Pallas kernels for 18%

profile of v5, /device:TPU:0, one launch (start us, length us, event | category | flops | bytes accessed | tf_op | source)
XLA Modules:
  0.0 148.0 jit_solution(11225162102310065426)
XLA Ops:
  3.3 5.9 %collective-permute-done.13 = bf16[256,512]{1,0:T(8,128)(2,1)S(1)} collective-permute-done((bf16[256,512]{1,0:T(8,128)(2,1)S(1)}, bf16[256,512]{1,0:T(8,128)(2,1)S(1)}, u32[]{:S(2)}, u32[]{:S(2)}) %collective-permute-start.13) | collective-permute-done | bytes 262176 | tf_op jit(solution)/shard_map/ppermute | solution.py:59
  9.2 2.1 %collective-permute-start.14 = (bf16[512,512]{1,0:T(8,128)(2,1)S(1)}, bf16[512,512]{1,0:T(8,128)(2,1)S(1)}, u32[]{:S(2)}, u32[]{:S(2)}) collective-permute-start(bf16[512,512]{1,0:T(8,128)(2,1)S(1)} %constant_dynamic-update-slice_fusion), channel_id=1, source_target_pairs={{0,32},{4,12},{8,40},{12,20},{16,48},{20,28},{24,56},{28,4},{32,64... | collective-permute-start | bytes 1572872 | tf_op jit(solution)/shard_map/ppermute | solution.py:47
  11.3 3.6 %collective-permute-start.15 = (bf16[512,512]{1,0:T(8,128)(2,1)S(1)}, bf16[512,512]{1,0:T(8,128)(2,1)S(1)}, u32[]{:S(2)}, u32[]{:S(2)}) collective-permute-start(bf16[512,512]{1,0:T(8,128)(2,1)S(1)} %constant_dynamic-update-slice_fusion), channel_id=1, source_target_pairs={{0,64},{4,20},{8,72},{12,28},{16,80},{20,4},{24,88},{28,12},{32,96... | collective-permute-start | bytes 1572872 | tf_op jit(solution)/shard_map/ppermute | solution.py:47
  16.0 4.6 %collective-permute-done.14 = bf16[512,512]{1,0:T(8,128)(2,1)S(1)} collective-permute-done((bf16[512,512]{1,0:T(8,128)(2,1)S(1)}, bf16[512,512]{1,0:T(8,128)(2,1)S(1)}, u32[]{:S(2)}, u32[]{:S(2)}) %collective-permute-start.14) | collective-permute-done | bytes 524320 | tf_op jit(solution)/shard_map/ppermute | solution.py:47
  20.6 7.1 %collective-permute-done.15 = bf16[512,512]{1,0:T(8,128)(2,1)S(1)} collective-permute-done((bf16[512,512]{1,0:T(8,128)(2,1)S(1)}, bf16[512,512]{1,0:T(8,128)(2,1)S(1)}, u32[]{:S(2)}, u32[]{:S(2)}) %collective-permute-start.15) | collective-permute-done | bytes 524320 | tf_op jit(solution)/shard_map/ppermute | solution.py:47
  29.5 2.4 %collective-permute-start.21 = (bf16[3,512,512]{2,1,0:T(8,128)(2,1)S(1)}, bf16[3,512,512]{2,1,0:T(8,128)(2,1)S(1)}, u32[]{:S(2)}, u32[]{:S(2)}) collective-permute-start(bf16[3,512,512]{2,1,0:T(8,128)(2,1)S(1)} %pad_maximum_fusion.refs_5_), channel_id=1, source_target_pairs={{0,3},{1,0},{2,1},{3,2},{4,7},{5,4},{6,5},{7,6},{8,11},{9,8},{10,9... | collective-permute-start | bytes 4718600 | tf_op jit(solution)/shard_map/ppermute | solution.py:55
  31.9 4.6 %prep.1 = (bf16[1280,512]{1,0:T(8,128)(2,1)S(1)}, bf16[1280,512]{1,0:T(8,128)(2,1)S(1)}, bf16[1280,512]{1,0:T(8,128)(2,1)S(1)}, bf16[1280,512]{1,0:T(8,128)(2,1)S(1)}) custom-call(s32[4]{0:T(128)S(1)} %pad_add_fusion.place_ref, bf16[2,128,5120]{2,1,0:T(8,128)(2,1)} %own_ref.2, bf16[2,128,5120]{2,1,0:T(8,128)(2,1)S(1)} %collective-permute-done.other_ref, ...), custom_call_target="tpu_custom_call" | custom-call | flops 1000000000 | bytes 10485760 | tf_op jit(solution)/shard_map/prep/pallas_call | solution.py:182
  37.4 2.1 %collective-permute-start.3 = (bf16[1280,512]{1,0:T(8,128)(2,1)S(1)}, bf16[1280,512]{1,0:T(8,128)(2,1)S(1)}, u32[]{:S(2)}, u32[]{:S(2)}) collective-permute-start(bf16[1280,512]{1,0:T(8,128)(2,1)S(1)} %get-tuple-element.34), channel_id=1, source_target_pairs={{0,64},{4,20},{8,72},{12,28},{16,80},{20,4},{24,88},{28,12},{32,96... | collective-permute-start | bytes 3932168 | tf_op jit(solution)/shard_map/ppermute | solution.py:47
  41.0 3.5 %acts.1 = (bf16[512,2048]{1,0:T(8,128)(2,1)S(1)}, bf16[512,512]{1,0:T(8,128)(2,1)S(1)}) custom-call(s32[4]{0:T(128)S(1)} %pad_add_fusion.place_ref, bf16[2,128,4096]{2,1,0:T(8,128)(2,1)} %theirs_ref.1, bf16[2,128,4096]{2,1,0:T(8,128)(2,1)} %collective-permute-done.5.other_ref, bf16[2,32]{1,0:T(2,128)(2,1)S(1)} %copy-done.1, ...), custom_call_target="tpu_custom_call" | custom-call | flops 1000000 | bytes 4000000 | tf_op jit(solution)/shard_map/acts/pallas_call | solution.py:131
  44.6 24.9 %collective-permute-done.2.refs_1_ = bf16[1280,512]{1,0:T(8,128)(2,1)S(1)} collective-permute-done((bf16[1280,512]{1,0:T(8,128)(2,1)S(1)}, bf16[1280,512]{1,0:T(8,128)(2,1)S(1)}, u32[]{:S(2)}, u32[]{:S(2)}) %collective-permute-start.2) | collective-permute-done | bytes 1310752 | tf_op jit(solution)/shard_map/ppermute | solution.py:47
  70.6 2.4 %collective-permute-start.9 = (bf16[512,512]{1,0:T(8,128)(2,1)S(1)}, bf16[512,512]{1,0:T(8,128)(2,1)S(1)}, u32[]{:S(2)}, u32[]{:S(2)}) collective-permute-start(bf16[512,512]{1,0:T(8,128)(2,1)S(1)} %get-tuple-element.37), channel_id=1, source_target_pairs={{0,96},{4,28},{8,104},{12,4},{16,112},{20,12},{24,120},{28,20},{32... | collective-permute-start | bytes 1572872 | tf_op jit(solution)/shard_map/ppermute | solution.py:47
  73.0 3.6 %product.4 = (bf16[320,512]{1,0:T(8,128)(2,1)S(1)}, bf16[320,512]{1,0:T(8,128)(2,1)S(1)}, bf16[320,512]{1,0:T(8,128)(2,1)S(1)}, bf16[320,512]{1,0:T(8,128)(2,1)S(1)}) custom-call(s32[4]{0:T(128)S(1)} %pad_add_fusion.place_ref, bf16[1280,512]{1,0:T(8,128)(2,1)S(1)} %get-tuple-element.32.refs_0_, bf16[1280,512]{1,0:T(8,128)(2,1)S(1)} %collective-permute-done.2.refs_1_, ...), custom_call_target="tpu_custom_call" | custom-call | flops 2684354560 | bytes 7340032 | tf_op jit(solution)/shard_map/product/pallas_call | solution.py:234
  78.4 6.5 %product.5 = (bf16[320,1024]{1,0:T(8,128)(2,1)S(1)}, bf16[320,1024]{1,0:T(8,128)(2,1)S(1)}, bf16[320,1024]{1,0:T(8,128)(2,1)S(1)}, bf16[320,1024]{1,0:T(8,128)(2,1)S(1)}) custom-call(s32[4]{0:T(128)S(1)} %pad_add_fusion.place_ref, bf16[1280,512]{1,0:T(8,128)(2,1)S(1)} %get-tuple-element.32.refs_0_, bf16[1280,512]{1,0:T(8,128)(2,1)S(1)} %collective-permute-done.2.refs_1_, ...), custom_call_target="tpu_custom_call" | custom-call | flops 5368709120 | bytes 7340032 | tf_op jit(solution)/shard_map/product/pallas_call | solution.py:234
  87.5 3.0 %collective-permute-start.23 = (bf16[320,1024]{1,0:T(8,128)(2,1)S(1)}, bf16[320,1024]{1,0:T(8,128)(2,1)S(1)}, u32[]{:S(2)}, u32[]{:S(2)}) collective-permute-start(bf16[320,1024]{1,0:T(8,128)(2,1)S(1)} %get-tuple-element.50), channel_id=1, source_target_pairs={{0,16},{4,68},{8,24},{12,76},{16,0},{20,84},{24,8},{28,92},{32,48}... | collective-permute-start | bytes 1966088 | tf_op jit(solution)/shard_map/ppermute | solution.py:51
  92.0 4.4 %collective-permute-start.18 = (bf16[320,512]{1,0:T(8,128)(2,1)S(1)}, bf16[320,512]{1,0:T(8,128)(2,1)S(1)}, u32[]{:S(2)}, u32[]{:S(2)}) collective-permute-start(bf16[320,512]{1,0:T(8,128)(2,1)S(1)} %get-tuple-element.46), channel_id=1, source_target_pairs={{0,16},{4,68},{8,24},{12,76},{16,0},{20,84},{24,8},{28,92},{32,48}... | collective-permute-start | bytes 983048 | tf_op jit(solution)/shard_map/ppermute | solution.py:51
  97.0 3.6 %product.3 = (bf16[320,512]{1,0:T(8,128)(2,1)S(1)}, bf16[320,512]{1,0:T(8,128)(2,1)S(1)}, bf16[320,512]{1,0:T(8,128)(2,1)S(1)}, bf16[320,512]{1,0:T(8,128)(2,1)S(1)}) custom-call(s32[4]{0:T(128)S(1)} %pad_add_fusion.place_ref, bf16[1280,512]{1,0:T(8,128)(2,1)S(1)} %get-tuple-element.32.refs_0_, bf16[1280,512]{1,0:T(8,128)(2,1)S(1)} %collective-permute-done.2.refs_1_, ...), custom_call_target="tpu_custom_call" | custom-call | flops 2684354560 | bytes 7340032 | tf_op jit(solution)/shard_map/product/pallas_call | solution.py:234
  100.6 6.7 %collective-permute-done.18.refs_2_ = bf16[320,512]{1,0:T(8,128)(2,1)S(1)} collective-permute-done((bf16[320,512]{1,0:T(8,128)(2,1)S(1)}, bf16[320,512]{1,0:T(8,128)(2,1)S(1)}, u32[]{:S(2)}, u32[]{:S(2)}) %collective-permute-start.18) | collective-permute-done | bytes 327712 | tf_op jit(solution)/shard_map/ppermute | solution.py:51
  107.3 3.8 %collective-permute-start.10 = (bf16[320,512]{1,0:T(8,128)(2,1)S(1)}, bf16[320,512]{1,0:T(8,128)(2,1)S(1)}, u32[]{:S(2)}, u32[]{:S(2)}) collective-permute-start(bf16[320,512]{1,0:T(8,128)(2,1)S(1)} %get-tuple-element.39), channel_id=1, source_target_pairs={{0,8},{4,36},{8,16},{12,44},{16,24},{20,52},{24,0},{28,60},{32,40}... | collective-permute-start | bytes 983048 | tf_op jit(solution)/shard_map/ppermute | solution.py:51
  111.1 2.3 %collective-permute-done.19.refs_3_ = bf16[320,512]{1,0:T(8,128)(2,1)S(1)} collective-permute-done((bf16[320,512]{1,0:T(8,128)(2,1)S(1)}, bf16[320,512]{1,0:T(8,128)(2,1)S(1)}, u32[]{:S(2)}, u32[]{:S(2)}) %collective-permute-start.19) | collective-permute-done | bytes 327712 | tf_op jit(solution)/shard_map/ppermute | solution.py:51
  115.1 2.0 %collective-permute-start.12 = (bf16[320,512]{1,0:T(8,128)(2,1)S(1)}, bf16[320,512]{1,0:T(8,128)(2,1)S(1)}, u32[]{:S(2)}, u32[]{:S(2)}) collective-permute-start(bf16[320,512]{1,0:T(8,128)(2,1)S(1)} %get-tuple-element.41), channel_id=1, source_target_pairs={{0,24},{4,100},{8,0},{12,108},{16,8},{20,116},{24,16},{28,124},{32... | collective-permute-start | bytes 983048 | tf_op jit(solution)/shard_map/ppermute | solution.py:51
  119.0 3.6 %collective-permute-done.11.refs_2_ = bf16[320,512]{1,0:T(8,128)(2,1)S(1)} collective-permute-done((bf16[320,512]{1,0:T(8,128)(2,1)S(1)}, bf16[320,512]{1,0:T(8,128)(2,1)S(1)}, u32[]{:S(2)}, u32[]{:S(2)}) %collective-permute-start.11) | collective-permute-done | bytes 327712 | tf_op jit(solution)/shard_map/ppermute | solution.py:51
  122.6 2.8 %collective-permute-done.12.refs_3_ = bf16[320,512]{1,0:T(8,128)(2,1)S(1)} collective-permute-done((bf16[320,512]{1,0:T(8,128)(2,1)S(1)}, bf16[320,512]{1,0:T(8,128)(2,1)S(1)}, u32[]{:S(2)}, u32[]{:S(2)}) %collective-permute-start.12) | collective-permute-done | bytes 327712 | tf_op jit(solution)/shard_map/ppermute | solution.py:51
  127.4 14.3 %all_to_all.5.shared = f32[128,1,128]{2,1,0:T(1,128)S(1)} all-to-all(f32[128,1,128]{2,1,0:T(1,128)S(1)} %get-tuple-element.53), channel_id=1, replica_groups=mesh['z'=4,'x'=4,'c'=2,'y'=4] {'z','x','c','y'}, dimensions={0} | all-to-all | bytes 131072 | tf_op jit(solution)/shard_map/all_to_all | solution.py:410
  141.7 6.1 %adam.1 = (f32[160,4096]{1,0:T(8,128)}, f32[160,4096]{1,0:T(8,128)}, f32[160,4096]{1,0:T(8,128)}, bf16[160,4096]{1,0:T(8,128)(2,1)}) custom-call(s32[4]{0:T(128)S(1)} %pad_add_fusion.place_ref, f32[128,1,128]{2,1,0:T(1,128)S(1)} %all_to_all.5.shared, bf16[160,512]{1,0:T(8,128)(2,1)} %get-tuple-element.54.refs_0_, ...), custom_call_target="tpu_custom_call" | custom-call | flops 10000000 | bytes 17000000 | tf_op jit(solution)/shard_map/adam/pallas_call | solution.py:358
  (53 shorter events, 21.3 us)
Async XLA Ops:
  0.6 31.3 %collective-permute-start = (bf16[2,128,5120]{2,1,0:T(8,128)(2,1)}, bf16[2,128,5120]{2,1,0:T(8,128)(2,1)S(1)}, u32[]{:S(2)}, u32[]{:S(2)}) collective-permute-start(bf16[2,128,5120]{2,1,0:T(8,128)(2,1)} %own_ref.2), channel_id=1, source_target_pairs={{0,4},{4,0},{1,5},{5,1},{2,6},{6,2},{3,7},{7,3},{8,12},{12,8},{9,1... | collective-permute-start | bytes 7864328 | tf_op jit(solution)/shard_map/ppermute | solution.py:59
  0.7 38.8 %collective-permute-start.5 = (bf16[2,128,4096]{2,1,0:T(8,128)(2,1)}, bf16[2,128,4096]{2,1,0:T(8,128)(2,1)}, u32[]{:S(2)}, u32[]{:S(2)}) collective-permute-start(bf16[2,128,4096]{2,1,0:T(8,128)(2,1)} %theirs_ref.1), channel_id=1, source_target_pairs={{0,4},{4,0},{1,5},{5,1},{2,6},{6,2},{3,7},{7,3},{8,12},{12,8},{9,1... | collective-permute-start | bytes 6291464 | tf_op jit(solution)/shard_map/ppermute | solution.py:59
  9.2 11.4 %collective-permute-start.14 = (bf16[512,512]{1,0:T(8,128)(2,1)S(1)}, bf16[512,512]{1,0:T(8,128)(2,1)S(1)}, u32[]{:S(2)}, u32[]{:S(2)}) collective-permute-start(bf16[512,512]{1,0:T(8,128)(2,1)S(1)} %constant_dynamic-update-slice_fusion), channel_id=1, source_target_pairs={{0,32},{4,12},{8,40},{12,20},{16,48},{20,28},{24,56},{28,4},{32,64... | collective-permute-start | bytes 1572872 | tf_op jit(solution)/shard_map/ppermute | solution.py:47
  11.3 16.4 %collective-permute-start.15 = (bf16[512,512]{1,0:T(8,128)(2,1)S(1)}, bf16[512,512]{1,0:T(8,128)(2,1)S(1)}, u32[]{:S(2)}, u32[]{:S(2)}) collective-permute-start(bf16[512,512]{1,0:T(8,128)(2,1)S(1)} %constant_dynamic-update-slice_fusion), channel_id=1, source_target_pairs={{0,64},{4,20},{8,72},{12,28},{16,80},{20,4},{24,88},{28,12},{32,96... | collective-permute-start | bytes 1572872 | tf_op jit(solution)/shard_map/ppermute | solution.py:47
  14.9 12.8 %collective-permute-start.16 = (bf16[512,512]{1,0:T(8,128)(2,1)S(1)}, bf16[512,512]{1,0:T(8,128)(2,1)S(1)}, u32[]{:S(2)}, u32[]{:S(2)}) collective-permute-start(bf16[512,512]{1,0:T(8,128)(2,1)S(1)} %constant_dynamic-update-slice_fusion), channel_id=1, source_target_pairs={{0,96},{4,28},{8,104},{12,4},{16,112},{20,12},{24,120},{28,20},{32... | collective-permute-start | bytes 1572872 | tf_op jit(solution)/shard_map/ppermute | solution.py:47
  20.6 16.8 %collective-permute-start.6 = (bf16[2,32]{1,0:T(2,128)(2,1)S(1)}, bf16[2,32]{1,0:T(2,128)(2,1)S(1)}, u32[]{:S(2)}, u32[]{:S(2)}) collective-permute-start(bf16[2,32]{1,0:T(2,128)(2,1)S(1)} %copy-done.1), channel_id=1, source_target_pairs={{0,4},{4,0},{1,5},{5,1},{2,6},{6,2},{3,7},{7,3},{8,12},{12,8},{9,1... | collective-permute-start | bytes 392 | tf_op jit(solution)/shard_map/ppermute | solution.py:59
  27.9 48.8 %collective-permute-start.20 = (bf16[3,512,512]{2,1,0:T(8,128)(2,1)S(1)}, bf16[3,512,512]{2,1,0:T(8,128)(2,1)S(1)}, u32[]{:S(2)}, u32[]{:S(2)}) collective-permute-start(bf16[3,512,512]{2,1,0:T(8,128)(2,1)S(1)} %pad_maximum_fusion.refs_5_), channel_id=1, source_target_pairs={{0,1},{1,2},{2,3},{3,0},{4,5},{5,6},{6,7},{7,4},{8,9},{9,10},{10,1... | collective-permute-start | bytes 4718600 | tf_op jit(solution)/shard_map/ppermute | solution.py:55
  29.5 48.9 %collective-permute-start.21 = (bf16[3,512,512]{2,1,0:T(8,128)(2,1)S(1)}, bf16[3,512,512]{2,1,0:T(8,128)(2,1)S(1)}, u32[]{:S(2)}, u32[]{:S(2)}) collective-permute-start(bf16[3,512,512]{2,1,0:T(8,128)(2,1)S(1)} %pad_maximum_fusion.refs_5_), channel_id=1, source_target_pairs={{0,3},{1,0},{2,1},{3,2},{4,7},{5,4},{6,5},{7,6},{8,11},{9,8},{10,9... | collective-permute-start | bytes 4718600 | tf_op jit(solution)/shard_map/ppermute | solution.py:55
  36.5 32.9 %collective-permute-start.2 = (bf16[1280,512]{1,0:T(8,128)(2,1)S(1)}, bf16[1280,512]{1,0:T(8,128)(2,1)S(1)}, u32[]{:S(2)}, u32[]{:S(2)}) collective-permute-start(bf16[1280,512]{1,0:T(8,128)(2,1)S(1)} %get-tuple-element.33), channel_id=1, source_target_pairs={{0,32},{4,12},{8,40},{12,20},{16,48},{20,28},{24,56},{28,4},{32,64... | collective-permute-start | bytes 3932168 | tf_op jit(solution)/shard_map/ppermute | solution.py:47
  37.4 32.1 %collective-permute-start.3 = (bf16[1280,512]{1,0:T(8,128)(2,1)S(1)}, bf16[1280,512]{1,0:T(8,128)(2,1)S(1)}, u32[]{:S(2)}, u32[]{:S(2)}) collective-permute-start(bf16[1280,512]{1,0:T(8,128)(2,1)S(1)} %get-tuple-element.34), channel_id=1, source_target_pairs={{0,64},{4,20},{8,72},{12,28},{16,80},{20,4},{24,88},{28,12},{32,96... | collective-permute-start | bytes 3932168 | tf_op jit(solution)/shard_map/ppermute | solution.py:47
  39.5 31.1 %collective-permute-start.4 = (bf16[1280,512]{1,0:T(8,128)(2,1)S(1)}, bf16[1280,512]{1,0:T(8,128)(2,1)S(1)}, u32[]{:S(2)}, u32[]{:S(2)}) collective-permute-start(bf16[1280,512]{1,0:T(8,128)(2,1)S(1)} %get-tuple-element.35), channel_id=1, source_target_pairs={{0,96},{4,28},{8,104},{12,4},{16,112},{20,12},{24,120},{28,20},{32... | collective-permute-start | bytes 3932168 | tf_op jit(solution)/shard_map/ppermute | solution.py:47
  69.5 18.1 %collective-permute-start.7 = (bf16[512,512]{1,0:T(8,128)(2,1)S(1)}, bf16[512,512]{1,0:T(8,128)(2,1)S(1)}, u32[]{:S(2)}, u32[]{:S(2)}) collective-permute-start(bf16[512,512]{1,0:T(8,128)(2,1)S(1)} %get-tuple-element.37), channel_id=1, source_target_pairs={{0,32},{4,12},{8,40},{12,20},{16,48},{20,28},{24,56},{28,4},{32,64... | collective-permute-start | bytes 1572872 | tf_op jit(solution)/shard_map/ppermute | solution.py:47
  69.5 21.1 %collective-permute-start.8 = (bf16[512,512]{1,0:T(8,128)(2,1)S(1)}, bf16[512,512]{1,0:T(8,128)(2,1)S(1)}, u32[]{:S(2)}, u32[]{:S(2)}) collective-permute-start(bf16[512,512]{1,0:T(8,128)(2,1)S(1)} %get-tuple-element.37), channel_id=1, source_target_pairs={{0,64},{4,20},{8,72},{12,28},{16,80},{20,4},{24,88},{28,12},{32,96... | collective-permute-start | bytes 1572872 | tf_op jit(solution)/shard_map/ppermute | solution.py:47
  70.6 21.4 %collective-permute-start.9 = (bf16[512,512]{1,0:T(8,128)(2,1)S(1)}, bf16[512,512]{1,0:T(8,128)(2,1)S(1)}, u32[]{:S(2)}, u32[]{:S(2)}) collective-permute-start(bf16[512,512]{1,0:T(8,128)(2,1)S(1)} %get-tuple-element.37), channel_id=1, source_target_pairs={{0,96},{4,28},{8,104},{12,4},{16,112},{20,12},{24,120},{28,20},{32... | collective-permute-start | bytes 1572872 | tf_op jit(solution)/shard_map/ppermute | solution.py:47
  76.6 19.8 %collective-permute-start.17 = (bf16[320,512]{1,0:T(8,128)(2,1)S(1)}, bf16[320,512]{1,0:T(8,128)(2,1)S(1)}, u32[]{:S(2)}, u32[]{:S(2)}) collective-permute-start(bf16[320,512]{1,0:T(8,128)(2,1)S(1)} %get-tuple-element.45), channel_id=1, source_target_pairs={{0,8},{4,36},{8,16},{12,44},{16,24},{20,52},{24,0},{28,60},{32,40}... | collective-permute-start | bytes 983048 | tf_op jit(solution)/shard_map/ppermute | solution.py:51
  84.9 30.2 %collective-permute-start.22 = (bf16[320,1024]{1,0:T(8,128)(2,1)S(1)}, bf16[320,1024]{1,0:T(8,128)(2,1)S(1)}, u32[]{:S(2)}, u32[]{:S(2)}) collective-permute-start(bf16[320,1024]{1,0:T(8,128)(2,1)S(1)} %get-tuple-element.49), channel_id=1, source_target_pairs={{0,8},{4,36},{8,16},{12,44},{16,24},{20,52},{24,0},{28,60},{32,40}... | collective-permute-start | bytes 1966088 | tf_op jit(solution)/shard_map/ppermute | solution.py:51
  87.5 29.6 %collective-permute-start.23 = (bf16[320,1024]{1,0:T(8,128)(2,1)S(1)}, bf16[320,1024]{1,0:T(8,128)(2,1)S(1)}, u32[]{:S(2)}, u32[]{:S(2)}) collective-permute-start(bf16[320,1024]{1,0:T(8,128)(2,1)S(1)} %get-tuple-element.50), channel_id=1, source_target_pairs={{0,16},{4,68},{8,24},{12,76},{16,0},{20,84},{24,8},{28,92},{32,48}... | collective-permute-start | bytes 1966088 | tf_op jit(solution)/shard_map/ppermute | solution.py:51
  90.5 26.6 %collective-permute-start.24 = (bf16[320,1024]{1,0:T(8,128)(2,1)S(1)}, bf16[320,1024]{1,0:T(8,128)(2,1)S(1)}, u32[]{:S(2)}, u32[]{:S(2)}) collective-permute-start(bf16[320,1024]{1,0:T(8,128)(2,1)S(1)} %get-tuple-element.51), channel_id=1, source_target_pairs={{0,24},{4,100},{8,0},{12,108},{16,8},{20,116},{24,16},{28,124},{32... | collective-permute-start | bytes 1966088 | tf_op jit(solution)/shard_map/ppermute | solution.py:51
  92.0 15.3 %collective-permute-start.18 = (bf16[320,512]{1,0:T(8,128)(2,1)S(1)}, bf16[320,512]{1,0:T(8,128)(2,1)S(1)}, u32[]{:S(2)}, u32[]{:S(2)}) collective-permute-start(bf16[320,512]{1,0:T(8,128)(2,1)S(1)} %get-tuple-element.46), channel_id=1, source_target_pairs={{0,16},{4,68},{8,24},{12,76},{16,0},{20,84},{24,8},{28,92},{32,48}... | collective-permute-start | bytes 983048 | tf_op jit(solution)/shard_map/ppermute | solution.py:51
  96.4 17.0 %collective-permute-start.19 = (bf16[320,512]{1,0:T(8,128)(2,1)S(1)}, bf16[320,512]{1,0:T(8,128)(2,1)S(1)}, u32[]{:S(2)}, u32[]{:S(2)}) collective-permute-start(bf16[320,512]{1,0:T(8,128)(2,1)S(1)} %get-tuple-element.47), channel_id=1, source_target_pairs={{0,24},{4,100},{8,0},{12,108},{16,8},{20,116},{24,16},{28,124},{32... | collective-permute-start | bytes 983048 | tf_op jit(solution)/shard_map/ppermute | solution.py:51
  107.3 11.7 %collective-permute-start.10 = (bf16[320,512]{1,0:T(8,128)(2,1)S(1)}, bf16[320,512]{1,0:T(8,128)(2,1)S(1)}, u32[]{:S(2)}, u32[]{:S(2)}) collective-permute-start(bf16[320,512]{1,0:T(8,128)(2,1)S(1)} %get-tuple-element.39), channel_id=1, source_target_pairs={{0,8},{4,36},{8,16},{12,44},{16,24},{20,52},{24,0},{28,60},{32,40}... | collective-permute-start | bytes 983048 | tf_op jit(solution)/shard_map/ppermute | solution.py:51
  119.0 22.7 %collective-permute-start.26 = (bf16[160,1024]{1,0:T(8,128)(2,1)}, bf16[160,1024]{1,0:T(8,128)(2,1)S(1)}, u32[]{:S(2)}, u32[]{:S(2)}) collective-permute-start(bf16[160,1024]{1,0:T(8,128)(2,1)} %get-tuple-element.57), channel_id=1, source_target_pairs={{0,4},{4,0},{1,5},{5,1},{2,6},{6,2},{3,7},{7,3},{8,12},{12,8},{9,1... | collective-permute-start | bytes 983048 | tf_op jit(solution)/shard_map/ppermute | solution.py:59
  126.9 14.8 %collective-permute-start.27 = (bf16[160,512]{1,0:T(8,128)(2,1)}, bf16[160,512]{1,0:T(8,128)(2,1)S(1)}, u32[]{:S(2)}, u32[]{:S(2)}) collective-permute-start(bf16[160,512]{1,0:T(8,128)(2,1)} %get-tuple-element.59), channel_id=1, source_target_pairs={{0,4},{4,0},{1,5},{5,1},{2,6},{6,2},{3,7},{7,3},{8,12},{12,8},{9,1... | collective-permute-start | bytes 491528 | tf_op jit(solution)/shard_map/ppermute | solution.py:59
  126.9 14.8 %collective-permute-start.25 = (bf16[160,512]{1,0:T(8,128)(2,1)}, bf16[160,512]{1,0:T(8,128)(2,1)S(1)}, u32[]{:S(2)}, u32[]{:S(2)}) collective-permute-start(bf16[160,512]{1,0:T(8,128)(2,1)} %get-tuple-element.55), channel_id=1, source_target_pairs={{0,4},{4,0},{1,5},{5,1},{2,6},{6,2},{3,7},{7,3},{8,12},{12,8},{9,1... | collective-permute-start | bytes 491528 | tf_op jit(solution)/shard_map/ppermute | solution.py:59
  (7 other events, 86.0 us)

commit v6 on v5

--- a/solution.py
+++ b/solution.py
@@ -285,7 +285,8 @@
     shapes = []
     for piece in pieces:
         both, width = piece[0].shape
-        shapes += [pltpu.HBM((both // 2, width), jnp.bfloat16)] * 2
+        given = pltpu.HBM((both // 2, width), jnp.bfloat16)
+        shapes += [jax.ShapeDtypeStruct((both // 2, width), jnp.bfloat16) if last else given, given]
     shapes.append(jax.ShapeDtypeStruct((128, 1, 128) if last else (8, 128), jnp.float32))
     *values, squares = pl.pallas_call(
         functools.partial(sums_kernel, len(pieces), last),
@@ -313,7 +314,7 @@
         at = pl.ds(pl.multiple_of((2 * lax.rem(y + offset, 4) + half) * piece, piece), piece)
         ats.append(at)
         copies = []
-        if side == 0:
+        if side == 0 and which < EARLY:
             from_grad = grads[2 * which].at[:, lead * piece : (lead + 1) * piece]
             copies.append(pltpu.make_async_copy(from_grad, grad_in.at[n // 2], in_sems.at[n, 3]))
         for i, source in enumerate(sources):
@@ -329,7 +330,10 @@
         for copy in fetches[n]:
             copy.wait()
         _, which, lead, side = blocks[n]
-        grad = grad_in[n // 2] if side == 0 else grads[2 * which + 1][:, lead * piece : (lead + 1) * piece]
+        if side == 0 and which < EARLY:
+            grad = grad_in[n // 2]
+        else:
+            grad = grads[2 * which + side][:, lead * piece : (lead + 1) * piece]
         clipped = factor[0:1, 0:1] * grad.astype(jnp.float32)
         new_moment = beta_first * held[:, at] + (1.0 - beta_first) * clipped
         new_second = beta_second * read[n, 0] + (1.0 - beta_second) * clipped * clipped
@@ -353,7 +357,7 @@
     hbm = pl.BlockSpec(memory_space=pltpu.HBM)
     wide = jax.ShapeDtypeStruct((own, rows), jnp.float32)
     flat = [a for pair in pairs for a in pair] + [second, master, moment]
-    spaces = [pltpu.HBM, pltpu.VMEM] * len(pairs) + [pltpu.HBM, pltpu.HBM, pltpu.VMEM]
+    spaces = [pltpu.HBM, pltpu.VMEM] * EARLY + [pltpu.VMEM] * (2 * (len(pairs) - EARLY)) + [pltpu.HBM, pltpu.HBM, pltpu.VMEM]
     flat = [pltpu.with_memory_space_constraint(a, space) for a, space in zip(flat, spaces)]
     return pl.pallas_call(
         functools.partial(adam_kernel, slots),

time: 149 us -> 149 us (level)
  no operation moved by 1% of the time
where the time goes in v6:
time: 149 us; the launch traced here: 148 us
  waiting for transfers between devices  59 us (40%)
  starting transfers between devices  40.3 us (27%)
  Pallas kernels  33.2 us (22%)
  blocking collectives  14.3 us (10%)
    ppermute x9, waiting for transfers between devices, gathered(): return lax.ppermute(a, DP, crossed(k, True))  37.7 us
    ppermute x9, starting transfers between devices, scattered(): return lax.ppermute(a, DP, crossed(k, False))  20.3 us
    ppermute x9, waiting for transfers between devices, scattered(): return lax.ppermute(a, DP, crossed(k, False))  15.3 us
    ppermute x9, starting transfers between devices, gathered(): return lax.ppermute(a, DP, crossed(k, True))  14.7 us
    all_to_all x1, blocking collectives, step(): shared = lax.all_to_all(squares, ALL, 0, 0, tiled=True)  14.3 us
    pallas_call x3, Pallas kernels, product(): pl.pallas_call(functools.partial(product_kernel, offsets, forms, width),...  13.7 us
    pallas_call x1, Pallas kernels, adam(): pl.pallas_call(functools.partial(adam_kernel, slots), in_specs=[SCALARS,...  6.12 us
    ppermute x8, waiting for transfers between devices, swapped(): return lax.ppermute(a, 'c', SWAP)  5.92 us
  transfers between devices with their start and end apart: 28, of which 9 were waited for; matrix products, arithmetic and copies ran while one was open for 0% of the time, Pallas kernels for 18%

profile of v6, /device:TPU:0, one launch (start us, length us, event | category | flops | bytes accessed | tf_op | source)
XLA Modules:
  0.0 148.0 jit_solution(17514238988768305250)
XLA Ops:
  3.3 5.9 %collective-permute-done.13 = bf16[256,512]{1,0:T(8,128)(2,1)S(1)} collective-permute-done((bf16[256,512]{1,0:T(8,128)(2,1)S(1)}, bf16[256,512]{1,0:T(8,128)(2,1)S(1)}, u32[]{:S(2)}, u32[]{:S(2)}) %collective-permute-start.13) | collective-permute-done | bytes 262176 | tf_op jit(solution)/shard_map/ppermute | solution.py:59
  9.2 2.1 %collective-permute-start.14 = (bf16[512,512]{1,0:T(8,128)(2,1)S(1)}, bf16[512,512]{1,0:T(8,128)(2,1)S(1)}, u32[]{:S(2)}, u32[]{:S(2)}) collective-permute-start(bf16[512,512]{1,0:T(8,128)(2,1)S(1)} %constant_dynamic-update-slice_fusion), channel_id=1, source_target_pairs={{0,32},{4,12},{8,40},{12,20},{16,48},{20,28},{24,56},{28,4},{32,64... | collective-permute-start | bytes 1572872 | tf_op jit(solution)/shard_map/ppermute | solution.py:47
  11.3 3.6 %collective-permute-start.15 = (bf16[512,512]{1,0:T(8,128)(2,1)S(1)}, bf16[512,512]{1,0:T(8,128)(2,1)S(1)}, u32[]{:S(2)}, u32[]{:S(2)}) collective-permute-start(bf16[512,512]{1,0:T(8,128)(2,1)S(1)} %constant_dynamic-update-slice_fusion), channel_id=1, source_target_pairs={{0,64},{4,20},{8,72},{12,28},{16,80},{20,4},{24,88},{28,12},{32,96... | collective-permute-start | bytes 1572872 | tf_op jit(solution)/shard_map/ppermute | solution.py:47
  16.0 4.6 %collective-permute-done.14 = bf16[512,512]{1,0:T(8,128)(2,1)S(1)} collective-permute-done((bf16[512,512]{1,0:T(8,128)(2,1)S(1)}, bf16[512,512]{1,0:T(8,128)(2,1)S(1)}, u32[]{:S(2)}, u32[]{:S(2)}) %collective-permute-start.14) | collective-permute-done | bytes 524320 | tf_op jit(solution)/shard_map/ppermute | solution.py:47
  20.6 7.1 %collective-permute-done.15 = bf16[512,512]{1,0:T(8,128)(2,1)S(1)} collective-permute-done((bf16[512,512]{1,0:T(8,128)(2,1)S(1)}, bf16[512,512]{1,0:T(8,128)(2,1)S(1)}, u32[]{:S(2)}, u32[]{:S(2)}) %collective-permute-start.15) | collective-permute-done | bytes 524320 | tf_op jit(solution)/shard_map/ppermute | solution.py:47
  29.5 2.4 %collective-permute-start.21 = (bf16[3,512,512]{2,1,0:T(8,128)(2,1)S(1)}, bf16[3,512,512]{2,1,0:T(8,128)(2,1)S(1)}, u32[]{:S(2)}, u32[]{:S(2)}) collective-permute-start(bf16[3,512,512]{2,1,0:T(8,128)(2,1)S(1)} %pad_maximum_fusion.refs_5_), channel_id=1, source_target_pairs={{0,3},{1,0},{2,1},{3,2},{4,7},{5,4},{6,5},{7,6},{8,11},{9,8},{10,9... | collective-permute-start | bytes 4718600 | tf_op jit(solution)/shard_map/ppermute | solution.py:55
  31.9 4.6 %prep.1 = (bf16[1280,512]{1,0:T(8,128)(2,1)S(1)}, bf16[1280,512]{1,0:T(8,128)(2,1)S(1)}, bf16[1280,512]{1,0:T(8,128)(2,1)S(1)}, bf16[1280,512]{1,0:T(8,128)(2,1)S(1)}) custom-call(s32[4]{0:T(128)S(1)} %pad_add_fusion.place_ref, bf16[2,128,5120]{2,1,0:T(8,128)(2,1)} %own_ref.2, bf16[2,128,5120]{2,1,0:T(8,128)(2,1)S(1)} %collective-permute-done.other_ref, ...), custom_call_target="tpu_custom_call" | custom-call | flops 1000000000 | bytes 10485760 | tf_op jit(solution)/shard_map/prep/pallas_call | solution.py:182
  37.4 2.1 %collective-permute-start.3 = (bf16[1280,512]{1,0:T(8,128)(2,1)S(1)}, bf16[1280,512]{1,0:T(8,128)(2,1)S(1)}, u32[]{:S(2)}, u32[]{:S(2)}) collective-permute-start(bf16[1280,512]{1,0:T(8,128)(2,1)S(1)} %get-tuple-element.34), channel_id=1, source_target_pairs={{0,64},{4,20},{8,72},{12,28},{16,80},{20,4},{24,88},{28,12},{32,96... | collective-permute-start | bytes 3932168 | tf_op jit(solution)/shard_map/ppermute | solution.py:47
  41.0 3.5 %acts.1 = (bf16[512,2048]{1,0:T(8,128)(2,1)S(1)}, bf16[512,512]{1,0:T(8,128)(2,1)S(1)}) custom-call(s32[4]{0:T(128)S(1)} %pad_add_fusion.place_ref, bf16[2,128,4096]{2,1,0:T(8,128)(2,1)} %theirs_ref.1, bf16[2,128,4096]{2,1,0:T(8,128)(2,1)} %collective-permute-done.5.other_ref, bf16[2,32]{1,0:T(2,128)(2,1)S(1)} %copy-done.1, ...), custom_call_target="tpu_custom_call" | custom-call | flops 1000000 | bytes 4000000 | tf_op jit(solution)/shard_map/acts/pallas_call | solution.py:131
  44.6 24.9 %collective-permute-done.2.refs_1_ = bf16[1280,512]{1,0:T(8,128)(2,1)S(1)} collective-permute-done((bf16[1280,512]{1,0:T(8,128)(2,1)S(1)}, bf16[1280,512]{1,0:T(8,128)(2,1)S(1)}, u32[]{:S(2)}, u32[]{:S(2)}) %collective-permute-start.2) | collective-permute-done | bytes 1310752 | tf_op jit(solution)/shard_map/ppermute | solution.py:47
  70.6 2.4 %collective-permute-start.9 = (bf16[512,512]{1,0:T(8,128)(2,1)S(1)}, bf16[512,512]{1,0:T(8,128)(2,1)S(1)}, u32[]{:S(2)}, u32[]{:S(2)}) collective-permute-start(bf16[512,512]{1,0:T(8,128)(2,1)S(1)} %get-tuple-element.37), channel_id=1, source_target_pairs={{0,96},{4,28},{8,104},{12,4},{16,112},{20,12},{24,120},{28,20},{32... | collective-permute-start | bytes 1572872 | tf_op jit(solution)/shard_map/ppermute | solution.py:47
  73.0 3.6 %product.4 = (bf16[320,512]{1,0:T(8,128)(2,1)S(1)}, bf16[320,512]{1,0:T(8,128)(2,1)S(1)}, bf16[320,512]{1,0:T(8,128)(2,1)S(1)}, bf16[320,512]{1,0:T(8,128)(2,1)S(1)}) custom-call(s32[4]{0:T(128)S(1)} %pad_add_fusion.place_ref, bf16[1280,512]{1,0:T(8,128)(2,1)S(1)} %get-tuple-element.32.refs_0_, bf16[1280,512]{1,0:T(8,128)(2,1)S(1)} %collective-permute-done.2.refs_1_, ...), custom_call_target="tpu_custom_call" | custom-call | flops 2684354560 | bytes 7340032 | tf_op jit(solution)/shard_map/product/pallas_call | solution.py:234
  78.4 6.5 %product.5 = (bf16[320,1024]{1,0:T(8,128)(2,1)S(1)}, bf16[320,1024]{1,0:T(8,128)(2,1)S(1)}, bf16[320,1024]{1,0:T(8,128)(2,1)S(1)}, bf16[320,1024]{1,0:T(8,128)(2,1)S(1)}) custom-call(s32[4]{0:T(128)S(1)} %pad_add_fusion.place_ref, bf16[1280,512]{1,0:T(8,128)(2,1)S(1)} %get-tuple-element.32.refs_0_, bf16[1280,512]{1,0:T(8,128)(2,1)S(1)} %collective-permute-done.2.refs_1_, ...), custom_call_target="tpu_custom_call" | custom-call | flops 5368709120 | bytes 7340032 | tf_op jit(solution)/shard_map/product/pallas_call | solution.py:234
  87.5 3.0 %collective-permute-start.23 = (bf16[320,1024]{1,0:T(8,128)(2,1)S(1)}, bf16[320,1024]{1,0:T(8,128)(2,1)S(1)}, u32[]{:S(2)}, u32[]{:S(2)}) collective-permute-start(bf16[320,1024]{1,0:T(8,128)(2,1)S(1)} %get-tuple-element.50), channel_id=1, source_target_pairs={{0,16},{4,68},{8,24},{12,76},{16,0},{20,84},{24,8},{28,92},{32,48}... | collective-permute-start | bytes 1966088 | tf_op jit(solution)/shard_map/ppermute | solution.py:51
  92.0 4.4 %collective-permute-start.18 = (bf16[320,512]{1,0:T(8,128)(2,1)S(1)}, bf16[320,512]{1,0:T(8,128)(2,1)S(1)}, u32[]{:S(2)}, u32[]{:S(2)}) collective-permute-start(bf16[320,512]{1,0:T(8,128)(2,1)S(1)} %get-tuple-element.46), channel_id=1, source_target_pairs={{0,16},{4,68},{8,24},{12,76},{16,0},{20,84},{24,8},{28,92},{32,48}... | collective-permute-start | bytes 983048 | tf_op jit(solution)/shard_map/ppermute | solution.py:51
  97.0 3.6 %product.3 = (bf16[320,512]{1,0:T(8,128)(2,1)S(1)}, bf16[320,512]{1,0:T(8,128)(2,1)S(1)}, bf16[320,512]{1,0:T(8,128)(2,1)S(1)}, bf16[320,512]{1,0:T(8,128)(2,1)S(1)}) custom-call(s32[4]{0:T(128)S(1)} %pad_add_fusion.place_ref, bf16[1280,512]{1,0:T(8,128)(2,1)S(1)} %get-tuple-element.32.refs_0_, bf16[1280,512]{1,0:T(8,128)(2,1)S(1)} %collective-permute-done.2.refs_1_, ...), custom_call_target="tpu_custom_call" | custom-call | flops 2684354560 | bytes 7340032 | tf_op jit(solution)/shard_map/product/pallas_call | solution.py:234
  100.6 6.7 %collective-permute-done.18.refs_2_ = bf16[320,512]{1,0:T(8,128)(2,1)S(1)} collective-permute-done((bf16[320,512]{1,0:T(8,128)(2,1)S(1)}, bf16[320,512]{1,0:T(8,128)(2,1)S(1)}, u32[]{:S(2)}, u32[]{:S(2)}) %collective-permute-start.18) | collective-permute-done | bytes 327712 | tf_op jit(solution)/shard_map/ppermute | solution.py:51
  107.3 3.8 %collective-permute-start.10 = (bf16[320,512]{1,0:T(8,128)(2,1)S(1)}, bf16[320,512]{1,0:T(8,128)(2,1)S(1)}, u32[]{:S(2)}, u32[]{:S(2)}) collective-permute-start(bf16[320,512]{1,0:T(8,128)(2,1)S(1)} %get-tuple-element.39), channel_id=1, source_target_pairs={{0,8},{4,36},{8,16},{12,44},{16,24},{20,52},{24,0},{28,60},{32,40}... | collective-permute-start | bytes 983048 | tf_op jit(solution)/shard_map/ppermute | solution.py:51
  111.1 2.3 %collective-permute-done.19.refs_3_ = bf16[320,512]{1,0:T(8,128)(2,1)S(1)} collective-permute-done((bf16[320,512]{1,0:T(8,128)(2,1)S(1)}, bf16[320,512]{1,0:T(8,128)(2,1)S(1)}, u32[]{:S(2)}, u32[]{:S(2)}) %collective-permute-start.19) | collective-permute-done | bytes 327712 | tf_op jit(solution)/shard_map/ppermute | solution.py:51
  115.1 2.0 %collective-permute-start.12 = (bf16[320,512]{1,0:T(8,128)(2,1)S(1)}, bf16[320,512]{1,0:T(8,128)(2,1)S(1)}, u32[]{:S(2)}, u32[]{:S(2)}) collective-permute-start(bf16[320,512]{1,0:T(8,128)(2,1)S(1)} %get-tuple-element.41), channel_id=1, source_target_pairs={{0,24},{4,100},{8,0},{12,108},{16,8},{20,116},{24,16},{28,124},{32... | collective-permute-start | bytes 983048 | tf_op jit(solution)/shard_map/ppermute | solution.py:51
  119.0 3.6 %collective-permute-done.11.refs_2_ = bf16[320,512]{1,0:T(8,128)(2,1)S(1)} collective-permute-done((bf16[320,512]{1,0:T(8,128)(2,1)S(1)}, bf16[320,512]{1,0:T(8,128)(2,1)S(1)}, u32[]{:S(2)}, u32[]{:S(2)}) %collective-permute-start.11) | collective-permute-done | bytes 327712 | tf_op jit(solution)/shard_map/ppermute | solution.py:51
  122.6 2.8 %collective-permute-done.12.refs_3_ = bf16[320,512]{1,0:T(8,128)(2,1)S(1)} collective-permute-done((bf16[320,512]{1,0:T(8,128)(2,1)S(1)}, bf16[320,512]{1,0:T(8,128)(2,1)S(1)}, u32[]{:S(2)}, u32[]{:S(2)}) %collective-permute-start.12) | collective-permute-done | bytes 327712 | tf_op jit(solution)/shard_map/ppermute | solution.py:51
  127.4 14.3 %all_to_all.5.shared = f32[128,1,128]{2,1,0:T(1,128)S(1)} all-to-all(f32[128,1,128]{2,1,0:T(1,128)S(1)} %get-tuple-element.53), channel_id=1, replica_groups=mesh['z'=4,'x'=4,'c'=2,'y'=4] {'z','x','c','y'}, dimensions={0} | all-to-all | bytes 131072 | tf_op jit(solution)/shard_map/all_to_all | solution.py:414
  141.7 6.1 %adam.1 = (f32[160,4096]{1,0:T(8,128)}, f32[160,4096]{1,0:T(8,128)}, f32[160,4096]{1,0:T(8,128)}, bf16[160,4096]{1,0:T(8,128)(2,1)}) custom-call(s32[4]{0:T(128)S(1)} %pad_add_fusion.place_ref, f32[128,1,128]{2,1,0:T(1,128)S(1)} %all_to_all.5.shared, bf16[160,512]{1,0:T(8,128)(2,1)} %get-tuple-element.54.refs_0_, ...), custom_call_target="tpu_custom_call" | custom-call | flops 10000000 | bytes 17000000 | tf_op jit(solution)/shard_map/adam/pallas_call | solution.py:362
  (53 shorter events, 21.3 us)
Async XLA Ops:
  0.6 31.3 %collective-permute-start = (bf16[2,128,5120]{2,1,0:T(8,128)(2,1)}, bf16[2,128,5120]{2,1,0:T(8,128)(2,1)S(1)}, u32[]{:S(2)}, u32[]{:S(2)}) collective-permute-start(bf16[2,128,5120]{2,1,0:T(8,128)(2,1)} %own_ref.2), channel_id=1, source_target_pairs={{0,4},{4,0},{1,5},{5,1},{2,6},{6,2},{3,7},{7,3},{8,12},{12,8},{9,1... | collective-permute-start | bytes 7864328 | tf_op jit(solution)/shard_map/ppermute | solution.py:59
  0.7 38.8 %collective-permute-start.5 = (bf16[2,128,4096]{2,1,0:T(8,128)(2,1)}, bf16[2,128,4096]{2,1,0:T(8,128)(2,1)}, u32[]{:S(2)}, u32[]{:S(2)}) collective-permute-start(bf16[2,128,4096]{2,1,0:T(8,128)(2,1)} %theirs_ref.1), channel_id=1, source_target_pairs={{0,4},{4,0},{1,5},{5,1},{2,6},{6,2},{3,7},{7,3},{8,12},{12,8},{9,1... | collective-permute-start | bytes 6291464 | tf_op jit(solution)/shard_map/ppermute | solution.py:59
  9.2 11.4 %collective-permute-start.14 = (bf16[512,512]{1,0:T(8,128)(2,1)S(1)}, bf16[512,512]{1,0:T(8,128)(2,1)S(1)}, u32[]{:S(2)}, u32[]{:S(2)}) collective-permute-start(bf16[512,512]{1,0:T(8,128)(2,1)S(1)} %constant_dynamic-update-slice_fusion), channel_id=1, source_target_pairs={{0,32},{4,12},{8,40},{12,20},{16,48},{20,28},{24,56},{28,4},{32,64... | collective-permute-start | bytes 1572872 | tf_op jit(solution)/shard_map/ppermute | solution.py:47
  11.3 16.4 %collective-permute-start.15 = (bf16[512,512]{1,0:T(8,128)(2,1)S(1)}, bf16[512,512]{1,0:T(8,128)(2,1)S(1)}, u32[]{:S(2)}, u32[]{:S(2)}) collective-permute-start(bf16[512,512]{1,0:T(8,128)(2,1)S(1)} %constant_dynamic-update-slice_fusion), channel_id=1, source_target_pairs={{0,64},{4,20},{8,72},{12,28},{16,80},{20,4},{24,88},{28,12},{32,96... | collective-permute-start | bytes 1572872 | tf_op jit(solution)/shard_map/ppermute | solution.py:47
  14.9 12.8 %collective-permute-start.16 = (bf16[512,512]{1,0:T(8,128)(2,1)S(1)}, bf16[512,512]{1,0:T(8,128)(2,1)S(1)}, u32[]{:S(2)}, u32[]{:S(2)}) collective-permute-start(bf16[512,512]{1,0:T(8,128)(2,1)S(1)} %constant_dynamic-update-slice_fusion), channel_id=1, source_target_pairs={{0,96},{4,28},{8,104},{12,4},{16,112},{20,12},{24,120},{28,20},{32... | collective-permute-start | bytes 1572872 | tf_op jit(solution)/shard_map/ppermute | solution.py:47
  20.6 16.8 %collective-permute-start.6 = (bf16[2,32]{1,0:T(2,128)(2,1)S(1)}, bf16[2,32]{1,0:T(2,128)(2,1)S(1)}, u32[]{:S(2)}, u32[]{:S(2)}) collective-permute-start(bf16[2,32]{1,0:T(2,128)(2,1)S(1)} %copy-done.1), channel_id=1, source_target_pairs={{0,4},{4,0},{1,5},{5,1},{2,6},{6,2},{3,7},{7,3},{8,12},{12,8},{9,1... | collective-permute-start | bytes 392 | tf_op jit(solution)/shard_map/ppermute | solution.py:59
  27.9 48.8 %collective-permute-start.20 = (bf16[3,512,512]{2,1,0:T(8,128)(2,1)S(1)}, bf16[3,512,512]{2,1,0:T(8,128)(2,1)S(1)}, u32[]{:S(2)}, u32[]{:S(2)}) collective-permute-start(bf16[3,512,512]{2,1,0:T(8,128)(2,1)S(1)} %pad_maximum_fusion.refs_5_), channel_id=1, source_target_pairs={{0,1},{1,2},{2,3},{3,0},{4,5},{5,6},{6,7},{7,4},{8,9},{9,10},{10,1... | collective-permute-start | bytes 4718600 | tf_op jit(solution)/shard_map/ppermute | solution.py:55
  29.5 48.9 %collective-permute-start.21 = (bf16[3,512,512]{2,1,0:T(8,128)(2,1)S(1)}, bf16[3,512,512]{2,1,0:T(8,128)(2,1)S(1)}, u32[]{:S(2)}, u32[]{:S(2)}) collective-permute-start(bf16[3,512,512]{2,1,0:T(8,128)(2,1)S(1)} %pad_maximum_fusion.refs_5_), channel_id=1, source_target_pairs={{0,3},{1,0},{2,1},{3,2},{4,7},{5,4},{6,5},{7,6},{8,11},{9,8},{10,9... | collective-permute-start | bytes 4718600 | tf_op jit(solution)/shard_map/ppermute | solution.py:55
  36.5 32.9 %collective-permute-start.2 = (bf16[1280,512]{1,0:T(8,128)(2,1)S(1)}, bf16[1280,512]{1,0:T(8,128)(2,1)S(1)}, u32[]{:S(2)}, u32[]{:S(2)}) collective-permute-start(bf16[1280,512]{1,0:T(8,128)(2,1)S(1)} %get-tuple-element.33), channel_id=1, source_target_pairs={{0,32},{4,12},{8,40},{12,20},{16,48},{20,28},{24,56},{28,4},{32,64... | collective-permute-start | bytes 3932168 | tf_op jit(solution)/shard_map/ppermute | solution.py:47
  37.4 32.1 %collective-permute-start.3 = (bf16[1280,512]{1,0:T(8,128)(2,1)S(1)}, bf16[1280,512]{1,0:T(8,128)(2,1)S(1)}, u32[]{:S(2)}, u32[]{:S(2)}) collective-permute-start(bf16[1280,512]{1,0:T(8,128)(2,1)S(1)} %get-tuple-element.34), channel_id=1, source_target_pairs={{0,64},{4,20},{8,72},{12,28},{16,80},{20,4},{24,88},{28,12},{32,96... | collective-permute-start | bytes 3932168 | tf_op jit(solution)/shard_map/ppermute | solution.py:47
  39.5 31.1 %collective-permute-start.4 = (bf16[1280,512]{1,0:T(8,128)(2,1)S(1)}, bf16[1280,512]{1,0:T(8,128)(2,1)S(1)}, u32[]{:S(2)}, u32[]{:S(2)}) collective-permute-start(bf16[1280,512]{1,0:T(8,128)(2,1)S(1)} %get-tuple-element.35), channel_id=1, source_target_pairs={{0,96},{4,28},{8,104},{12,4},{16,112},{20,12},{24,120},{28,20},{32... | collective-permute-start | bytes 3932168 | tf_op jit(solution)/shard_map/ppermute | solution.py:47
  69.5 18.1 %collective-permute-start.7 = (bf16[512,512]{1,0:T(8,128)(2,1)S(1)}, bf16[512,512]{1,0:T(8,128)(2,1)S(1)}, u32[]{:S(2)}, u32[]{:S(2)}) collective-permute-start(bf16[512,512]{1,0:T(8,128)(2,1)S(1)} %get-tuple-element.37), channel_id=1, source_target_pairs={{0,32},{4,12},{8,40},{12,20},{16,48},{20,28},{24,56},{28,4},{32,64... | collective-permute-start | bytes 1572872 | tf_op jit(solution)/shard_map/ppermute | solution.py:47
  69.5 21.1 %collective-permute-start.8 = (bf16[512,512]{1,0:T(8,128)(2,1)S(1)}, bf16[512,512]{1,0:T(8,128)(2,1)S(1)}, u32[]{:S(2)}, u32[]{:S(2)}) collective-permute-start(bf16[512,512]{1,0:T(8,128)(2,1)S(1)} %get-tuple-element.37), channel_id=1, source_target_pairs={{0,64},{4,20},{8,72},{12,28},{16,80},{20,4},{24,88},{28,12},{32,96... | collective-permute-start | bytes 1572872 | tf_op jit(solution)/shard_map/ppermute | solution.py:47
  70.6 21.4 %collective-permute-start.9 = (bf16[512,512]{1,0:T(8,128)(2,1)S(1)}, bf16[512,512]{1,0:T(8,128)(2,1)S(1)}, u32[]{:S(2)}, u32[]{:S(2)}) collective-permute-start(bf16[512,512]{1,0:T(8,128)(2,1)S(1)} %get-tuple-element.37), channel_id=1, source_target_pairs={{0,96},{4,28},{8,104},{12,4},{16,112},{20,12},{24,120},{28,20},{32... | collective-permute-start | bytes 1572872 | tf_op jit(solution)/shard_map/ppermute | solution.py:47
  76.6 19.8 %collective-permute-start.17 = (bf16[320,512]{1,0:T(8,128)(2,1)S(1)}, bf16[320,512]{1,0:T(8,128)(2,1)S(1)}, u32[]{:S(2)}, u32[]{:S(2)}) collective-permute-start(bf16[320,512]{1,0:T(8,128)(2,1)S(1)} %get-tuple-element.45), channel_id=1, source_target_pairs={{0,8},{4,36},{8,16},{12,44},{16,24},{20,52},{24,0},{28,60},{32,40}... | collective-permute-start | bytes 983048 | tf_op jit(solution)/shard_map/ppermute | solution.py:51
  84.9 30.2 %collective-permute-start.22 = (bf16[320,1024]{1,0:T(8,128)(2,1)S(1)}, bf16[320,1024]{1,0:T(8,128)(2,1)S(1)}, u32[]{:S(2)}, u32[]{:S(2)}) collective-permute-start(bf16[320,1024]{1,0:T(8,128)(2,1)S(1)} %get-tuple-element.49), channel_id=1, source_target_pairs={{0,8},{4,36},{8,16},{12,44},{16,24},{20,52},{24,0},{28,60},{32,40}... | collective-permute-start | bytes 1966088 | tf_op jit(solution)/shard_map/ppermute | solution.py:51
  87.5 29.6 %collective-permute-start.23 = (bf16[320,1024]{1,0:T(8,128)(2,1)S(1)}, bf16[320,1024]{1,0:T(8,128)(2,1)S(1)}, u32[]{:S(2)}, u32[]{:S(2)}) collective-permute-start(bf16[320,1024]{1,0:T(8,128)(2,1)S(1)} %get-tuple-element.50), channel_id=1, source_target_pairs={{0,16},{4,68},{8,24},{12,76},{16,0},{20,84},{24,8},{28,92},{32,48}... | collective-permute-start | bytes 1966088 | tf_op jit(solution)/shard_map/ppermute | solution.py:51
  90.5 26.6 %collective-permute-start.24 = (bf16[320,1024]{1,0:T(8,128)(2,1)S(1)}, bf16[320,1024]{1,0:T(8,128)(2,1)S(1)}, u32[]{:S(2)}, u32[]{:S(2)}) collective-permute-start(bf16[320,1024]{1,0:T(8,128)(2,1)S(1)} %get-tuple-element.51), channel_id=1, source_target_pairs={{0,24},{4,100},{8,0},{12,108},{16,8},{20,116},{24,16},{28,124},{32... | collective-permute-start | bytes 1966088 | tf_op jit(solution)/shard_map/ppermute | solution.py:51
  92.0 15.3 %collective-permute-start.18 = (bf16[320,512]{1,0:T(8,128)(2,1)S(1)}, bf16[320,512]{1,0:T(8,128)(2,1)S(1)}, u32[]{:S(2)}, u32[]{:S(2)}) collective-permute-start(bf16[320,512]{1,0:T(8,128)(2,1)S(1)} %get-tuple-element.46), channel_id=1, source_target_pairs={{0,16},{4,68},{8,24},{12,76},{16,0},{20,84},{24,8},{28,92},{32,48}... | collective-permute-start | bytes 983048 | tf_op jit(solution)/shard_map/ppermute | solution.py:51
  96.4 17.0 %collective-permute-start.19 = (bf16[320,512]{1,0:T(8,128)(2,1)S(1)}, bf16[320,512]{1,0:T(8,128)(2,1)S(1)}, u32[]{:S(2)}, u32[]{:S(2)}) collective-permute-start(bf16[320,512]{1,0:T(8,128)(2,1)S(1)} %get-tuple-element.47), channel_id=1, source_target_pairs={{0,24},{4,100},{8,0},{12,108},{16,8},{20,116},{24,16},{28,124},{32... | collective-permute-start | bytes 983048 | tf_op jit(solution)/shard_map/ppermute | solution.py:51
  107.3 11.7 %collective-permute-start.10 = (bf16[320,512]{1,0:T(8,128)(2,1)S(1)}, bf16[320,512]{1,0:T(8,128)(2,1)S(1)}, u32[]{:S(2)}, u32[]{:S(2)}) collective-permute-start(bf16[320,512]{1,0:T(8,128)(2,1)S(1)} %get-tuple-element.39), channel_id=1, source_target_pairs={{0,8},{4,36},{8,16},{12,44},{16,24},{20,52},{24,0},{28,60},{32,40}... | collective-permute-start | bytes 983048 | tf_op jit(solution)/shard_map/ppermute | solution.py:51
  119.0 22.7 %collective-permute-start.26 = (bf16[160,1024]{1,0:T(8,128)(2,1)}, bf16[160,1024]{1,0:T(8,128)(2,1)S(1)}, u32[]{:S(2)}, u32[]{:S(2)}) collective-permute-start(bf16[160,1024]{1,0:T(8,128)(2,1)} %get-tuple-element.57), channel_id=1, source_target_pairs={{0,4},{4,0},{1,5},{5,1},{2,6},{6,2},{3,7},{7,3},{8,12},{12,8},{9,1... | collective-permute-start | bytes 983048 | tf_op jit(solution)/shard_map/ppermute | solution.py:59
  126.9 14.8 %collective-permute-start.27 = (bf16[160,512]{1,0:T(8,128)(2,1)}, bf16[160,512]{1,0:T(8,128)(2,1)S(1)}, u32[]{:S(2)}, u32[]{:S(2)}) collective-permute-start(bf16[160,512]{1,0:T(8,128)(2,1)} %get-tuple-element.59), channel_id=1, source_target_pairs={{0,4},{4,0},{1,5},{5,1},{2,6},{6,2},{3,7},{7,3},{8,12},{12,8},{9,1... | collective-permute-start | bytes 491528 | tf_op jit(solution)/shard_map/ppermute | solution.py:59
  126.9 14.8 %collective-permute-start.25 = (bf16[160,512]{1,0:T(8,128)(2,1)}, bf16[160,512]{1,0:T(8,128)(2,1)S(1)}, u32[]{:S(2)}, u32[]{:S(2)}) collective-permute-start(bf16[160,512]{1,0:T(8,128)(2,1)} %get-tuple-element.55), channel_id=1, source_target_pairs={{0,4},{4,0},{1,5},{5,1},{2,6},{6,2},{3,7},{7,3},{8,12},{12,8},{9,1... | collective-permute-start | bytes 491528 | tf_op jit(solution)/shard_map/ppermute | solution.py:59
  (7 other events, 86.0 us)
